TPU v7x, 32 devices: a whole 2x2x4 slice. The times are simulated.
32 devices in a mesh: data: 2 (over x), model: 4 (over z), stage: 4 (over y, core).
Axes of the slice: x: 2, y: 2, z: 4, core: 2. Of those that a mesh axis runs over, the one named last changes fastest.
Arguments:
- x_in: bfloat16 [6, 512, 1536], P('data'), parts along dimension 0
- y_target: bfloat16 [6, 512, 1536], P('data'), parts along dimension 0
- w_qkv: bfloat16 [4, 1536, 3, 12, 128], P('stage', None, None, 'model')
- w_out: bfloat16 [4, 12, 128, 1536], P('stage', 'model')
- w_up: bfloat16 [4, 1536, 6144], P('stage', None, 'model')
- w_down: bfloat16 [4, 6144, 1536], P('stage', 'model')
- norm_gain: bfloat16 [4, 2, 1536], P('stage')
Outputs:
- output 1: float32 [2], P('data'), parts along dimension 0
- output 2: float32 [8, 1536, 3, 12, 128], P(('data', 'stage'), None, None, 'model'), parts along dimension 0
- output 3: float32 [8, 12, 128, 1536], P(('data', 'stage'), 'model'), parts along dimension 0
- output 4: float32 [8, 1536, 6144], P(('data', 'stage'), None, 'model'), parts along dimension 0
- output 5: float32 [8, 6144, 1536], P(('data', 'stage'), 'model'), parts along dimension 0
- output 6: float32 [8, 2, 1536], P(('data', 'stage')), parts along dimension 0
There are 2 independent parts. A program takes and returns all parts, laid end to end along the dimension named above; an argument that names none is the same for every part.
All inputs are finite; a program needn't handle non-finite values.
Results may differ from a plain program's by a relative error of at most 0.00722361.
Values are sent between devices in bfloat16 or wider.
A program may use at most 1 GiB of HBM per device.

v0:
```python
import jax
import jax.numpy as jnp
from jax import lax
from jax.sharding import PartitionSpec as P

NORM_EPS = 1e-6
NEG_BIG = -1e30


def rms_inverse(hid32):
    return lax.rsqrt(jnp.mean(hid32 * hid32, axis=-1, keepdims=True) + NORM_EPS)


def rms_backward(hid32, gain32, inv_rms, d_norm):
    normed = hid32 * inv_rms
    d_gain = jnp.sum(d_norm * normed, axis=(0, 1))
    d_normed = d_norm * gain32
    d_hid = inv_rms * (d_normed - normed * jnp.mean(d_normed * normed, axis=-1, keepdims=True))
    return d_hid, d_gain


def gelu_tanh(up_act):
    return jax.nn.gelu(up_act, approximate=True)


def causal_probs(q_blk, k_all, q_start, attn_scale):
    scores = jnp.einsum("bqhe,bkhe->bhqk", q_blk, k_all, preferred_element_type=jnp.float32) * attn_scale
    q_pos = q_start + jnp.arange(q_blk.shape[1])
    k_pos = jnp.arange(k_all.shape[1])
    scores = jnp.where(k_pos[None, :] <= q_pos[:, None], scores, NEG_BIG)
    return jax.nn.softmax(scores, axis=-1)


def attend_forward(q_blk, k_all, v_all, q_start, attn_scale):
    attn_probs = causal_probs(q_blk, k_all, q_start, attn_scale).astype(jnp.bfloat16)
    return jnp.einsum("bhqk,bkhe->bqhe", attn_probs, v_all, preferred_element_type=jnp.float32).astype(jnp.bfloat16)


def attend_backward(q_blk, k_all, v_all, d_attn, q_start, attn_scale):
    attn_probs = causal_probs(q_blk, k_all, q_start, attn_scale)
    d_probs = jnp.einsum("bqhe,bkhe->bhqk", d_attn, v_all, preferred_element_type=jnp.float32)
    d_scores = attn_probs * (d_probs - jnp.sum(attn_probs * d_probs, axis=-1, keepdims=True)) * attn_scale
    d_scores = d_scores.astype(jnp.bfloat16)
    d_q = jnp.einsum("bhqk,bkhe->bqhe", d_scores, k_all, preferred_element_type=jnp.float32)
    d_k = jnp.einsum("bhqk,bqhe->bkhe", d_scores, q_blk, preferred_element_type=jnp.float32)
    d_v = jnp.einsum("bhqk,bqhe->bkhe", attn_probs.astype(jnp.bfloat16), d_attn, preferred_element_type=jnp.float32)
    return d_q, d_k, d_v


def store_at(buf_all, new_val, index, is_valid):
    old_val = lax.dynamic_index_in_dim(buf_all, index, 0, keepdims=False)
    return lax.dynamic_update_index_in_dim(buf_all, jnp.where(is_valid, new_val, old_val), index, 0)


def load_at(buf_all, index):
    return lax.dynamic_index_in_dim(buf_all, index, 0, keepdims=False)


def solution(mesh):
    n_stage = mesh.shape["stage"]
    n_chunks = max(4, n_stage)
    n_ticks = n_chunks + n_stage - 1
    fwd_perm = [(src_dev, src_dev + 1) for src_dev in range(n_stage - 1)]
    bwd_perm = [(src_dev + 1, src_dev) for src_dev in range(n_stage - 1)]

    def device_fn(x_in, y_target, w_qkv, w_out, w_up, w_down, norm_gain):
        n_batch, seq_len, d_model = x_in.shape
        heads_loc = w_qkv.shape[3]
        head_dim = w_qkv.shape[4]
        ff_loc = w_up.shape[2]
        chunk_len = seq_len // n_chunks
        attn_scale = head_dim ** -0.5
        elem_count = n_batch * seq_len * d_model
        stage_idx = lax.axis_index("stage")
        is_first = stage_idx == 0
        is_last = stage_idx == n_stage - 1
        wqkv_loc = w_qkv[0]
        wout_loc = w_out[0]
        wup_loc = w_up[0]
        wdown_loc = w_down[0]
        gain_a = norm_gain[0, 0].astype(jnp.float32)
        gain_b = norm_gain[0, 1].astype(jnp.float32)
        act_shape = (n_batch, chunk_len, d_model)
        head_shape = (n_batch, chunk_len, heads_loc, head_dim)
        cache_shape = (n_batch, seq_len, heads_loc, head_dim)

        def put_rows(cache, new_rows, q_start, is_valid):
            old_rows = lax.dynamic_slice_in_dim(cache, q_start, chunk_len, 1)
            return lax.dynamic_update_slice_in_dim(cache, jnp.where(is_valid, new_rows, old_rows), q_start, 1)

        def layer_forward(h_in, q_start, is_valid, k_cache, v_cache):
            h32 = h_in.astype(jnp.float32)
            norm_a = (h32 * rms_inverse(h32) * gain_a).astype(jnp.bfloat16)
            qkv_act = jnp.einsum("btd,djhe->btjhe", norm_a, wqkv_loc, preferred_element_type=jnp.float32).astype(jnp.bfloat16)
            q_new = qkv_act[:, :, 0]
            k_cache = put_rows(k_cache, qkv_act[:, :, 1], q_start, is_valid)
            v_cache = put_rows(v_cache, qkv_act[:, :, 2], q_start, is_valid)
            attn_act = attend_forward(q_new, k_cache, v_cache, q_start, attn_scale)
            attn_part = jnp.einsum("bthe,hed->btd", attn_act, wout_loc, preferred_element_type=jnp.float32)
            mid_hid = h32 + lax.psum(attn_part, "model")
            norm_b = (mid_hid * rms_inverse(mid_hid) * gain_b).astype(jnp.bfloat16)
            up_act = jnp.einsum("btd,df->btf", norm_b, wup_loc, preferred_element_type=jnp.float32)
            gelu_act = gelu_tanh(up_act).astype(jnp.bfloat16)
            down_part = jnp.einsum("btf,fd->btd", gelu_act, wdown_loc, preferred_element_type=jnp.float32)
            h_out = (mid_hid + lax.psum(down_part, "model")).astype(jnp.bfloat16)
            return h_out, k_cache, v_cache, (h_in, mid_hid, q_new, attn_act, up_act)

        def fwd_tick(carry, tick_idx):
            recv_act, k_cache, v_cache, saved_bufs, out_grads, loss_sum = carry
            c_idx = tick_idx - stage_idx
            is_valid = (c_idx >= 0) & (c_idx < n_chunks)
            c_safe = jnp.clip(c_idx, 0, n_chunks - 1)
            q_start = c_safe * chunk_len
            x_rows = lax.dynamic_slice_in_dim(x_in, q_start, chunk_len, 1)
            h_in = jnp.where(is_first, x_rows, recv_act)
            h_out, k_cache, v_cache, saved = layer_forward(h_in, q_start, is_valid, k_cache, v_cache)
            saved_bufs = tuple(store_at(buf_all, new_val, c_safe, is_valid) for buf_all, new_val in zip(saved_bufs, saved))
            y_rows = lax.dynamic_slice_in_dim(y_target, q_start, chunk_len, 1)
            loss_diff = h_out.astype(jnp.float32) - y_rows.astype(jnp.float32)
            use_loss = is_valid & is_last
            loss_sum = loss_sum + jnp.where(use_loss, jnp.sum(loss_diff * loss_diff), 0.0)
            out_grads = store_at(out_grads, (loss_diff / elem_count).astype(jnp.bfloat16), c_safe, use_loss)
            recv_act = lax.ppermute(h_out, "stage", fwd_perm)
            return (recv_act, k_cache, v_cache, saved_bufs, out_grads, loss_sum), None

        saved_init = (
            jnp.zeros((n_chunks,) + act_shape, jnp.bfloat16),
            jnp.zeros((n_chunks,) + act_shape, jnp.float32),
            jnp.zeros((n_chunks,) + head_shape, jnp.bfloat16),
            jnp.zeros((n_chunks,) + head_shape, jnp.bfloat16),
            jnp.zeros((n_chunks, n_batch, chunk_len, ff_loc), jnp.float32),
        )
        fwd_init = (
            jnp.zeros(act_shape, jnp.bfloat16),
            jnp.zeros(cache_shape, jnp.bfloat16),
            jnp.zeros(cache_shape, jnp.bfloat16),
            saved_init,
            jnp.zeros((n_chunks,) + act_shape, jnp.bfloat16),
            jnp.zeros((), jnp.float32),
        )
        fwd_state = lax.scan(fwd_tick, fwd_init, jnp.arange(n_ticks))[0]
        k_cache = fwd_state[1]
        v_cache = fwd_state[2]
        saved_bufs = fwd_state[3]
        out_grads = fwd_state[4]
        loss_val = 0.5 * lax.psum(fwd_state[5], "stage") / elem_count

        def layer_backward(d_out, q_start, is_valid, saved, dk_acc, dv_acc):
            h_in, mid_hid, q_new, attn_act, up_act = saved
            h32 = h_in.astype(jnp.float32)
            inv_a = rms_inverse(h32)
            norm_a = (h32 * inv_a * gain_a).astype(jnp.bfloat16)
            inv_b = rms_inverse(mid_hid)
            norm_b = (mid_hid * inv_b * gain_b).astype(jnp.bfloat16)
            gelu_act, gelu_vjp = jax.vjp(gelu_tanh, up_act)
            grad_down = jnp.einsum("btf,btd->fd", gelu_act.astype(jnp.bfloat16), d_out, preferred_element_type=jnp.float32)
            d_gelu = jnp.einsum("btd,fd->btf", d_out, wdown_loc, preferred_element_type=jnp.float32)
            d_up = gelu_vjp(d_gelu)[0].astype(jnp.bfloat16)
            grad_up = jnp.einsum("btd,btf->df", norm_b, d_up, preferred_element_type=jnp.float32)
            d_norm_b = lax.psum(jnp.einsum("btf,df->btd", d_up, wup_loc, preferred_element_type=jnp.float32), "model")
            d_mid_norm, grad_gain_b = rms_backward(mid_hid, gain_b, inv_b, d_norm_b)
            d_mid = d_out.astype(jnp.float32) + d_mid_norm
            d_mid16 = d_mid.astype(jnp.bfloat16)
            grad_out = jnp.einsum("bthe,btd->hed", attn_act, d_mid16, preferred_element_type=jnp.float32)
            d_attn = jnp.einsum("btd,hed->bthe", d_mid16, wout_loc, preferred_element_type=jnp.float32).astype(jnp.bfloat16)
            d_q, d_k, d_v = attend_backward(q_new, k_cache, v_cache, d_attn, q_start, attn_scale)
            dk_acc = dk_acc + jnp.where(is_valid, d_k, 0.0)
            dv_acc = dv_acc + jnp.where(is_valid, d_v, 0.0)
            dk_rows = lax.dynamic_slice_in_dim(dk_acc, q_start, chunk_len, 1)
            dv_rows = lax.dynamic_slice_in_dim(dv_acc, q_start, chunk_len, 1)
            d_qkv = jnp.stack([d_q, dk_rows, dv_rows], axis=2).astype(jnp.bfloat16)
            grad_qkv = jnp.einsum("btd,btjhe->djhe", norm_a, d_qkv, preferred_element_type=jnp.float32)
            d_norm_a = lax.psum(jnp.einsum("btjhe,djhe->btd", d_qkv, wqkv_loc, preferred_element_type=jnp.float32), "model")
            d_h_norm, grad_gain_a = rms_backward(h32, gain_a, inv_a, d_norm_a)
            d_in = (d_mid + d_h_norm).astype(jnp.bfloat16)
            grad_new = (grad_qkv, grad_out, grad_up, grad_down, jnp.stack([grad_gain_a, grad_gain_b]))
            return d_in, dk_acc, dv_acc, grad_new

        def bwd_tick(carry, tick_idx):
            recv_grad, dk_acc, dv_acc, grad_sums = carry
            back_step = tick_idx - (n_stage - 1 - stage_idx)
            is_valid = (back_step >= 0) & (back_step < n_chunks)
            c_safe = jnp.clip(n_chunks - 1 - back_step, 0, n_chunks - 1)
            q_start = c_safe * chunk_len
            d_out = jnp.where(is_last, load_at(out_grads, c_safe), recv_grad)
            saved = tuple(load_at(buf_all, c_safe) for buf_all in saved_bufs)
            d_in, dk_acc, dv_acc, grad_new = layer_backward(d_out, q_start, is_valid, saved, dk_acc, dv_acc)
            grad_sums = tuple(grad_acc + jnp.where(is_valid, grad_part, 0.0) for grad_acc, grad_part in zip(grad_sums, grad_new))
            recv_grad = lax.ppermute(d_in, "stage", bwd_perm)
            return (recv_grad, dk_acc, dv_acc, grad_sums), None

        grad_init = (
            jnp.zeros(wqkv_loc.shape, jnp.float32),
            jnp.zeros(wout_loc.shape, jnp.float32),
            jnp.zeros(wup_loc.shape, jnp.float32),
            jnp.zeros(wdown_loc.shape, jnp.float32),
            jnp.zeros((2, d_model), jnp.float32),
        )
        bwd_init = (
            jnp.zeros(act_shape, jnp.bfloat16),
            jnp.zeros(cache_shape, jnp.float32),
            jnp.zeros(cache_shape, jnp.float32),
            grad_init,
        )
        grad_sums = lax.scan(bwd_tick, bwd_init, jnp.arange(n_ticks))[0][3]
        return (loss_val.reshape(1),) + tuple(grad_part[None] for grad_part in grad_sums)

    act_spec = P("data", None, None)
    weight_specs = (
        P("stage", None, None, "model", None),
        P("stage", "model", None, None),
        P("stage", None, "model"),
        P("stage", "model", None),
        P("stage", None, None),
    )
    grad_specs = (
        P(("data", "stage"), None, None, "model", None),
        P(("data", "stage"), "model", None, None),
        P(("data", "stage"), None, "model"),
        P(("data", "stage"), "model", None),
        P(("data", "stage"), None, None),
    )
    return jax.shard_map(
        device_fn,
        mesh=mesh,
        in_specs=(act_spec, act_spec) + weight_specs,
        out_specs=(P("data"),) + grad_specs,
        check_vma=False,
    )
```

profile of v0, /device:TPU:0, one launch (start us, length us, event | category | flops | bytes accessed | tf_op | source)
XLA Modules:
  0.0 3660.0 jit_solution(417130789901607119)
XLA Ops:
  32.7 1715.4 %while.55 = (s32[]{:T(128)}, bf16[3,128,1536]{2,1,0:T(8,128)(2,1)}, bf16[3,512,3,128]{3,1,2,0:T(8,128)(2,1)}, bf16[3,512,3,128]{3,1,2,0:T(8,128)(2,1)S(1)}, bf16...) while((s32[]{:T(128)}, bf16[3,128,1536]{2,1,0:T(8,128)(2,1)}, ...), condition=%wide.region_8.9_spmd, body=%wide.region_0.8_spmd.sunk | while | flops 5770905088 | bytes 186258512 | solution.py:141
  59.6 94.2 %all-reduce.5.cloned.1.call-done = f32[3,128,1536]{2,1,0:T(8,128)} async-done(((f32[3,128,1536]{2,1,0:T(8,128)}), f32[3,128,1536]{2,1,0:T(8,128)}) %all-reduce.5.cloned.1.call-update) | async-done | bytes 2359312 | tf_op jit(solution)/shard_map/while/body/eval_jaxpr/psum | solution.py:100
  174.0 86.3 %all-reduce.7.cloned.1.call-done = f32[3,128,1536]{2,1,0:T(8,128)} async-done(((f32[3,128,1536]{2,1,0:T(8,128)}), f32[3,128,1536]{2,1,0:T(8,128)}) %all-reduce.7.cloned.1.call-update) | async-done | bytes 2359312 | tf_op jit(solution)/shard_map/while/body/eval_jaxpr/psum | solution.py:105
  299.9 99.7 %all-reduce.5.cloned.1.call-done = f32[3,128,1536]{2,1,0:T(8,128)} async-done(((f32[3,128,1536]{2,1,0:T(8,128)}), f32[3,128,1536]{2,1,0:T(8,128)}) %all-reduce.5.cloned.1.call-update) | async-done | bytes 2359312 | tf_op jit(solution)/shard_map/while/body/eval_jaxpr/psum | solution.py:100
  419.9 86.1 %all-reduce.7.cloned.1.call-done = f32[3,128,1536]{2,1,0:T(8,128)} async-done(((f32[3,128,1536]{2,1,0:T(8,128)}), f32[3,128,1536]{2,1,0:T(8,128)}) %all-reduce.7.cloned.1.call-update) | async-done | bytes 2359312 | tf_op jit(solution)/shard_map/while/body/eval_jaxpr/psum | solution.py:105
  545.8 99.6 %all-reduce.5.cloned.1.call-done = f32[3,128,1536]{2,1,0:T(8,128)} async-done(((f32[3,128,1536]{2,1,0:T(8,128)}), f32[3,128,1536]{2,1,0:T(8,128)}) %all-reduce.5.cloned.1.call-update) | async-done | bytes 2359312 | tf_op jit(solution)/shard_map/while/body/eval_jaxpr/psum | solution.py:100
  665.6 86.2 %all-reduce.7.cloned.1.call-done = f32[3,128,1536]{2,1,0:T(8,128)} async-done(((f32[3,128,1536]{2,1,0:T(8,128)}), f32[3,128,1536]{2,1,0:T(8,128)}) %all-reduce.7.cloned.1.call-update) | async-done | bytes 2359312 | tf_op jit(solution)/shard_map/while/body/eval_jaxpr/psum | solution.py:105
  791.5 99.6 %all-reduce.5.cloned.1.call-done = f32[3,128,1536]{2,1,0:T(8,128)} async-done(((f32[3,128,1536]{2,1,0:T(8,128)}), f32[3,128,1536]{2,1,0:T(8,128)}) %all-reduce.5.cloned.1.call-update) | async-done | bytes 2359312 | tf_op jit(solution)/shard_map/while/body/eval_jaxpr/psum | solution.py:100
  911.4 86.3 %all-reduce.7.cloned.1.call-done = f32[3,128,1536]{2,1,0:T(8,128)} async-done(((f32[3,128,1536]{2,1,0:T(8,128)}), f32[3,128,1536]{2,1,0:T(8,128)}) %all-reduce.7.cloned.1.call-update) | async-done | bytes 2359312 | tf_op jit(solution)/shard_map/while/body/eval_jaxpr/psum | solution.py:105
  1037.4 99.7 %all-reduce.5.cloned.1.call-done = f32[3,128,1536]{2,1,0:T(8,128)} async-done(((f32[3,128,1536]{2,1,0:T(8,128)}), f32[3,128,1536]{2,1,0:T(8,128)}) %all-reduce.5.cloned.1.call-update) | async-done | bytes 2359312 | tf_op jit(solution)/shard_map/while/body/eval_jaxpr/psum | solution.py:100
  1157.3 86.2 %all-reduce.7.cloned.1.call-done = f32[3,128,1536]{2,1,0:T(8,128)} async-done(((f32[3,128,1536]{2,1,0:T(8,128)}), f32[3,128,1536]{2,1,0:T(8,128)}) %all-reduce.7.cloned.1.call-update) | async-done | bytes 2359312 | tf_op jit(solution)/shard_map/while/body/eval_jaxpr/psum | solution.py:105
  1283.2 99.6 %all-reduce.5.cloned.1.call-done = f32[3,128,1536]{2,1,0:T(8,128)} async-done(((f32[3,128,1536]{2,1,0:T(8,128)}), f32[3,128,1536]{2,1,0:T(8,128)}) %all-reduce.5.cloned.1.call-update) | async-done | bytes 2359312 | tf_op jit(solution)/shard_map/while/body/eval_jaxpr/psum | solution.py:100
  1403.1 86.2 %all-reduce.7.cloned.1.call-done = f32[3,128,1536]{2,1,0:T(8,128)} async-done(((f32[3,128,1536]{2,1,0:T(8,128)}), f32[3,128,1536]{2,1,0:T(8,128)}) %all-reduce.7.cloned.1.call-update) | async-done | bytes 2359312 | tf_op jit(solution)/shard_map/while/body/eval_jaxpr/psum | solution.py:105
  1529.0 99.6 %all-reduce.5.cloned.1.call-done = f32[3,128,1536]{2,1,0:T(8,128)} async-done(((f32[3,128,1536]{2,1,0:T(8,128)}), f32[3,128,1536]{2,1,0:T(8,128)}) %all-reduce.5.cloned.1.call-update) | async-done | bytes 2359312 | tf_op jit(solution)/shard_map/while/body/eval_jaxpr/psum | solution.py:100
  1648.9 86.2 %all-reduce.7.cloned.1.call-done = f32[3,128,1536]{2,1,0:T(8,128)} async-done(((f32[3,128,1536]{2,1,0:T(8,128)}), f32[3,128,1536]{2,1,0:T(8,128)}) %all-reduce.7.cloned.1.call-update) | async-done | bytes 2359312 | tf_op jit(solution)/shard_map/while/body/eval_jaxpr/psum | solution.py:105
  1748.1 15.1 psum.41
  1765.0 1886.7 %while.56 = (s32[]{:T(128)}, bf16[3,128,1536]{2,1,0:T(8,128)(2,1)}, f32[3,512,3,128]{3,1,2,0:T(8,128)}, f32[3,512,3,128]{3,1,2,0:T(8,128)}, f32[1536,3,3,128]{3,...) while((s32[]{:T(128)}, bf16[3,128,1536]{2,1,0:T(8,128)(2,1)}, ...), condition=%wide.region_22.23_spmd.clone, body=%wide.region_10.22_spmd.clone.sunk | while | flops 11710740480 | bytes 282709760 | solution.py:205
  1786.0 88.3 %all-reduce.9.cloned.1.call-done = f32[3,128,1536]{2,1,0:T(8,128)} async-done(((f32[3,128,1536]{2,1,0:T(8,128)}), f32[3,128,1536]{2,1,0:T(8,128)}) %all-reduce.9.cloned.1.call-update) | async-done | bytes 2359312 | tf_op jit(solution)/shard_map/while/body/eval_jaxpr/psum | solution.py:160
  1941.1 72.4 %all-reduce.11.cloned.1.call-done = f32[3,128,1536]{2,1,0:T(8,128)} async-done(((f32[3,128,1536]{2,1,0:T(8,128)}), f32[3,128,1536]{2,1,0:T(8,128)}) %all-reduce.11.cloned.1.call-update) | async-done | bytes 2359312 | tf_op jit(solution)/shard_map/while/body/eval_jaxpr/psum | solution.py:173
  2049.8 93.1 %all-reduce.9.cloned.1.call-done = f32[3,128,1536]{2,1,0:T(8,128)} async-done(((f32[3,128,1536]{2,1,0:T(8,128)}), f32[3,128,1536]{2,1,0:T(8,128)}) %all-reduce.9.cloned.1.call-update) | async-done | bytes 2359312 | tf_op jit(solution)/shard_map/while/body/eval_jaxpr/psum | solution.py:160
  2215.4 68.2 %all-reduce.11.cloned.1.call-done = f32[3,128,1536]{2,1,0:T(8,128)} async-done(((f32[3,128,1536]{2,1,0:T(8,128)}), f32[3,128,1536]{2,1,0:T(8,128)}) %all-reduce.11.cloned.1.call-update) | async-done | bytes 2359312 | tf_op jit(solution)/shard_map/while/body/eval_jaxpr/psum | solution.py:173
  2322.0 91.0 %all-reduce.9.cloned.1.call-done = f32[3,128,1536]{2,1,0:T(8,128)} async-done(((f32[3,128,1536]{2,1,0:T(8,128)}), f32[3,128,1536]{2,1,0:T(8,128)}) %all-reduce.9.cloned.1.call-update) | async-done | bytes 2359312 | tf_op jit(solution)/shard_map/while/body/eval_jaxpr/psum | solution.py:160
  2485.5 68.2 %all-reduce.11.cloned.1.call-done = f32[3,128,1536]{2,1,0:T(8,128)} async-done(((f32[3,128,1536]{2,1,0:T(8,128)}), f32[3,128,1536]{2,1,0:T(8,128)}) %all-reduce.11.cloned.1.call-update) | async-done | bytes 2359312 | tf_op jit(solution)/shard_map/while/body/eval_jaxpr/psum | solution.py:173
  2592.1 91.0 %all-reduce.9.cloned.1.call-done = f32[3,128,1536]{2,1,0:T(8,128)} async-done(((f32[3,128,1536]{2,1,0:T(8,128)}), f32[3,128,1536]{2,1,0:T(8,128)}) %all-reduce.9.cloned.1.call-update) | async-done | bytes 2359312 | tf_op jit(solution)/shard_map/while/body/eval_jaxpr/psum | solution.py:160
  2755.6 68.2 %all-reduce.11.cloned.1.call-done = f32[3,128,1536]{2,1,0:T(8,128)} async-done(((f32[3,128,1536]{2,1,0:T(8,128)}), f32[3,128,1536]{2,1,0:T(8,128)}) %all-reduce.11.cloned.1.call-update) | async-done | bytes 2359312 | tf_op jit(solution)/shard_map/while/body/eval_jaxpr/psum | solution.py:173
  2862.2 91.0 %all-reduce.9.cloned.1.call-done = f32[3,128,1536]{2,1,0:T(8,128)} async-done(((f32[3,128,1536]{2,1,0:T(8,128)}), f32[3,128,1536]{2,1,0:T(8,128)}) %all-reduce.9.cloned.1.call-update) | async-done | bytes 2359312 | tf_op jit(solution)/shard_map/while/body/eval_jaxpr/psum | solution.py:160
  3025.7 68.2 %all-reduce.11.cloned.1.call-done = f32[3,128,1536]{2,1,0:T(8,128)} async-done(((f32[3,128,1536]{2,1,0:T(8,128)}), f32[3,128,1536]{2,1,0:T(8,128)}) %all-reduce.11.cloned.1.call-update) | async-done | bytes 2359312 | tf_op jit(solution)/shard_map/while/body/eval_jaxpr/psum | solution.py:173
  3132.3 91.0 %all-reduce.9.cloned.1.call-done = f32[3,128,1536]{2,1,0:T(8,128)} async-done(((f32[3,128,1536]{2,1,0:T(8,128)}), f32[3,128,1536]{2,1,0:T(8,128)}) %all-reduce.9.cloned.1.call-update) | async-done | bytes 2359312 | tf_op jit(solution)/shard_map/while/body/eval_jaxpr/psum | solution.py:160
  3295.8 68.2 %all-reduce.11.cloned.1.call-done = f32[3,128,1536]{2,1,0:T(8,128)} async-done(((f32[3,128,1536]{2,1,0:T(8,128)}), f32[3,128,1536]{2,1,0:T(8,128)}) %all-reduce.11.cloned.1.call-update) | async-done | bytes 2359312 | tf_op jit(solution)/shard_map/while/body/eval_jaxpr/psum | solution.py:173
  3402.4 91.0 %all-reduce.9.cloned.1.call-done = f32[3,128,1536]{2,1,0:T(8,128)} async-done(((f32[3,128,1536]{2,1,0:T(8,128)}), f32[3,128,1536]{2,1,0:T(8,128)}) %all-reduce.9.cloned.1.call-update) | async-done | bytes 2359312 | tf_op jit(solution)/shard_map/while/body/eval_jaxpr/psum | solution.py:160
  3519.9 13.0 bitcast_add_fusion.4
  3565.9 68.2 %all-reduce.11.cloned.1.call-done = f32[3,128,1536]{2,1,0:T(8,128)} async-done(((f32[3,128,1536]{2,1,0:T(8,128)}), f32[3,128,1536]{2,1,0:T(8,128)}) %all-reduce.11.cloned.1.call-update) | async-done | bytes 2359312 | tf_op jit(solution)/shard_map/while/body/eval_jaxpr/psum | solution.py:173
  (1007 shorter events, 1184.8 us)
Async XLA Ops:
  32.9 120.8 %all-reduce.5.cloned.1.call-start = ((), (), s32[]{:S(2)}) async-start(), calls=%async_computation | async-start | bytes 4718592 | tf_op jit(solution)/shard_map/while/body/eval_jaxpr/psum | solution.py:100
  56.3 203.9 %all-reduce.7.cloned.1.call-start = ((), (), s32[]{:S(2)}) async-start(), calls=%async_computation.1 | async-start | bytes 4718592 | tf_op jit(solution)/shard_map/while/body/eval_jaxpr/psum | solution.py:105
  273.2 126.3 %all-reduce.5.cloned.1.call-start = ((), (), s32[]{:S(2)}) async-start(), calls=%async_computation | async-start | bytes 4718592 | tf_op jit(solution)/shard_map/while/body/eval_jaxpr/psum | solution.py:100
  296.6 209.4 %all-reduce.7.cloned.1.call-start = ((), (), s32[]{:S(2)}) async-start(), calls=%async_computation.1 | async-start | bytes 4718592 | tf_op jit(solution)/shard_map/while/body/eval_jaxpr/psum | solution.py:105
  519.1 126.2 %all-reduce.5.cloned.1.call-start = ((), (), s32[]{:S(2)}) async-start(), calls=%async_computation | async-start | bytes 4718592 | tf_op jit(solution)/shard_map/while/body/eval_jaxpr/psum | solution.py:100
  542.5 209.3 %all-reduce.7.cloned.1.call-start = ((), (), s32[]{:S(2)}) async-start(), calls=%async_computation.1 | async-start | bytes 4718592 | tf_op jit(solution)/shard_map/while/body/eval_jaxpr/psum | solution.py:105
  764.8 126.3 %all-reduce.5.cloned.1.call-start = ((), (), s32[]{:S(2)}) async-start(), calls=%async_computation | async-start | bytes 4718592 | tf_op jit(solution)/shard_map/while/body/eval_jaxpr/psum | solution.py:100
  788.2 209.5 %all-reduce.7.cloned.1.call-start = ((), (), s32[]{:S(2)}) async-start(), calls=%async_computation.1 | async-start | bytes 4718592 | tf_op jit(solution)/shard_map/while/body/eval_jaxpr/psum | solution.py:105
  1010.7 126.3 %all-reduce.5.cloned.1.call-start = ((), (), s32[]{:S(2)}) async-start(), calls=%async_computation | async-start | bytes 4718592 | tf_op jit(solution)/shard_map/while/body/eval_jaxpr/psum | solution.py:100
  1034.1 209.4 %all-reduce.7.cloned.1.call-start = ((), (), s32[]{:S(2)}) async-start(), calls=%async_computation.1 | async-start | bytes 4718592 | tf_op jit(solution)/shard_map/while/body/eval_jaxpr/psum | solution.py:105
  1256.5 126.3 %all-reduce.5.cloned.1.call-start = ((), (), s32[]{:S(2)}) async-start(), calls=%async_computation | async-start | bytes 4718592 | tf_op jit(solution)/shard_map/while/body/eval_jaxpr/psum | solution.py:100
  1279.9 209.4 %all-reduce.7.cloned.1.call-start = ((), (), s32[]{:S(2)}) async-start(), calls=%async_computation.1 | async-start | bytes 4718592 | tf_op jit(solution)/shard_map/while/body/eval_jaxpr/psum | solution.py:105
  1502.3 126.3 %all-reduce.5.cloned.1.call-start = ((), (), s32[]{:S(2)}) async-start(), calls=%async_computation | async-start | bytes 4718592 | tf_op jit(solution)/shard_map/while/body/eval_jaxpr/psum | solution.py:100
  1525.7 209.4 %all-reduce.7.cloned.1.call-start = ((), (), s32[]{:S(2)}) async-start(), calls=%async_computation.1 | async-start | bytes 4718592 | tf_op jit(solution)/shard_map/while/body/eval_jaxpr/psum | solution.py:105
  1765.2 109.1 %all-reduce.9.cloned.1.call-start = ((), (), s32[]{:S(2)}) async-start(), calls=%async_computation.2 | async-start | bytes 4718592 | tf_op jit(solution)/shard_map/while/body/eval_jaxpr/psum | solution.py:160
  1779.9 233.6 %all-reduce.11.cloned.1.call-start = ((), (), s32[]{:S(2)}) async-start(), calls=%async_computation.3 | async-start | bytes 4718592 | tf_op jit(solution)/shard_map/while/body/eval_jaxpr/psum | solution.py:173
  2029.1 113.8 %all-reduce.9.cloned.1.call-start = ((), (), s32[]{:S(2)}) async-start(), calls=%async_computation.2 | async-start | bytes 4718592 | tf_op jit(solution)/shard_map/while/body/eval_jaxpr/psum | solution.py:160
  2043.7 239.9 %all-reduce.11.cloned.1.call-start = ((), (), s32[]{:S(2)}) async-start(), calls=%async_computation.3 | async-start | bytes 4718592 | tf_op jit(solution)/shard_map/while/body/eval_jaxpr/psum | solution.py:173
  2288.5 11.4 collective-permute-start.1
  2301.3 111.7 %all-reduce.9.cloned.1.call-start = ((), (), s32[]{:S(2)}) async-start(), calls=%async_computation.2 | async-start | bytes 4718592 | tf_op jit(solution)/shard_map/while/body/eval_jaxpr/psum | solution.py:160
  2315.9 237.8 %all-reduce.11.cloned.1.call-start = ((), (), s32[]{:S(2)}) async-start(), calls=%async_computation.3 | async-start | bytes 4718592 | tf_op jit(solution)/shard_map/while/body/eval_jaxpr/psum | solution.py:173
  2558.6 11.4 collective-permute-start.1
  2571.3 111.7 %all-reduce.9.cloned.1.call-start = ((), (), s32[]{:S(2)}) async-start(), calls=%async_computation.2 | async-start | bytes 4718592 | tf_op jit(solution)/shard_map/while/body/eval_jaxpr/psum | solution.py:160
  2586.0 237.8 %all-reduce.11.cloned.1.call-start = ((), (), s32[]{:S(2)}) async-start(), calls=%async_computation.3 | async-start | bytes 4718592 | tf_op jit(solution)/shard_map/while/body/eval_jaxpr/psum | solution.py:173
  2828.7 11.4 collective-permute-start.1
  2841.4 111.7 %all-reduce.9.cloned.1.call-start = ((), (), s32[]{:S(2)}) async-start(), calls=%async_computation.2 | async-start | bytes 4718592 | tf_op jit(solution)/shard_map/while/body/eval_jaxpr/psum | solution.py:160
  2856.1 237.8 %all-reduce.11.cloned.1.call-start = ((), (), s32[]{:S(2)}) async-start(), calls=%async_computation.3 | async-start | bytes 4718592 | tf_op jit(solution)/shard_map/while/body/eval_jaxpr/psum | solution.py:173
  3098.8 11.4 collective-permute-start.1
  3111.5 111.7 %all-reduce.9.cloned.1.call-start = ((), (), s32[]{:S(2)}) async-start(), calls=%async_computation.2 | async-start | bytes 4718592 | tf_op jit(solution)/shard_map/while/body/eval_jaxpr/psum | solution.py:160
  3126.2 237.8 %all-reduce.11.cloned.1.call-start = ((), (), s32[]{:S(2)}) async-start(), calls=%async_computation.3 | async-start | bytes 4718592 | tf_op jit(solution)/shard_map/while/body/eval_jaxpr/psum | solution.py:173
  3381.6 111.7 %all-reduce.9.cloned.1.call-start = ((), (), s32[]{:S(2)}) async-start(), calls=%async_computation.2 | async-start | bytes 4718592 | tf_op jit(solution)/shard_map/while/body/eval_jaxpr/psum | solution.py:160
  3396.3 237.8 %all-reduce.11.cloned.1.call-start = ((), (), s32[]{:S(2)}) async-start(), calls=%async_computation.3 | async-start | bytes 4718592 | tf_op jit(solution)/shard_map/while/body/eval_jaxpr/psum | solution.py:173
  (255 other events, 2121.0 us)
Sparse Core Ops, SparseCore 0:
  56.4 97.2 all-reduce.4
  166.7 93.5 all-reduce.6
  296.7 102.7 all-reduce.4
  412.6 93.4 all-reduce.6
  542.6 102.6 all-reduce.4
  658.3 93.5 all-reduce.6
  788.3 102.7 all-reduce.4
  904.1 93.6 all-reduce.6
  1034.2 102.7 all-reduce.4
  1150.0 93.4 all-reduce.6
  1280.0 102.7 all-reduce.4
  1395.7 93.5 all-reduce.6
  1525.8 102.7 all-reduce.4
  1641.5 93.5 all-reduce.6
  1780.0 94.2 all-reduce.8
  1919.9 93.5 all-reduce.10
  2043.8 99.0 all-reduce.8
  2190.0 93.5 all-reduce.10
  2316.0 96.9 all-reduce.8
  2460.1 93.5 all-reduce.10
  2586.1 96.9 all-reduce.8
  2730.2 93.5 all-reduce.10
  2856.2 96.9 all-reduce.8
  3000.3 93.5 all-reduce.10
  3126.3 96.9 all-reduce.8
  3270.4 93.5 all-reduce.10
  3396.4 96.9 all-reduce.8
  3540.5 93.5 all-reduce.10
where the time goes:
time: 3680 us; the launch traced here: 3660 us
  waiting for transfers between devices  2410 us (65%)
  matrix products  723 us (20%)
  other arithmetic  262 us (7%)
  local copies, waits for them, and re-layouts  185 us (5%)
    psum x7, waiting for transfers between devices, layer_forward(): mid_hid = h32 + lax.psum(attn_part, 'model')  692 us
    psum x7, waiting for transfers between devices, layer_backward(): lax.psum(jnp.einsum('btf,df->btd', d_up, wup_loc, preferred_element_type=...  636 us
    psum x7, waiting for transfers between devices, layer_forward(): h_out = (mid_hid + lax.psum(down_part, 'model')).astype(jnp.bfloat16)  604 us
    psum x7, waiting for transfers between devices, layer_backward(): lax.psum(jnp.einsum('btjhe,djhe->btd', d_qkv, wqkv_loc, preferred_element...  481 us
    dot_general x7, matrix products, attend_backward(): jnp.einsum('bhqk,bqhe->bkhe', d_scores, q_blk, preferred_element_type=jnp...  90.6 us
    dynamic_slice x35, local copies, waits for them, and re-layouts, store_at(): old_val = lax.dynamic_index_in_dim(buf_all, index, 0, keepdims=False)  83 us
    dot_general x7, matrix products, attend_backward(): jnp.einsum('bhqk,bkhe->bqhe', d_scores, k_all, preferred_element_type=jnp...  77.9 us
    dot_general x7, matrix products, layer_backward(): jnp.einsum('btd,btf->df', norm_b, d_up, preferred_element_type=jnp.float32)  76.1 us
  transfers between devices with their start and end apart: 42, of which 28 were waited for; matrix products, arithmetic and copies ran while one was open for 11% of the time, Pallas kernels for 0%

commit v1 on v0

v1 whole, which is shorter than its diff:
```python
import jax
import jax.numpy as jnp
from jax import lax
from jax.experimental import pallas as pl
from jax.experimental.pallas import tpu as pltpu
from jax.sharding import PartitionSpec as P

NORM_EPS = 1e-6
NEG_BIG = -1e30
MESH = pl.DeviceIdType.MESH
GELU_K = 0.7978845608028654
GELU_C = 0.044715
F32 = jnp.float32
BF16 = jnp.bfloat16


def dot_nn(a, b):
    return lax.dot_general(a, b, (((1,), (0,)), ((), ())), preferred_element_type=F32)


def dot_nt(a, b):
    return lax.dot_general(a, b, (((1,), (1,)), ((), ())), preferred_element_type=F32)


def dot_tn(a, b):
    return lax.dot_general(a, b, (((0,), (0,)), ((), ())), preferred_element_type=F32)


def rms_inverse(v32):
    return lax.rsqrt(jnp.mean(v32 * v32, axis=-1, keepdims=True) + NORM_EPS)


def layer_step(dims, x_in, y_target, w_qkv, w_out, w_up, w_down, gain):
    nz, ns = dims["model"], dims["stage"]
    n_seq, seq_len, d_model = x_in.shape
    qkv_w = w_qkv.shape[1]
    att_w = w_out.shape[0]
    ff_w = w_up.shape[1]
    head_dim = 128
    n_head = att_w // head_dim
    tok = 128
    row = tok // nz
    per_seq = seq_len // tok
    n_unit = n_seq * per_seq
    n_chunk = n_unit // 2
    scale = head_dim ** -0.5
    inv_count = 1.0 / (n_seq * seq_len * d_model)
    last_z, last_s = nz - 1, ns - 1
    sub_rows = 16

    def kernel(x_ref, y_ref, wqkv_h, wout_h, wup_h, wdown_h, gain_ref,
               a_out, b_out, d_out, dm_out, dqkv_out, o_out, z_out, du_out, red_out,
               wqkv, wout, wup, wdown, hslot, yslot, dslot, abuf, bbuf, dbuf, dmbuf,
               qkv_all, u_all, m_all, ost, zst, dust, dqkvst, dattst, part,
               recv_r, recv_l, send_r, send_l, accq, hout, dmid, dkacc, dvacc,
               lossacc, ga8, gb8, gx,
               w_sem, hsem, ysem, dsem, hs_sem, save_sem,
               ag_rs, ag_sr, ag_sl, rs_rr, rs_rl, rs_sr, rs_sl, loss_sem, gx_s, gx_r):
        z = lax.axis_index("model")
        st = lax.axis_index("stage")
        is_first = st == 0
        is_last = st == last_s

        def rdma(src, dst, ssem, rsem, dev):
            return pltpu.make_async_remote_copy(src_ref=src, dst_ref=dst, send_sem=ssem, recv_sem=rsem,
                                                device_id=dev, device_id_type=MESH)

        def rows_of(k):
            return pl.ds(pl.multiple_of(k * row, row), row)

        w_copies = [pltpu.make_async_copy(src, dst, w_sem.at[i])
                    for i, (src, dst) in enumerate(((wqkv_h, wqkv), (wout_h, wout), (wup_h, wup), (wdown_h, wdown)))]

        def unit_rows(u):
            return lax.div(u, per_seq), pl.ds(pl.multiple_of(lax.rem(u, per_seq) * tok + z * row, row), row)

        def x_copy(u):
            q, rs = unit_rows(u)
            return pltpu.make_async_copy(x_ref.at[q, rs, :], hslot.at[u], hsem.at[u])

        def y_copy(u):
            q, rs = unit_rows(u)
            return pltpu.make_async_copy(y_ref.at[q, rs, :], yslot.at[u], ysem.at[u])

        @pl.when(is_first)
        def _():
            @pl.loop(0, n_unit)
            def _(u):
                x_copy(u).start()

        for cp in w_copies:
            cp.start()

        @pl.when(is_last)
        def _():
            @pl.loop(0, n_unit)
            def _(u):
                y_copy(u).start()

        barrier = pltpu.get_barrier_semaphore()
        for dz in range(1, nz):
            pl.semaphore_signal(barrier, inc=1, device_id={"model": lax.rem(z + dz, nz)}, device_id_type=MESH)

        @pl.when(st < last_s)
        def _():
            pl.semaphore_signal(barrier, inc=1, device_id={"stage": st + 1}, device_id_type=MESH)

        @pl.when(st > 0)
        def _():
            pl.semaphore_signal(barrier, inc=1, device_id={"stage": st - 1}, device_id_type=MESH)

        qkv_all[...] = jnp.zeros_like(qkv_all)
        lossacc[...] = jnp.zeros_like(lossacc)
        ga8[...] = jnp.zeros_like(ga8)
        gb8[...] = jnp.zeros_like(gb8)
        @pl.when((st == 0) | (st == last_s))
        def _():
            pl.semaphore_wait(barrier, nz)

        @pl.when((st > 0) & (st < last_s))
        def _():
            pl.semaphore_wait(barrier, nz + 1)

        def h_in_copy(u):
            return rdma(hout.at[0], hslot.at[u], hs_sem.at[0], hsem.at[u], {"stage": st})

        def h_send(s, u):
            return rdma(hout.at[s], hslot.at[u], hs_sem.at[s], hsem.at[u], {"stage": st + 1})

        def d_send(s, u):
            return rdma(hout.at[s], dslot.at[u], hs_sem.at[s], dsem.at[u], {"stage": st - 1})

        def ag_right(buf, kind, s, j):
            blk = buf.at[s, rows_of(j), :]
            return rdma(blk, blk, ag_sr.at[kind, s, j], ag_rs.at[kind, s, j], {"model": z + 1})

        def ag_left(buf, kind, s, j):
            blk = buf.at[s, rows_of(j), :]
            return rdma(blk, blk, ag_sl.at[kind, s, j], ag_rs.at[kind, s, j], {"model": z - 1})

        def ag_start(buf, kind, s):
            @pl.when(z < last_z)
            def _():
                ag_right(buf, kind, s, z).start()

            @pl.when(z > 0)
            def _():
                ag_left(buf, kind, s, z).start()

        def ag_step(buf, kind, s, t):
            @pl.when(z >= t)
            def _():
                ag_right(buf, kind, s, z - t).wait_recv()

                @pl.when(z < last_z)
                def _():
                    ag_right(buf, kind, s, z - t).start()

            @pl.when(z + t <= last_z)
            def _():
                ag_left(buf, kind, s, z + t).wait_recv()

                @pl.when(z > 0)
                def _():
                    ag_left(buf, kind, s, z + t).start()

        def ag_drain(buf, kind, s):
            for j in range(nz):
                @pl.when((z >= j) & (z < last_z))
                def _():
                    ag_right(buf, kind, s, j).wait_send()

                @pl.when((z <= j) & (z > 0))
                def _():
                    ag_left(buf, kind, s, j).wait_send()

        def rs_right(s, k):
            return rdma(send_r.at[s, k], recv_r.at[s, k], rs_sr.at[s, k], rs_rr.at[s, k], {"model": z + 1})

        def rs_left(s, k):
            return rdma(send_l.at[s, k], recv_l.at[s, k], rs_sl.at[s, k], rs_rl.at[s, k], {"model": z - 1})

        def rs_step(s, t):
            kr = last_z - t + z
            kl = t - last_z + z

            @pl.when(z == 0)
            def _():
                send_r[s, kr] = part[s, rows_of(kr), :].astype(BF16)
                rs_right(s, kr).start()

            @pl.when((z > 0) & (z <= t))
            def _():
                rs_right(s, kr).wait_recv()
                send_r[s, kr] = (part[s, rows_of(kr), :] + recv_r[s, kr].astype(F32)).astype(BF16)
                rs_right(s, kr).start()

            @pl.when(z == last_z)
            def _():
                send_l[s, kl] = part[s, rows_of(kl), :].astype(BF16)
                rs_left(s, kl).start()

            @pl.when((z < last_z) & (last_z - z <= t))
            def _():
                rs_left(s, kl).wait_recv()
                send_l[s, kl] = (part[s, rows_of(kl), :] + recv_l[s, kl].astype(F32)).astype(BF16)
                rs_left(s, kl).start()

        def rs_final(s):
            accq[s] = part[s, rows_of(z), :]

            @pl.when(z > 0)
            def _():
                rs_right(s, z).wait_recv()
                accq[s] += recv_r[s, z].astype(F32)

            @pl.when(z < last_z)
            def _():
                rs_left(s, z).wait_recv()
                accq[s] += recv_l[s, z].astype(F32)

        def rs_drain(s):
            for k in range(1, nz):
                @pl.when(z < k)
                def _():
                    rs_right(s, k).wait_send()

            for k in range(nz - 1):
                @pl.when(z > k)
                def _():
                    rs_left(s, k).wait_send()

        def save(kind, src, dst, s, u):
            return pltpu.make_async_copy(src.at[s], dst.at[u], save_sem.at[kind, s])

        def softmax_of(u, p, i):
            first = u - p
            cols = pl.ds(i * head_dim, head_dim)
            q = qkv_all[u, :, cols]
            k = qkv_all[pl.ds(first, per_seq), :, pl.ds(att_w + i * head_dim, head_dim)].reshape(seq_len, head_dim)
            v = qkv_all[pl.ds(first, per_seq), :, pl.ds(2 * att_w + i * head_dim, head_dim)].reshape(seq_len, head_dim)
            sc = dot_nt(q, k) * scale
            q_pos = p * tok + lax.broadcasted_iota(jnp.int32, sc.shape, 0)
            k_pos = lax.broadcasted_iota(jnp.int32, sc.shape, 1)
            sc = jnp.where(k_pos <= q_pos, sc, NEG_BIG)
            e = jnp.exp(sc - jnp.max(sc, axis=-1, keepdims=True))
            pr = e * (1.0 / jnp.sum(e, axis=-1, keepdims=True))
            return q, k, v, pr

        gain_a = gain_ref[0:1, :]
        gain_b = gain_ref[1:2, :]

        def fwd_chunk(c, carry):
            for s in range(2):
                u = 2 * c + s

                @pl.when(is_first)
                def _():
                    x_copy(u).wait()

                @pl.when(st > 0)
                def _():
                    h_in_copy(u).wait_recv()

                h32 = hslot[u].astype(F32)
                abuf[s, rows_of(z), :] = (h32 * rms_inverse(h32) * gain_a).astype(BF16)
                ag_start(abuf, 0, s)
            for t in range(1, nz):
                for s in range(2):
                    ag_step(abuf, 0, s, t)

            @pl.when(c == 0)
            def _():
                w_copies[0].wait()
                w_copies[1].wait()

            def attention_part(s, carry):
                u = 2 * c + s
                p = lax.rem(u, per_seq)
                save(0, abuf, a_out, s, u).start()
                qkv_all[u] = dot_nn(abuf[s], wqkv[...]).astype(BF16)
                for i in range(n_head):
                    _, _, v, pr = softmax_of(u, p, i)
                    ost[s, :, pl.ds(i * head_dim, head_dim)] = dot_nn(pr.astype(BF16), v).astype(BF16)
                save(1, ost, o_out, s, u).start()
                part[s] = dot_nn(ost[s], wout[...])
                rs_step(s, 0)
                return carry

            lax.fori_loop(0, 2, attention_part, 0)
            for t in range(1, nz - 1):
                for s in range(2):
                    rs_step(s, t)
            for s in range(2):
                u = 2 * c + s
                rs_final(s)
                m = hslot[u].astype(F32) + accq[s]
                m_all[u] = m
                bbuf[s, rows_of(z), :] = (m * rms_inverse(m) * gain_b).astype(BF16)
                ag_start(bbuf, 1, s)
            for s in range(2):
                rs_drain(s)
                ag_drain(abuf, 0, s)
            for t in range(1, nz):
                for s in range(2):
                    ag_step(bbuf, 1, s, t)

            @pl.when(c == 0)
            def _():
                w_copies[2].wait()
                w_copies[3].wait()

            def mlp_part(s, carry):
                u = 2 * c + s
                save(0, abuf, a_out, s, u).wait()
                save(2, bbuf, b_out, s, u).start()
                u_all[u] = dot_nn(bbuf[s], wup[...])

                def act(r, carry):
                    rr = pl.ds(pl.multiple_of(r * sub_rows, sub_rows), sub_rows)
                    v = u_all[u, rr, :]
                    th = jnp.tanh(GELU_K * (v + GELU_C * (v * v * v)))
                    zst[s, rr, :] = (0.5 * v * (1.0 + th)).astype(BF16)
                    return carry

                lax.fori_loop(0, tok // sub_rows, act, 0)
                save(3, zst, z_out, s, u).start()
                part[s] = dot_nn(zst[s], wdown[...])
                rs_step(s, 0)
                return carry

            lax.fori_loop(0, 2, mlp_part, 0)
            for t in range(1, nz - 1):
                for s in range(2):
                    rs_step(s, t)
            for s in range(2):
                u = 2 * c + s
                rs_final(s)
                h_new = (m_all[u] + accq[s]).astype(BF16)

                @pl.when(st < last_s)
                def _():
                    hout[s] = h_new
                    h_send(s, u).start()

                @pl.when(is_last)
                def _():
                    y_copy(u).wait()
                    diff = h_new.astype(F32) - yslot[u].astype(F32)
                    dslot[u] = (diff * inv_count).astype(BF16)
                    lossacc[...] += jnp.sum((diff * diff).reshape(row // 8, 8, d_model), axis=0)
            for s in range(2):
                u = 2 * c + s
                rs_drain(s)
                ag_drain(bbuf, 1, s)

                @pl.when(st < last_s)
                def _():
                    h_send(s, u).wait_send()

                save(1, ost, o_out, s, u).wait()
                save(2, bbuf, b_out, s, u).wait()
                save(3, zst, z_out, s, u).wait()
            return carry

        lax.fori_loop(0, n_chunk, fwd_chunk, 0)

        def loss_send():
            return rdma(lossacc, lossacc, loss_sem.at[0], loss_sem.at[1], {"stage": st - 1})

        @pl.when(is_last)
        def _():
            loss_send().start()

        def bwd_chunk(step, carry):
            c = n_chunk - 1 - step
            for s in (1, 0):
                u = 2 * c + s

                @pl.when(st < last_s)
                def _():
                    d_send(0, u).wait_recv()

                dbuf[s, rows_of(z), :] = dslot[u]
                ag_start(dbuf, 2, s)
            for t in range(1, nz):
                for s in (1, 0):
                    ag_step(dbuf, 2, s, t)

            def mlp_back(i, carry):
                s = 1 - i
                u = 2 * c + s
                save(4, dbuf, d_out, s, u).start()
                part[s] = dot_nt(dbuf[s], wdown[...])

                def act(r, carry):
                    rr = pl.ds(pl.multiple_of(r * sub_rows, sub_rows), sub_rows)
                    v = u_all[u, rr, :]
                    v2 = v * v
                    th = jnp.tanh(GELU_K * (v + GELU_C * (v2 * v)))
                    slope = 0.5 * (1.0 + th) + 0.5 * v * (1.0 - th * th) * (GELU_K * (1.0 + 3.0 * GELU_C * v2))
                    dust[s, rr, :] = (part[s, rr, :] * slope).astype(BF16)
                    return carry

                lax.fori_loop(0, tok // sub_rows, act, 0)
                save(5, dust, du_out, s, u).start()
                part[s] = dot_nt(dust[s], wup[...])
                rs_step(s, 0)
                return carry

            lax.fori_loop(0, 2, mlp_back, 0)
            for t in range(1, nz - 1):
                for s in (1, 0):
                    rs_step(s, t)
            for s in (1, 0):
                u = 2 * c + s
                rs_final(s)
                m = m_all[u]
                inv = rms_inverse(m)
                normed = m * inv
                dn = accq[s]
                gb8[...] += jnp.sum((dn * normed).reshape(row // 8, 8, d_model), axis=0)
                dn = dn * gain_b
                dm = dslot[u].astype(F32) + inv * (dn - normed * jnp.mean(dn * normed, axis=-1, keepdims=True))
                dmid[s] = dm
                dmbuf[s, rows_of(z), :] = dm.astype(BF16)
                ag_start(dmbuf, 3, s)
            for s in (1, 0):
                rs_drain(s)
                ag_drain(dbuf, 2, s)
            for t in range(1, nz):
                for s in (1, 0):
                    ag_step(dmbuf, 3, s, t)

            def attention_back(i, carry):
                s = 1 - i
                u = 2 * c + s
                p = lax.rem(u, per_seq)
                save(4, dbuf, d_out, s, u).wait()
                save(6, dmbuf, dm_out, s, u).start()

                @pl.when(p == per_seq - 1)
                def _():
                    dkacc[...] = jnp.zeros_like(dkacc)
                    dvacc[...] = jnp.zeros_like(dvacc)

                dattst[s] = dot_nt(dmbuf[s], wout[...]).astype(BF16)
                p_rows = pl.ds(pl.multiple_of(p * tok, tok), tok)
                for h in range(n_head):
                    cols = pl.ds(h * head_dim, head_dim)
                    q, k, v, pr = softmax_of(u, p, h)
                    da = dattst[s, :, cols]
                    dp = dot_nt(da, v)
                    ds = (pr * (dp - jnp.sum(pr * dp, axis=-1, keepdims=True)) * scale).astype(BF16)
                    dvacc[:, cols] += dot_tn(pr.astype(BF16), da)
                    dkacc[:, cols] += dot_tn(ds, q)
                    dqkvst[s, :, cols] = dot_nn(ds, k).astype(BF16)
                dqkvst[s, :, pl.ds(att_w, att_w)] = dkacc[p_rows, :].astype(BF16)
                dqkvst[s, :, pl.ds(2 * att_w, att_w)] = dvacc[p_rows, :].astype(BF16)
                save(7, dqkvst, dqkv_out, s, u).start()
                part[s] = dot_nt(dqkvst[s], wqkv[...])
                rs_step(s, 0)
                return carry

            lax.fori_loop(0, 2, attention_back, 0)
            for t in range(1, nz - 1):
                for s in (1, 0):
                    rs_step(s, t)
            for s in (1, 0):
                u = 2 * c + s
                rs_final(s)
                h32 = hslot[u].astype(F32)
                inv = rms_inverse(h32)
                normed = h32 * inv
                dn = accq[s]
                ga8[...] += jnp.sum((dn * normed).reshape(row // 8, 8, d_model), axis=0)

                @pl.when(st > 0)
                def _():
                    dg = dn * gain_a
                    hout[s] = (dmid[s] + inv * (dg - normed * jnp.mean(dg * normed, axis=-1, keepdims=True))).astype(BF16)
                    d_send(s, u).start()
            for s in (1, 0):
                u = 2 * c + s
                rs_drain(s)
                ag_drain(dmbuf, 3, s)

                @pl.when(st > 0)
                def _():
                    d_send(s, u).wait_send()

                save(5, dust, du_out, s, u).wait()
                save(6, dmbuf, dm_out, s, u).wait()
                save(7, dqkvst, dqkv_out, s, u).wait()
            return carry

        lax.fori_loop(0, n_chunk, bwd_chunk, 0)

        @pl.when(is_last)
        def _():
            loss_send().wait_send()

        @pl.when(st < last_s)
        def _():
            loss_send().wait_recv()

            @pl.when(st > 0)
            def _():
                loss_send().start()
                loss_send().wait_send()

        loss_row = jnp.sum(jnp.sum(lossacc[...], axis=0, keepdims=True), axis=1, keepdims=True)
        gx[z, 0:1, :] = jnp.sum(ga8[...], axis=0, keepdims=True)
        gx[z, 1:2, :] = jnp.sum(gb8[...], axis=0, keepdims=True)
        gx[z, 2:8, :] = jnp.broadcast_to(loss_row, (6, d_model))

        def gx_send(dz):
            return rdma(gx.at[z], gx.at[z], gx_s.at[dz], gx_r.at[z], {"model": lax.rem(z + dz, nz)})

        def gx_recv(dz):
            j = lax.rem(z + dz, nz)
            return rdma(gx.at[j], gx.at[j], gx_s.at[dz], gx_r.at[j], {"model": j})

        for dz in range(1, nz):
            gx_send(dz).start()
        for dz in range(1, nz):
            gx_recv(dz).wait_recv()
        red_out[...] = gx[0] + gx[1] + gx[2] + gx[3]
        for dz in range(1, nz):
            gx_send(dz).wait_send()

    any_spec = pl.BlockSpec(memory_space=pl.ANY)
    vmem_spec = pl.BlockSpec(memory_space=pltpu.VMEM)

    def out(width):
        return jax.ShapeDtypeStruct((n_unit, tok, width), BF16)

    dma = pltpu.SemaphoreType.DMA
    return pl.pallas_call(
        kernel,
        out_shape=(out(d_model), out(d_model), out(d_model), out(d_model), out(qkv_w), out(att_w), out(ff_w), out(ff_w),
                   jax.ShapeDtypeStruct((8, d_model), F32)),
        in_specs=[any_spec] * 6 + [vmem_spec],
        out_specs=(any_spec,) * 8 + (vmem_spec,),
        scratch_shapes=[
            pltpu.VMEM((d_model, qkv_w), BF16), pltpu.VMEM((att_w, d_model), BF16),
            pltpu.VMEM((d_model, ff_w), BF16), pltpu.VMEM((ff_w, d_model), BF16),
            pltpu.VMEM((n_unit, row, d_model), BF16), pltpu.VMEM((n_unit, row, d_model), BF16),
            pltpu.VMEM((n_unit, row, d_model), BF16),
            pltpu.VMEM((2, tok, d_model), BF16), pltpu.VMEM((2, tok, d_model), BF16),
            pltpu.VMEM((2, tok, d_model), BF16), pltpu.VMEM((2, tok, d_model), BF16),
            pltpu.VMEM((n_unit, tok, qkv_w), BF16), pltpu.VMEM((n_unit, tok, ff_w), F32),
            pltpu.VMEM((n_unit, row, d_model), F32),
            pltpu.VMEM((2, tok, att_w), BF16), pltpu.VMEM((2, tok, ff_w), BF16), pltpu.VMEM((2, tok, ff_w), BF16),
            pltpu.VMEM((2, tok, qkv_w), BF16), pltpu.VMEM((2, tok, att_w), BF16), pltpu.VMEM((2, tok, d_model), F32),
            pltpu.VMEM((2, nz, row, d_model), BF16), pltpu.VMEM((2, nz, row, d_model), BF16),
            pltpu.VMEM((2, nz, row, d_model), BF16), pltpu.VMEM((2, nz, row, d_model), BF16),
            pltpu.VMEM((2, row, d_model), F32), pltpu.VMEM((2, row, d_model), BF16), pltpu.VMEM((2, row, d_model), F32),
            pltpu.VMEM((seq_len, att_w), F32), pltpu.VMEM((seq_len, att_w), F32),
            pltpu.VMEM((8, d_model), F32), pltpu.VMEM((8, d_model), F32), pltpu.VMEM((8, d_model), F32),
            pltpu.VMEM((nz, 8, d_model), F32),
            dma((4,)), dma((n_unit,)), dma((n_unit,)), dma((n_unit,)), dma((2,)), dma((8, 2)),
            dma((4, 2, nz)), dma((4, 2, nz)), dma((4, 2, nz)),
            dma((2, nz)), dma((2, nz)), dma((2, nz)), dma((2, nz)), dma((2,)), dma((nz,)), dma((nz,)),
        ],
        compiler_params=pltpu.CompilerParams(collective_id=0, has_side_effects=True, vmem_limit_bytes=66_000_000),
        name="layer_step",
    )(x_in, y_target, w_qkv, w_out, w_up, w_down, gain)


def weight_grad(act, grad):
    return lax.dot_general(act, grad, (((0, 1), (0, 1)), ((), ())), preferred_element_type=F32)


def solution(mesh):
    dims = dict(mesh.shape)

    def device_fn(x_in, y_target, w_qkv, w_out, w_up, w_down, norm_gain):
        n_batch, seq_len, d_model = x_in.shape
        heads, head_dim = w_qkv.shape[3], w_qkv.shape[4]
        a, b, d, dm, dqkv, o, zz, du, red = layer_step(
            dims, x_in, y_target,
            w_qkv[0].reshape(d_model, 3 * heads * head_dim), w_out[0].reshape(heads * head_dim, d_model),
            w_up[0], w_down[0], norm_gain[0].astype(F32))
        grad_qkv = weight_grad(a, dqkv).reshape(1, d_model, 3, heads, head_dim)
        grad_out = weight_grad(o, dm).reshape(1, heads, head_dim, d_model)
        grad_up = weight_grad(b, du)[None]
        grad_down = weight_grad(zz, d)[None]
        loss = 0.5 * red[2, 0:1] / (n_batch * seq_len * d_model)
        return loss, grad_qkv, grad_out, grad_up, grad_down, red[None, 0:2]

    act_spec = P("data", None, None)
    weight_specs = (
        P("stage", None, None, "model", None),
        P("stage", "model", None, None),
        P("stage", None, "model"),
        P("stage", "model", None),
        P("stage", None, None),
    )
    grad_specs = (
        P(("data", "stage"), None, None, "model", None),
        P(("data", "stage"), "model", None, None),
        P(("data", "stage"), None, "model"),
        P(("data", "stage"), "model", None),
        P(("data", "stage"), None, None),
    )
    return jax.shard_map(
        device_fn,
        mesh=mesh,
        in_specs=(act_spec, act_spec) + weight_specs,
        out_specs=(P("data"),) + grad_specs,
        check_vma=False,
    )
```

time: 3680 us -> 1160 us (0.32)
  waiting for transfers between devices: 2410 us -> 0 us
  Pallas kernels: 0 us -> 1090 us
  matrix products: 723 us -> 40.2 us
  other arithmetic: 262 us -> 1.3 us
  local copies, waits for them, and re-layouts: 185 us -> 18.7 us
    psum x28 -> x0, waiting for transfers between devices: 2410 us -> none  [the longest x7 692 us: layer_forward(): mid_hid = h32 + lax.psum(attn_part, 'model')]
    pallas_call x0 -> x1, Pallas kernels: none -> 1090 us  [layer_step(): pl.pallas_call(kernel, out_shape=(out(d_model), out(d_model), out(d_model...]
    dot_general x119 -> x4, matrix products: 663 us -> 40.2 us  [weight_grad(): lax.dot_general(act, grad, (((0, 1), (0, 1)), ((), ())), preferred_elemen...]
    dynamic_slice x63 -> x0, local copies, waits for them, and re-layouts: 121 us -> none  [the longest x35 83 us: store_at(): old_val = lax.dynamic_index_in_dim(buf_all, index, 0, keepdims=False)]
    reduce_sum x49 -> x0, other arithmetic: 119 us -> none  [the longest x14 45.9 us: rms_backward(): d_gain = jnp.sum(d_norm * normed, axis=(0, 1))]
    dynamic_update_slice x35 -> x0, other arithmetic: 87.8 us -> none  [the longest x28 73.1 us: store_at(): lax.dynamic_update_index_in_dim(buf_all, jnp.where(is_valid, new_val, old...]
    sub x14 -> x0, matrix products: 60 us -> none  [causal_probs(): return jax.nn.softmax(scores, axis=-1)]
  transfers between devices with their start and end apart: 42 -> 0, of which waited for: 28 -> 0; matrix products, arithmetic and copies ran while one was open for 11% -> 0% of each run, Pallas kernels for 0% -> 0%
where the time goes in v1:
time: 1160 us
  Pallas kernels  1090 us (94%)
  matrix products  40.2 us (3%)
  local copies, waits for them, and re-layouts  18.7 us (2%)
    pallas_call x1, Pallas kernels, layer_step(): pl.pallas_call(kernel, out_shape=(out(d_model), out(d_model), out(d_model...  1090 us
    dot_general x4, matrix products, weight_grad(): lax.dot_general(act, grad, (((0, 1), (0, 1)), ((), ())), preferred_elemen...  40.2 us

profile of v1, /device:TPU:0, one launch (start us, length us, event | category | flops | bytes accessed | tf_op | source)
XLA Modules:
  0.0 1155.6 jit_solution(2196070049018367352)
XLA Ops:
  0.6 1.3 bitcast_convert_fusion.gain_ref
  1.9 4.3 copy.19
  6.2 3.7 copy.20.wqkv_h
  9.9 1093.0 %layer_step.1 = (bf16[12,128,1536]{2,1,0:T(8,128)(2,1)}, bf16[12,128,1536]{2,1,0:T(8,128)(2,1)}, bf16[12,128,1536]{2,1,0:T(8,128)(2,1)}, bf16[12,128,1536]{2,1,0...) custom-call(bf16[3,512,1536]{2,1,0:T(8,128)(2,1)} %x_ref.1, ...), custom_call_target="tpu_custom_call" | custom-call | tf_op jit(solution)/shard_map/layer_step/pallas_call | solution.py:539
  1102.8 1.2 slice.6
  1104.7 10.7 fusion
  1115.4 0.0 copy-start
  1115.4 8.1 copy.25
  1123.5 1.4 slice_bitcast_fusion
  1124.9 0.0 copy-done
  1124.9 0.0 slice-start
  1124.9 0.0 slice-start.2
  1124.9 5.9 fusion.1
  1130.8 0.0 slice-start.1
  1130.8 0.0 slice-start.3
  1130.8 13.1 %convolution_bitcast_fusion.1 = f32[1,1536,1536]{2,1,0:T(8,128)} fusion(bf16[12,128,1536]{2,1,0:T(8,128)(2,1)} %get-tuple-element.20, bf16[12,128,1536]{2,1,0:T(8,128)(2,1)} %get-tuple-element.21), kind=kOutput, calls=%fused_computation.1 | convolution fusion | flops 7247757312 | bytes 18874368 | tf_op jit(solution)/shard_map/dot_general | solution.py:572
  1144.0 0.0 slice-done
  1144.0 0.0 slice-done.2
  1144.0 0.0 slice-done.1
  1144.0 0.0 slice-done.3
  1144.0 10.5 convolution_bitcast_fusion
  (2 shorter events, 0.0 us)
Async XLA Ops:
  1115.4 9.5 copy-start
  1124.9 19.1 %slice-start = ((s8[4718592]{0:T(1024)(128)(4,1)}), s8[4194304]{0:T(1024)(128)(4,1)S(1)}, s32[]{:S(2)}) async-start(s8[4718592]{0:T(1024)(128)(4,1)} %bitcast.36), calls=%async_computation | async-start | bytes 8388608
  1124.9 19.1 %slice-start.2 = ((s8[4718592]{0:T(1024)(128)(4,1)}), s8[4194304]{0:T(1024)(128)(4,1)S(1)}, s32[]{:S(2)}) async-start(s8[4718592]{0:T(1024)(128)(4,1)} %bitcast.38), calls=%async_computation.2 | async-start | bytes 8388608
  1130.8 13.2 %slice-start.1 = ((s8[4718592]{0:T(1024)(128)(4,1)}), s8[524288]{0:T(1024)(128)(4,1)S(1)}, s32[]{:S(2)}) async-start(s8[4718592]{0:T(1024)(128)(4,1)} %bitcast.36), calls=%async_computation.1 | async-start | bytes 1048576
  1130.8 13.2 %slice-start.3 = ((s8[4718592]{0:T(1024)(128)(4,1)}), s8[524288]{0:T(1024)(128)(4,1)S(1)}, s32[]{:S(2)}) async-start(s8[4718592]{0:T(1024)(128)(4,1)} %bitcast.38), calls=%async_computation.3 | async-start | bytes 1048576

commit v2 on v0

v2 whole, which is shorter than its diff:
```python
import jax
import jax.numpy as jnp
from jax import lax
from jax.experimental import pallas as pl
from jax.experimental.pallas import tpu as pltpu
from jax.sharding import PartitionSpec as P

NORM_EPS = 1e-6
NEG_BIG = -1e30
MESH = pl.DeviceIdType.MESH
GELU_K = 0.7978845608028654
GELU_C = 0.044715
F32 = jnp.float32
BF16 = jnp.bfloat16


def dot_nn(a, b):
    return lax.dot_general(a, b, (((1,), (0,)), ((), ())), preferred_element_type=F32)


def dot_nt(a, b):
    return lax.dot_general(a, b, (((1,), (1,)), ((), ())), preferred_element_type=F32)


def dot_tn(a, b):
    return lax.dot_general(a, b, (((0,), (0,)), ((), ())), preferred_element_type=F32)


def rms_inverse(v32):
    return lax.rsqrt(jnp.mean(v32 * v32, axis=-1, keepdims=True) + NORM_EPS)


FWD_ORDER = (0, 1, 7, 5, 10, 13, 11, 2, 8, 6, 14, 12, 3, 4, 9)
BWD_ORDER = (10, 5, 0, 11, 2, 8, 12, 6, 3, 4, 13, 9, 7, 1, 14)


def lags(order):
    place = {phase: i for i, phase in enumerate(order)}
    lag = [0]
    for phase in range(1, len(order)):
        lag.append(lag[-1] + (1 if place[phase] < place[phase - 1] else 0))
    return lag


def layer_step(dims, x_in, y_target, w_qkv, w_out, w_up, w_down, gain):
    nz, ns = dims["model"], dims["stage"]
    n_seq, seq_len, d_model = x_in.shape
    n_slab, _, head_dim = w_qkv.shape
    qkv_w = n_slab * head_dim
    att_w = w_out.shape[0]
    ff_w = w_up.shape[1]
    n_head = att_w // head_dim
    tok = 128
    row = tok // nz
    per_seq = seq_len // tok
    n_unit = n_seq * per_seq
    scale = head_dim ** -0.5
    inv_count = 1.0 / (n_seq * seq_len * d_model)
    last_z, last_s = nz - 1, ns - 1
    sub_rows = 16
    n_send, n_recv, n_gath = 2, 3, 4

    def kernel(x_ref, y_ref, wqkv_h, wout_h, wup_h, wdown_h, gain_ref,
               a_out, b_out, d_out, dm_out, dqkv_out, o_out, z_out, du_out, red_out,
               wqkv, wout, wup, wdown, hslot, yslot, a_all, d_all, bbuf, dmbuf, xtmp,
               qkv_all, u_all, m_all, ost, zst, dust, dqkvst, datt, part,
               recv_r, recv_l, send_r, send_l, accq, hout, aout, dkacc, dvacc,
               gains, gain_next, lossacc, ga8, gb8, gx,
               w_sem, hsem, ysem, x_sem, gain_sem, hand_sem, save_sem,
               a_rs, d_rs, g1_sr, g1_sl, b_rs, dm_rs, g2_sr, g2_sl,
               rs_rr, rs_rl, rs_sr, rs_sl, loss_sem, gx_s, gx_r):
        z = lax.axis_index("model")
        st = lax.axis_index("stage")
        is_first = st == 0
        is_last = st == last_s

        def rdma(src, dst, ssem, rsem, **dev):
            return pltpu.make_async_remote_copy(src_ref=src, dst_ref=dst, send_sem=ssem, recv_sem=rsem,
                                                device_id=dev, device_id_type=MESH)

        def rows_of(k):
            return pl.ds(pl.multiple_of(k * row, row), row)

        qkv_copies = [pltpu.make_async_copy(wqkv_h.at[i], wqkv.at[:, pl.ds(i * head_dim, head_dim)], w_sem.at[i])
                      for i in range(n_slab)]
        w_copies = [pltpu.make_async_copy(src, dst, w_sem.at[n_slab + i])
                    for i, (src, dst) in enumerate(((wout_h, wout), (wup_h, wup), (wdown_h, wdown)))]

        def tokens_of(u):
            return lax.div(u, per_seq), pl.multiple_of(lax.rem(u, per_seq) * tok, tok)

        def x_copy(u):
            q, first = tokens_of(u)
            return pltpu.make_async_copy(x_ref.at[q, pl.ds(first, tok), :], a_all.at[u], hsem.at[u])

        def x_again(u):
            q, first = tokens_of(u)
            slot = lax.rem(u, n_send)
            return pltpu.make_async_copy(x_ref.at[q, pl.ds(first, tok), :], xtmp.at[slot], x_sem.at[slot])

        def y_copy(u):
            q, first = tokens_of(u)
            rs = pl.ds(pl.multiple_of(first + z * row, row), row)
            return pltpu.make_async_copy(y_ref.at[q, rs, :], yslot.at[u], ysem.at[u])

        @pl.when(is_first)
        def _():
            @pl.loop(0, n_unit)
            def _(u):
                x_copy(u).start()

        for cp in qkv_copies + w_copies:
            cp.start()

        @pl.when(is_last)
        def _():
            @pl.loop(0, n_unit)
            def _(u):
                y_copy(u).start()

        barrier = pltpu.get_barrier_semaphore()
        for i in range(1, nz * ns):
            dz, dst = i % nz, i // nz
            pl.semaphore_signal(barrier, inc=1, device_id_type=MESH,
                                device_id={"model": lax.rem(z + dz, nz), "stage": lax.rem(st + dst, ns)})
        qkv_all[...] = jnp.zeros_like(qkv_all)
        lossacc[...] = jnp.zeros_like(lossacc)
        ga8[...] = jnp.zeros_like(ga8)
        gb8[...] = jnp.zeros_like(gb8)
        gains[...] = gain_ref[...].astype(F32)
        pl.semaphore_wait(barrier, nz * ns - 1)

        def gain_send():
            return rdma(gains, gain_next, gain_sem.at[0], gain_sem.at[1], stage=st - 1)

        @pl.when(st > 0)
        def _():
            gain_send().start()

        class Gather:
            def __init__(self, buf, slot, rsem, sr, sl, sslot):
                self.buf, self.slot, self.rsem, self.sr, self.sl, self.sslot = buf, slot, rsem, sr, sl, sslot

            def block(self, j):
                return self.buf.at[self.slot, rows_of(j), :]

            def right(self, j):
                return rdma(self.block(j), self.block(j), self.sr.at[self.sslot, j], self.rsem.at[self.slot, j], model=z + 1)

            def left(self, j):
                return rdma(self.block(j), self.block(j), self.sl.at[self.sslot, j], self.rsem.at[self.slot, j], model=z - 1)

            def start(self):
                @pl.when(z < last_z)
                def _():
                    self.right(z).start()

                @pl.when(z > 0)
                def _():
                    self.left(z).start()

            def step(self, t):
                @pl.when(z >= t)
                def _():
                    self.right(z - t).wait_recv()

                    @pl.when(z < last_z)
                    def _():
                        self.right(z - t).start()

                @pl.when(z + t <= last_z)
                def _():
                    self.left(z + t).wait_recv()

                    @pl.when(z > 0)
                    def _():
                        self.left(z + t).start()

            def own(self):
                self.right(z).wait_recv()

            def drain(self):
                for j in range(nz):
                    @pl.when((z > j) & (z < last_z))
                    def _():
                        self.right(j).wait_send()

                    @pl.when((z < j) & (z > 0))
                    def _():
                        self.left(j).wait_send()

            def drain_own(self):
                @pl.when(z < last_z)
                def _():
                    self.right(z).wait_send()

                @pl.when(z > 0)
                def _():
                    self.left(z).wait_send()

        def gather_a(u):
            return Gather(a_all, u, a_rs, g1_sr, g1_sl, lax.rem(u, n_gath))

        def gather_d(u):
            return Gather(d_all, u, d_rs, g1_sr, g1_sl, lax.rem(u, n_gath))

        def gather_b(u):
            return Gather(bbuf, lax.rem(u, n_gath), b_rs, g2_sr, g2_sl, lax.rem(u, n_gath))

        def gather_dm(u):
            return Gather(dmbuf, lax.rem(u, n_gath), dm_rs, g2_sr, g2_sl, lax.rem(u, n_gath))

        class Scatter:
            def __init__(self, op, u):
                self.op, self.ss, self.rs = op, lax.rem(u, n_send), lax.rem(u, n_recv)

            def right(self, k):
                return rdma(send_r.at[self.op, self.ss, k - 1], recv_r.at[self.op, self.rs, k - 1],
                            rs_sr.at[self.op, self.ss, k - 1], rs_rr.at[self.op, self.rs, k - 1], model=z + 1)

            def left(self, k):
                return rdma(send_l.at[self.op, self.ss, k], recv_l.at[self.op, self.rs, k],
                            rs_sl.at[self.op, self.ss, k], rs_rl.at[self.op, self.rs, k], model=z - 1)

            def mine(self, k):
                return part[self.op, self.ss, rows_of(k), :]

            def step(self, t):
                op, ss, rs = self.op, self.ss, self.rs
                kr = last_z - t + z
                kl = t - last_z + z

                @pl.when(z == 0)
                def _():
                    send_r[op, ss, kr - 1] = self.mine(kr).astype(BF16)
                    self.right(kr).start()

                @pl.when(z == last_z)
                def _():
                    send_l[op, ss, kl] = self.mine(kl).astype(BF16)
                    self.left(kl).start()

                if t > 0:
                    @pl.when((z > 0) & (z <= t))
                    def _():
                        self.right(kr).wait_recv()
                        send_r[op, ss, kr - 1] = (self.mine(kr) + recv_r[op, rs, kr - 1].astype(F32)).astype(BF16)
                        self.right(kr).start()

                    @pl.when((z < last_z) & (last_z - z <= t))
                    def _():
                        self.left(kl).wait_recv()
                        send_l[op, ss, kl] = (self.mine(kl) + recv_l[op, rs, kl].astype(F32)).astype(BF16)
                        self.left(kl).start()

            def final(self):
                accq[...] = self.mine(z)

                @pl.when(z > 0)
                def _():
                    self.right(z).wait_recv()
                    accq[...] += recv_r[self.op, self.rs, z - 1].astype(F32)

                @pl.when(z < last_z)
                def _():
                    self.left(z).wait_recv()
                    accq[...] += recv_l[self.op, self.rs, z].astype(F32)

            def drain(self):
                for k in range(1, nz):
                    @pl.when(z < k)
                    def _():
                        self.right(k).wait_send()

                for k in range(nz - 1):
                    @pl.when(z > k)
                    def _():
                        self.left(k).wait_send()

        def save(kind, src, src_slot, dst, u):
            return pltpu.make_async_copy(src.at[src_slot], dst.at[u], save_sem.at[kind, lax.rem(u, n_gath)])

        def two(u):
            return lax.rem(u, n_send)

        def four(u):
            return lax.rem(u, n_gath)

        def save_a(u):
            return save(0, a_all, u, a_out, u)

        def save_o(u):
            return save(1, ost, two(u), o_out, u)

        def save_b(u):
            return save(2, bbuf, four(u), b_out, u)

        def save_z(u):
            return save(3, zst, two(u), z_out, u)

        def save_d(u):
            return save(4, d_all, u, d_out, u)

        def save_du(u):
            return save(5, dust, two(u), du_out, u)

        def save_dm(u):
            return save(6, dmbuf, four(u), dm_out, u)

        def save_dqkv(u):
            return save(7, dqkvst, two(u), dqkv_out, u)

        gain_a = gains[0:1, :]
        gain_b = gains[1:2, :]

        def hand_h(u, j):
            s = two(j)
            return rdma(hout.at[s], hslot.at[u], hand_sem.at[s, 3], hsem.at[u], stage=st + 1)

        def hand_block(buf, sems, u, j, dz, next_stage):
            s = two(j)
            return rdma(aout.at[s], buf.at[u, rows_of(z), :], hand_sem.at[s, dz + 1], sems.at[u, z],
                        model=z + dz, stage=next_stage)

        def hand_all(buf, sems, u, j, next_stage, act):
            act(hand_block(buf, sems, u, j, 0, next_stage))

            @pl.when(z < last_z)
            def _():
                act(hand_block(buf, sems, u, j, 1, next_stage))

            @pl.when(z > 0)
            def _():
                act(hand_block(buf, sems, u, j, -1, next_stage))

        def begin(cp):
            cp.start()

        def sent(cp):
            cp.wait_send()

        def softmax_of(u, p, i):
            first = u - p
            cols = pl.ds(i * head_dim, head_dim)
            q = qkv_all[u, :, cols]
            k = qkv_all[pl.ds(first, per_seq), :, pl.ds(att_w + i * head_dim, head_dim)].reshape(seq_len, head_dim)
            v = qkv_all[pl.ds(first, per_seq), :, pl.ds(2 * att_w + i * head_dim, head_dim)].reshape(seq_len, head_dim)
            sc = dot_nt(q, k) * scale
            q_pos = p * tok + lax.broadcasted_iota(jnp.int32, sc.shape, 0)
            k_pos = lax.broadcasted_iota(jnp.int32, sc.shape, 1)
            sc = jnp.where(k_pos <= q_pos, sc, NEG_BIG)
            e = jnp.exp(sc - jnp.max(sc, axis=-1, keepdims=True))
            pr = e * (1.0 / jnp.sum(e, axis=-1, keepdims=True))
            return q, k, v, pr

        def fold(v):
            return jnp.sum(v.reshape(v.shape[0] // 8, 8, d_model), axis=0)

        def f_enter(j, u):
            @pl.when(is_first)
            def _():
                x_copy(u).wait()
                hslot[u] = a_all[u, rows_of(z), :]
                for k in range(nz):
                    rs = pl.ds(k * row, row)
                    h32 = a_all[u, rs, :].astype(F32)
                    a_all[u, rs, :] = (h32 * rms_inverse(h32) * gain_a).astype(BF16)

        def f_gather_a(t):
            def run(j, u):
                @pl.when(st > 0)
                def _():
                    gather_a(u).step(t)
                    if t == last_z:
                        gather_a(u).own()
            return run

        def f_attention(j, u):
            @pl.when(j == 0)
            def _():
                for cp in qkv_copies:
                    cp.wait()
                w_copies[0].wait()

            s = two(u)
            p = lax.rem(u, per_seq)
            save_a(u).start()
            qkv_all[u] = dot_nn(a_all[u], wqkv[...]).astype(BF16)
            for i in range(n_head):
                _, _, v, pr = softmax_of(u, p, i)
                ost[s, :, pl.ds(i * head_dim, head_dim)] = dot_nn(pr.astype(BF16), v).astype(BF16)
            save_o(u).start()
            part[0, s] = dot_nn(ost[s], wout[...])
            Scatter(0, u).step(0)

        def scatter_step(op, t):
            def run(j, u):
                Scatter(op, u).step(t)
            return run

        def f_middle(j, u):
            sc = Scatter(0, u)
            sc.final()

            @pl.when(st > 0)
            def _():
                rdma(hout.at[0], hslot.at[u], hand_sem.at[0, 3], hsem.at[u], stage=st).wait_recv()

            m = hslot[u].astype(F32) + accq[...]
            m_all[u] = m
            bbuf[four(u), rows_of(z), :] = (m * rms_inverse(m) * gain_b).astype(BF16)
            gather_b(u).start()
            sc.drain()
            save_o(u).wait()

            @pl.when(st > 0)
            def _():
                gather_a(u).drain()

        def f_gather_b(t):
            def run(j, u):
                gather_b(u).step(t)
            return run

        def f_mlp(j, u):
            @pl.when(j == 0)
            def _():
                w_copies[1].wait()
                w_copies[2].wait()

            s = two(u)
            save_a(u).wait()
            save_b(u).start()
            u_all[u] = dot_nn(bbuf[four(u)], wup[...])

            def act(r, carry):
                rr = pl.ds(pl.multiple_of(r * sub_rows, sub_rows), sub_rows)
                v = u_all[u, rr, :]
                th = jnp.tanh(GELU_K * (v + GELU_C * (v * v * v)))
                zst[s, rr, :] = (0.5 * v * (1.0 + th)).astype(BF16)
                return carry

            lax.fori_loop(0, tok // sub_rows, act, 0)
            save_z(u).start()
            part[1, s] = dot_nn(zst[s], wdown[...])
            Scatter(1, u).step(0)

        def f_leave(j, u):
            sc = Scatter(1, u)
            sc.final()
            s = two(j)
            h_new = (m_all[u] + accq[...]).astype(BF16)

            @pl.when(st < last_s)
            def _():
                @pl.when(j == 0)
                def _():
                    gain_send().wait_recv()

                @pl.when(j >= n_send)
                def _():
                    hand_all(a_all, a_rs, u, j, st + 1, sent)
                    hand_h(u, j).wait_send()

                h32 = h_new.astype(F32)
                aout[s] = (h32 * rms_inverse(h32) * gain_next[0:1, :]).astype(BF16)
                hand_all(a_all, a_rs, u, j, st + 1, begin)
                hout[s] = h_new
                hand_h(u, j).start()

            @pl.when(is_last)
            def _():
                y_copy(u).wait()
                diff = h_new.astype(F32) - yslot[u].astype(F32)
                d_all[u, rows_of(z), :] = (diff * inv_count).astype(BF16)
                lossacc[...] += fold(diff * diff)

            sc.drain()
            gather_b(u).drain()
            gather_b(u).drain_own()
            save_b(u).wait()
            save_z(u).wait()

        def run_phases(order, phases, back):
            lag = lags(order)

            def body(i, carry):
                for phase in order:
                    j = i - lag[phase]

                    @pl.when((j >= 0) & (j < n_unit))
                    def _():
                        phases[phase](j, (n_unit - 1 - j) if back else j)
                return carry

            lax.fori_loop(0, n_unit + lag[-1], body, 0)

        def hand_finish(buf, sems, next_stage, with_h):
            for j in range(n_unit - n_send, n_unit):
                hand_all(buf, sems, j, j, next_stage, sent)
                if with_h:
                    hand_h(j, j).wait_send()

        run_phases(FWD_ORDER, (
            f_enter, f_gather_a(1), f_gather_a(2), f_gather_a(3), f_attention, scatter_step(0, 1), scatter_step(0, 2),
            f_middle, f_gather_b(1), f_gather_b(2), f_gather_b(3), f_mlp, scatter_step(1, 1), scatter_step(1, 2),
            f_leave), False)

        def loss_send():
            return rdma(lossacc, lossacc, loss_sem.at[0], loss_sem.at[1], stage=st - 1)

        @pl.when(is_last)
        def _():
            loss_send().start()

        @pl.when(st < last_s)
        def _():
            hand_finish(a_all, a_rs, st + 1, True)

        def b_enter(j, u):
            @pl.when(is_last)
            def _():
                gather_d(u).start()

        def b_gather_d(t):
            def run(j, u):
                gather_d(u).step(t)
                if t == last_z:
                    @pl.when(st < last_s)
                    def _():
                        gather_d(u).own()
            return run

        def b_mlp(j, u):
            s = two(u)
            save_d(u).start()
            part[0, s] = dot_nt(d_all[u], wdown[...])

            def act(r, carry):
                rr = pl.ds(pl.multiple_of(r * sub_rows, sub_rows), sub_rows)
                v = u_all[u, rr, :]
                v2 = v * v
                th = jnp.tanh(GELU_K * (v + GELU_C * (v2 * v)))
                slope = 0.5 * (1.0 + th) + 0.5 * v * (1.0 - th * th) * (GELU_K * (1.0 + 3.0 * GELU_C * v2))
                dust[s, rr, :] = (part[0, s, rr, :] * slope).astype(BF16)
                return carry

            lax.fori_loop(0, tok // sub_rows, act, 0)
            save_du(u).start()
            part[0, s] = dot_nt(dust[s], wup[...])
            Scatter(0, u).step(0)

        def b_middle(j, u):
            sc = Scatter(0, u)
            sc.final()
            m = m_all[u]
            inv = rms_inverse(m)
            normed = m * inv
            dn = accq[...]
            gb8[...] += fold(dn * normed)
            dn = dn * gain_b
            dm = d_all[u, rows_of(z), :].astype(F32) + inv * (
                dn - normed * jnp.mean(dn * normed, axis=-1, keepdims=True))
            m_all[u] = dm
            dmbuf[four(u), rows_of(z), :] = dm.astype(BF16)
            gather_dm(u).start()
            sc.drain()
            gather_d(u).drain()

            @pl.when(is_last)
            def _():
                gather_d(u).drain_own()

            save_du(u).wait()

        def b_gather_dm(t):
            def run(j, u):
                gather_dm(u).step(t)
            return run

        def b_attention(j, u):
            s = two(u)
            p = lax.rem(u, per_seq)
            save_d(u).wait()
            save_dm(u).start()

            @pl.when(is_first)
            def _():
                x_again(u).start()

            @pl.when(p == per_seq - 1)
            def _():
                dkacc[...] = jnp.zeros_like(dkacc)
                dvacc[...] = jnp.zeros_like(dvacc)

            datt[...] = dot_nt(dmbuf[four(u)], wout[...]).astype(BF16)
            p_rows = pl.ds(pl.multiple_of(p * tok, tok), tok)
            for h in range(n_head):
                cols = pl.ds(h * head_dim, head_dim)
                q, k, v, pr = softmax_of(u, p, h)
                da = datt[:, cols]
                dp = dot_nt(da, v)
                ds = (pr * (dp - jnp.sum(pr * dp, axis=-1, keepdims=True)) * scale).astype(BF16)
                dvacc[:, cols] += dot_tn(pr.astype(BF16), da)
                dkacc[:, cols] += dot_tn(ds, q)
                dqkvst[s, :, cols] = dot_nn(ds, k).astype(BF16)
            dqkvst[s, :, pl.ds(att_w, att_w)] = dkacc[p_rows, :].astype(BF16)
            dqkvst[s, :, pl.ds(2 * att_w, att_w)] = dvacc[p_rows, :].astype(BF16)
            save_dqkv(u).start()
            part[1, s] = dot_nt(dqkvst[s], wqkv[...])

            @pl.when(st > 0)
            def _():
                Scatter(1, u).step(0)

        def b_scatter(t):
            def run(j, u):
                @pl.when(st > 0)
                def _():
                    Scatter(1, u).step(t)
            return run

        def b_leave(j, u):
            s = two(j)

            @pl.when(st > 0)
            def _():
                sc = Scatter(1, u)
                sc.final()
                h32 = hslot[u].astype(F32)
                inv = rms_inverse(h32)
                normed = h32 * inv
                dn = accq[...]
                ga8[...] += fold(dn * normed)

                @pl.when(j >= n_send)
                def _():
                    hand_all(d_all, d_rs, u, j, st - 1, sent)

                dg = dn * gain_a
                aout[s] = (m_all[u] + inv * (
                    dg - normed * jnp.mean(dg * normed, axis=-1, keepdims=True))).astype(BF16)
                hand_all(d_all, d_rs, u, j, st - 1, begin)
                sc.drain()

            @pl.when(is_first)
            def _():
                x_again(u).wait()
                for k in range(nz):
                    rs = pl.ds(k * row, row)
                    h32 = xtmp[two(u), rs, :].astype(F32)
                    ga8[...] += fold(part[1, two(u), rs, :] * (h32 * rms_inverse(h32)))

            gather_dm(u).drain()
            gather_dm(u).drain_own()
            save_dm(u).wait()
            save_dqkv(u).wait()

        run_phases(BWD_ORDER, (
            b_enter, b_gather_d(1), b_gather_d(2), b_gather_d(3), b_mlp, scatter_step(0, 1), scatter_step(0, 2),
            b_middle, b_gather_dm(1), b_gather_dm(2), b_gather_dm(3), b_attention, b_scatter(1), b_scatter(2),
            b_leave), True)

        @pl.when(st > 0)
        def _():
            hand_finish(d_all, d_rs, st - 1, False)
            gain_send().wait_send()

        @pl.when(is_last)
        def _():
            loss_send().wait_send()

        @pl.when(st < last_s)
        def _():
            loss_send().wait_recv()

            @pl.when(st > 0)
            def _():
                loss_send().start()
                loss_send().wait_send()

        loss_row = jnp.sum(jnp.sum(lossacc[...], axis=0, keepdims=True), axis=1, keepdims=True)
        gx[z, 0:1, :] = jnp.sum(ga8[...], axis=0, keepdims=True)
        gx[z, 1:2, :] = jnp.sum(gb8[...], axis=0, keepdims=True)
        gx[z, 2:8, :] = jnp.broadcast_to(loss_row, (6, d_model))

        def gx_send(dz):
            return rdma(gx.at[z], gx.at[z], gx_s.at[dz], gx_r.at[z], model=lax.rem(z + dz, nz))

        def gx_recv(dz):
            k = lax.rem(z + dz, nz)
            return rdma(gx.at[k], gx.at[k], gx_s.at[dz], gx_r.at[k], model=k)

        for dz in range(1, nz):
            gx_send(dz).start()
        for dz in range(1, nz):
            gx_recv(dz).wait_recv()
        red_out[...] = gx[0] + gx[1] + gx[2] + gx[3]
        for dz in range(1, nz):
            gx_send(dz).wait_send()

    any_spec = pl.BlockSpec(memory_space=pl.ANY)
    vmem_spec = pl.BlockSpec(memory_space=pltpu.VMEM)

    def out(width):
        return jax.ShapeDtypeStruct((n_unit, tok, width), BF16)

    dma = pltpu.SemaphoreType.DMA
    vmem = pltpu.VMEM
    return pl.pallas_call(
        kernel,
        out_shape=(out(d_model), out(d_model), out(d_model), out(d_model), out(qkv_w), out(att_w), out(ff_w), out(ff_w),
                   jax.ShapeDtypeStruct((8, d_model), F32)),
        in_specs=[any_spec] * 6 + [vmem_spec],
        out_specs=(any_spec,) * 8 + (vmem_spec,),
        scratch_shapes=[
            vmem((d_model, qkv_w), BF16), vmem((att_w, d_model), BF16), vmem((d_model, ff_w), BF16), vmem((ff_w, d_model), BF16),
            vmem((n_unit, row, d_model), BF16), vmem((n_unit, row, d_model), BF16),
            vmem((n_unit, tok, d_model), BF16), vmem((n_unit, tok, d_model), BF16),
            vmem((n_gath, tok, d_model), BF16), vmem((n_gath, tok, d_model), BF16), vmem((n_send, tok, d_model), BF16),
            vmem((n_unit, tok, qkv_w), BF16), vmem((n_unit, tok, ff_w), F32), vmem((n_unit, row, d_model), F32),
            vmem((n_send, tok, att_w), BF16), vmem((n_send, tok, ff_w), BF16), vmem((n_send, tok, ff_w), BF16),
            vmem((n_send, tok, qkv_w), BF16), vmem((tok, att_w), BF16), vmem((2, n_send, tok, d_model), F32),
            vmem((2, n_recv, nz - 1, row, d_model), BF16), vmem((2, n_recv, nz - 1, row, d_model), BF16),
            vmem((2, n_send, nz - 1, row, d_model), BF16), vmem((2, n_send, nz - 1, row, d_model), BF16),
            vmem((row, d_model), F32), vmem((n_send, row, d_model), BF16), vmem((n_send, row, d_model), BF16),
            vmem((seq_len, att_w), F32), vmem((seq_len, att_w), F32),
            vmem((2, d_model), F32), vmem((2, d_model), F32),
            vmem((8, d_model), F32), vmem((8, d_model), F32), vmem((8, d_model), F32), vmem((nz, 8, d_model), F32),
            dma((n_slab + 3,)), dma((n_unit,)), dma((n_unit,)), dma((n_send,)), dma((2,)), dma((n_send, 4)), dma((8, n_gath)),
            dma((n_unit, nz)), dma((n_unit, nz)), dma((n_gath, nz)), dma((n_gath, nz)),
            dma((n_gath, nz)), dma((n_gath, nz)), dma((n_gath, nz)), dma((n_gath, nz)),
            dma((2, n_recv, nz - 1)), dma((2, n_recv, nz - 1)), dma((2, n_send, nz - 1)), dma((2, n_send, nz - 1)),
            dma((2,)), dma((nz,)), dma((nz,)),
        ],
        compiler_params=pltpu.CompilerParams(collective_id=0, has_side_effects=True, vmem_limit_bytes=67_043_328),
        name="layer_step",
    )(x_in, y_target, w_qkv, w_out, w_up, w_down, gain)


def weight_grad(act, grad):
    return lax.dot_general(act, grad, (((0, 1), (0, 1)), ((), ())), preferred_element_type=F32)


def solution(mesh):
    dims = dict(mesh.shape)

    def device_fn(x_in, y_target, w_qkv, w_out, w_up, w_down, norm_gain):
        n_batch, seq_len, d_model = x_in.shape
        heads, head_dim = w_qkv.shape[3], w_qkv.shape[4]
        a, b, d, dm, dqkv, o, zz, du, red = layer_step(
            dims, x_in, y_target,
            w_qkv[0].transpose(1, 2, 0, 3).reshape(3 * heads, d_model, head_dim),
            w_out[0].reshape(heads * head_dim, d_model), w_up[0], w_down[0], norm_gain[0])
        grad_qkv = weight_grad(a, dqkv).reshape(1, d_model, 3, heads, head_dim)
        grad_out = weight_grad(o, dm).reshape(1, heads, head_dim, d_model)
        grad_up = weight_grad(b, du)[None]
        grad_down = weight_grad(zz, d)[None]
        loss = 0.5 * red[2, 0:1] / (n_batch * seq_len * d_model)
        return loss, grad_qkv, grad_out, grad_up, grad_down, red[None, 0:2]

    act_spec = P("data", None, None)
    weight_specs = (
        P("stage", None, None, "model", None),
        P("stage", "model", None, None),
        P("stage", None, "model"),
        P("stage", "model", None),
        P("stage", None, None),
    )
    grad_specs = (
        P(("data", "stage"), None, None, "model", None),
        P(("data", "stage"), "model", None, None),
        P(("data", "stage"), None, "model"),
        P(("data", "stage"), "model", None),
        P(("data", "stage"), None, None),
    )
    return jax.shard_map(
        device_fn,
        mesh=mesh,
        in_specs=(act_spec, act_spec) + weight_specs,
        out_specs=(P("data"),) + grad_specs,
        check_vma=False,
    )
```

time: 3680 us -> 857 us (0.23)
  waiting for transfers between devices: 2410 us -> 0 us
  Pallas kernels: 0 us -> 803 us
  matrix products: 723 us -> 40.2 us
  other arithmetic: 262 us -> 0.01 us
  local copies, waits for them, and re-layouts: 185 us -> 10.7 us
    psum x28 -> x0, waiting for transfers between devices: 2410 us -> none  [the longest x7 692 us: layer_forward(): mid_hid = h32 + lax.psum(attn_part, 'model')]
    pallas_call x0 -> x1, Pallas kernels: none -> 803 us  [layer_step(): pl.pallas_call(kernel, out_shape=(out(d_model), out(d_model), out(d_model...]
    dot_general x119 -> x4, matrix products: 663 us -> 40.2 us  [weight_grad(): lax.dot_general(act, grad, (((0, 1), (0, 1)), ((), ())), preferred_elemen...]
    dynamic_slice x63 -> x0, local copies, waits for them, and re-layouts: 121 us -> none  [the longest x35 83 us: store_at(): old_val = lax.dynamic_index_in_dim(buf_all, index, 0, keepdims=False)]
    reduce_sum x49 -> x0, other arithmetic: 119 us -> none  [the longest x14 45.9 us: rms_backward(): d_gain = jnp.sum(d_norm * normed, axis=(0, 1))]
    dynamic_update_slice x35 -> x0, other arithmetic: 87.8 us -> none  [the longest x28 73.1 us: store_at(): lax.dynamic_update_index_in_dim(buf_all, jnp.where(is_valid, new_val, old...]
    sub x14 -> x0, matrix products: 60 us -> none  [causal_probs(): return jax.nn.softmax(scores, axis=-1)]
  transfers between devices with their start and end apart: 42 -> 0, of which waited for: 28 -> 0; matrix products, arithmetic and copies ran while one was open for 11% -> 0% of each run, Pallas kernels for 0% -> 0%
where the time goes in v2:
time: 857 us
  Pallas kernels  803 us (94%)
  matrix products  40.2 us (5%)
  local copies, waits for them, and re-layouts  10.7 us (1%)
    pallas_call x1, Pallas kernels, layer_step(): pl.pallas_call(kernel, out_shape=(out(d_model), out(d_model), out(d_model...  803 us
    dot_general x4, matrix products, weight_grad(): lax.dot_general(act, grad, (((0, 1), (0, 1)), ((), ())), preferred_elemen...  40.2 us

profile of v2, /device:TPU:0, one launch (start us, length us, event | category | flops | bytes accessed | tf_op | source)
XLA Modules:
  0.0 856.8 jit_solution(1265529855405079061)
XLA Ops:
  0.6 803.4 %layer_step.1 = (bf16[12,128,1536]{2,1,0:T(8,128)(2,1)}, bf16[12,128,1536]{2,1,0:T(8,128)(2,1)}, bf16[12,128,1536]{2,1,0:T(8,128)(2,1)}, bf16[12,128,1536]{2,1,0...) custom-call(bf16[3,512,1536]{2,1,0:T(8,128)(2,1)} %x_ref.1, ...), custom_call_target="tpu_custom_call" | custom-call | tf_op jit(solution)/shard_map/layer_step/pallas_call | solution.py:710
  804.0 1.2 slice.6
  805.9 10.7 %fusion = f32[1536,1152,1]{0,1,2:T(8,128)} fusion(bf16[12,128,1536]{2,1,0:T(8,128)(2,1)} %get-tuple-element.16, bf16[12,128,1152]{2,1,0:T(8,128)(2,1)} %get-tuple-element.17), kind=kOutput, calls=%fused_computation.3 | convolution fusion | flops 5435817984 | bytes 15335424 | tf_op jit(solution)/shard_map/dot_general | solution.py:742
  816.5 0.0 copy-start
  816.5 8.1 copy.17
  824.7 1.4 slice_bitcast_fusion
  826.1 0.0 copy-done
  826.1 0.0 slice-start
  826.1 0.0 slice-start.2
  826.1 5.9 fusion.1
  832.0 0.0 slice-start.1
  832.0 0.0 slice-start.3
  832.0 13.1 %convolution_bitcast_fusion.1 = f32[1,1536,1536]{2,1,0:T(8,128)} fusion(bf16[12,128,1536]{2,1,0:T(8,128)(2,1)} %get-tuple-element.20, bf16[12,128,1536]{2,1,0:T(8,128)(2,1)} %get-tuple-element.21), kind=kOutput, calls=%fused_computation.1 | convolution fusion | flops 7247757312 | bytes 18874368 | tf_op jit(solution)/shard_map/dot_general | solution.py:742
  845.1 0.0 slice-done
  845.1 0.0 slice-done.2
  845.2 0.0 slice-done.1
  845.2 0.0 slice-done.3
  845.2 10.5 %convolution_bitcast_fusion = f32[1,1536,1536]{2,1,0:T(8,128)} fusion(bf16[12,128,1536]{2,1,0:T(8,128)(2,1)S(1)} %bitcast.42, bf16[12,128,1536]{2,1,0:T(8,128)(2,1)S(1)} %bitcast.40), kind=kOutput, calls=%fused_computation | convolution fusion | flops 7247757312 | bytes 18874368 | tf_op jit(solution)/shard_map/dot_general | solution.py:742
  (2 shorter events, 0.0 us)
Async XLA Ops:
  816.5 9.5 %copy-start = (bf16[12,128,384]{2,1,0:T(8,128)(2,1)S(1)}, bf16[12,128,384]{2,1,0:T(8,128)(2,1)}, u32[]{:S(2)}) copy-start(bf16[12,128,384]{2,1,0:T(8,128)(2,1)} %get-tuple-element.18) | copy-start | bytes 3538948
  826.1 19.1 %slice-start = ((s8[4718592]{0:T(1024)(128)(4,1)}), s8[4194304]{0:T(1024)(128)(4,1)S(1)}, s32[]{:S(2)}) async-start(s8[4718592]{0:T(1024)(128)(4,1)} %bitcast.39), calls=%async_computation | async-start | bytes 8388608
  826.1 19.1 %slice-start.2 = ((s8[4718592]{0:T(1024)(128)(4,1)}), s8[4194304]{0:T(1024)(128)(4,1)S(1)}, s32[]{:S(2)}) async-start(s8[4718592]{0:T(1024)(128)(4,1)} %bitcast.41), calls=%async_computation.2 | async-start | bytes 8388608
  832.0 13.2 %slice-start.1 = ((s8[4718592]{0:T(1024)(128)(4,1)}), s8[524288]{0:T(1024)(128)(4,1)S(1)}, s32[]{:S(2)}) async-start(s8[4718592]{0:T(1024)(128)(4,1)} %bitcast.39), calls=%async_computation.1 | async-start | bytes 1048576
  832.0 13.2 %slice-start.3 = ((s8[4718592]{0:T(1024)(128)(4,1)}), s8[524288]{0:T(1024)(128)(4,1)S(1)}, s32[]{:S(2)}) async-start(s8[4718592]{0:T(1024)(128)(4,1)} %bitcast.41), calls=%async_computation.3 | async-start | bytes 1048576

commit v3 on v2

v3 whole, which is shorter than its diff:
```python
import jax
import jax.numpy as jnp
from jax import lax
from jax.experimental import pallas as pl
from jax.experimental.pallas import tpu as pltpu
from jax.sharding import PartitionSpec as P

NORM_EPS = 1e-6
NEG_BIG = -1e30
MESH = pl.DeviceIdType.MESH
GELU_K = 0.7978845608028654
GELU_C = 0.044715
F32 = jnp.float32
BF16 = jnp.bfloat16


def dot_nn(a, b):
    return lax.dot_general(a, b, (((1,), (0,)), ((), ())), preferred_element_type=F32)


def dot_nt(a, b):
    return lax.dot_general(a, b, (((1,), (1,)), ((), ())), preferred_element_type=F32)


def dot_tn(a, b):
    return lax.dot_general(a, b, (((0,), (0,)), ((), ())), preferred_element_type=F32)


def rms_inverse(v32):
    return lax.rsqrt(jnp.mean(v32 * v32, axis=-1, keepdims=True) + NORM_EPS)


FWD_ORDER = (4, 10, 0, 1, 7, 8, 5, 2, 9, 6, 3)
BWD_ORDER = (9, 3, 6, 4, 1, 10, 0, 5, 7, 8, 2)


def lags(order):
    place = {phase: i for i, phase in enumerate(order)}
    lag = [0]
    for phase in range(1, len(order)):
        lag.append(lag[-1] + (1 if place[phase] < place[phase - 1] else 0))
    return lag


def layer_step(dims, x_in, y_target, w_qkv, w_out, w_up, w_down, gain):
    nz, ns = dims["model"], dims["stage"]
    n_seq, seq_len, d_model = x_in.shape
    n_slab, _, head_dim = w_qkv.shape
    qkv_w = n_slab * head_dim
    att_w = w_out.shape[0]
    ff_w = w_up.shape[1]
    n_head = att_w // head_dim
    tok = 128
    row = tok // nz
    per_seq = seq_len // tok
    n_unit = n_seq * per_seq
    scale = head_dim ** -0.5
    inv_count = 1.0 / (n_seq * seq_len * d_model)
    last_z, last_s = nz - 1, ns - 1
    sub_rows = 16
    half = tok // 2
    n_send, n_recv, n_gath, n_hand = 1, 2, 3, 2
    quarters = range(2)

    def kernel(x_ref, y_ref, wqkv_h, wout_h, wup_h, wdown_h, gain_ref,
               a_out, b_out, d_out, dm_out, dqkv_out, o_out, z_out, du_out, red_out,
               wqkv, wout, wup, wdown, hslot, yslot, a_all, d_all, bbuf, dmbuf, xtmp,
               qkv_all, u_all, m_all, ost, zst, dust, dqkvst, datt, part,
               recv_o, recv_i, send_p, hout, aout, dkacc, dvacc,
               gains, gain_next, lossacc, ga8, gb8, gx,
               w_sem, hsem, ysem, x_sem, gain_sem, hand_sem, save_sem,
               a_rs, d_rs, g1_si, g1_so, b_rs, dm_rs, g2_si, g2_so,
               rs_ro, rs_ri, rs_s, loss_sem, gx_s, gx_r):
        z = lax.axis_index("model")
        st = lax.axis_index("stage")
        is_first = st == 0
        is_last = st == last_s
        inner = (z > 0) & (z < last_z)
        outer = (z == 0) | (z == last_z)
        side = lax.div(z, 2)
        near = 2 * side
        far = 2 - near
        inner_peer = 1 + lax.rem(z, 2)
        outer_peer = last_z * side
        my_half = pl.ds(pl.multiple_of(side * half, half), half)

        def rdma(src, dst, ssem, rsem, **dev):
            return pltpu.make_async_remote_copy(src_ref=src, dst_ref=dst, send_sem=ssem, recv_sem=rsem,
                                                device_id=dev, device_id_type=MESH)

        def rows_of(k):
            return pl.ds(pl.multiple_of(k * row, row), row)

        qkv_copies = [pltpu.make_async_copy(wqkv_h.at[i], wqkv.at[:, pl.ds(i * head_dim, head_dim)], w_sem.at[i])
                      for i in range(n_slab)]
        w_copies = [pltpu.make_async_copy(src, dst, w_sem.at[n_slab + i])
                    for i, (src, dst) in enumerate(((wout_h, wout), (wup_h, wup), (wdown_h, wdown)))]

        def tokens_of(u):
            return lax.div(u, per_seq), pl.multiple_of(lax.rem(u, per_seq) * tok, tok)

        def x_copy(u):
            q, first = tokens_of(u)
            return pltpu.make_async_copy(x_ref.at[q, pl.ds(first, tok), :], a_all.at[u], hsem.at[u])

        def x_again(u):
            q, first = tokens_of(u)
            slot = lax.rem(u, n_send)
            return pltpu.make_async_copy(x_ref.at[q, pl.ds(first, tok), :], xtmp.at[slot], x_sem.at[slot])

        def y_copy(u):
            q, first = tokens_of(u)
            rs = pl.ds(pl.multiple_of(first + side * half, half), half)
            slot = lax.rem(u, n_hand)
            return pltpu.make_async_copy(y_ref.at[q, rs, :], yslot.at[slot], ysem.at[slot])

        @pl.when(is_first)
        def _():
            @pl.loop(0, n_unit)
            def _(u):
                x_copy(u).start()

        for cp in qkv_copies + w_copies:
            cp.start()

        barrier = pltpu.get_barrier_semaphore()
        for i in range(1, nz * ns):
            dz, dst = i % nz, i // nz
            pl.semaphore_signal(barrier, inc=1, device_id_type=MESH,
                                device_id={"model": lax.rem(z + dz, nz), "stage": lax.rem(st + dst, ns)})
        qkv_all[...] = jnp.zeros_like(qkv_all)
        lossacc[...] = jnp.zeros_like(lossacc)
        ga8[...] = jnp.zeros_like(ga8)
        gb8[...] = jnp.zeros_like(gb8)
        gains[...] = gain_ref[...].astype(F32)
        pl.semaphore_wait(barrier, nz * ns - 1)

        def gain_send():
            return rdma(gains, gain_next, gain_sem.at[0], gain_sem.at[1], stage=st - 1)

        @pl.when(st > 0)
        def _():
            gain_send().start()

        class Gather:
            def __init__(self, buf, slot, rsem, si, so, sslot):
                self.buf, self.slot, self.rsem, self.si, self.so, self.sslot = buf, slot, rsem, si, so, sslot

            def block(self, k):
                return self.buf.at[self.slot, rows_of(k), :]

            def inward(self, k, q):
                return rdma(self.block(k), self.block(k), self.si.at[self.sslot, q], self.rsem.at[self.slot, k],
                            model=inner_peer)

            def outward(self, k):
                return rdma(self.block(k), self.block(k), self.so.at[self.sslot, k], self.rsem.at[self.slot, k],
                            model=outer_peer)

            def send(self, q):
                self.inward(near + q, q).start()
                self.outward(near + q).start()

            def relay(self):
                @pl.when(inner)
                def _():
                    for q in quarters:
                        self.outward(far + q).wait_recv()
                        self.outward(far + q).start()

            def collect(self):
                @pl.when(outer)
                def _():
                    for k in range(nz):
                        self.outward(k).wait_recv()

            def own(self):
                @pl.when(inner)
                def _():
                    for q in quarters:
                        self.outward(near + q).wait_recv()

            def drain(self):
                @pl.when(inner)
                def _():
                    for q in quarters:
                        self.outward(far + q).wait_send()

            def drain_own(self):
                @pl.when(inner)
                def _():
                    for q in quarters:
                        self.inward(near + q, q).wait_send()
                        self.outward(near + q).wait_send()

        def gather_a(u):
            return Gather(a_all, u, a_rs, g1_si, g1_so, lax.rem(u, n_gath))

        def gather_d(u):
            return Gather(d_all, u, d_rs, g1_si, g1_so, lax.rem(u, n_gath))

        def gather_b(u):
            return Gather(bbuf, lax.rem(u, n_gath), b_rs, g2_si, g2_so, lax.rem(u, n_gath))

        def gather_dm(u):
            return Gather(dmbuf, lax.rem(u, n_gath), dm_rs, g2_si, g2_so, lax.rem(u, n_gath))

        class Scatter:
            def __init__(self, op, u):
                self.op, self.ss, self.rs = op, lax.rem(u, n_send), lax.rem(u, n_recv)

            def in_copy(self, k):
                return rdma(send_p.at[self.op, self.ss, k], recv_o.at[self.op, self.rs, k],
                            rs_s.at[self.op, self.ss, k], rs_ro.at[self.op, self.rs, k], model=inner_peer)

            def cross_copy(self, k, q):
                return rdma(send_p.at[self.op, self.ss, k], recv_i.at[self.op, self.rs, q],
                            rs_s.at[self.op, self.ss, k], rs_ri.at[self.op, self.rs, q], model=inner_peer)

            def mine(self, k):
                return part[self.op, self.ss, rows_of(k), :]

            def start(self):
                @pl.when(outer)
                def _():
                    for k in (far, far + 1, near, near + 1):
                        send_p[self.op, self.ss, k] = self.mine(k).astype(BF16)
                        self.in_copy(k).start()

            def relay(self):
                @pl.when(inner)
                def _():
                    for q in quarters:
                        k = far + q
                        self.in_copy(k).wait_recv()
                        send_p[self.op, self.ss, k] = (
                            self.mine(k) + recv_o[self.op, self.rs, k].astype(F32)).astype(BF16)
                        self.cross_copy(k, q).start()

            def total(self, q):
                k = near + q
                self.in_copy(k).wait_recv()
                self.cross_copy(k, q).wait_recv()
                return (self.mine(k) + recv_o[self.op, self.rs, k].astype(F32)) + recv_i[self.op, self.rs, q].astype(F32)

            def drain(self):
                @pl.when(outer)
                def _():
                    for k in range(nz):
                        self.in_copy(k).wait_send()

                @pl.when(inner)
                def _():
                    for q in quarters:
                        self.cross_copy(far + q, q).wait_send()

        def save(kind, src, src_slot, dst, u):
            return pltpu.make_async_copy(src.at[src_slot], dst.at[u], save_sem.at[kind, lax.rem(u, n_gath)])

        def sslot(u):
            return lax.rem(u, n_send)

        def gslot(u):
            return lax.rem(u, n_gath)

        def q_rows(q):
            return pl.ds(q * row, row)

        def save_a(u):
            return save(0, a_all, u, a_out, u)

        def save_o(u):
            return save(1, ost, sslot(u), o_out, u)

        def save_b(u):
            return save(2, bbuf, gslot(u), b_out, u)

        def save_z(u):
            return save(3, zst, sslot(u), z_out, u)

        def save_d(u):
            return save(4, d_all, u, d_out, u)

        def save_du(u):
            return save(5, dust, sslot(u), du_out, u)

        def save_dm(u):
            return save(6, dmbuf, gslot(u), dm_out, u)

        def save_dqkv(u):
            return save(7, dqkvst, sslot(u), dqkv_out, u)

        gain_a = gains[0:1, :]
        gain_b = gains[1:2, :]

        def hand_h(u, j):
            s = lax.rem(j, n_hand)
            return rdma(hout.at[s], hslot.at[u], hand_sem.at[s, 6], hsem.at[u], stage=st + 1)

        def hand_quarter(buf, sems, u, j, q, next_stage, act):
            s = lax.rem(j, n_hand)
            k = near + q
            for i, peer in enumerate((inner_peer, outer_peer, z)):
                act(rdma(aout.at[s, q_rows(q), :], buf.at[u, rows_of(k), :], hand_sem.at[s, 3 * q + i], sems.at[u, k],
                         model=peer, stage=next_stage))

        def hand_sent(buf, sems, u, j, next_stage, with_h):
            for q in quarters:
                hand_quarter(buf, sems, u, j, q, next_stage, sent)
            if with_h:
                hand_h(u, j).wait_send()

        def begin(cp):
            cp.start()

        def sent(cp):
            cp.wait_send()

        def softmax_of(u, p, i):
            first = u - p
            cols = pl.ds(i * head_dim, head_dim)
            q = qkv_all[u, :, cols]
            k = qkv_all[pl.ds(first, per_seq), :, pl.ds(att_w + i * head_dim, head_dim)].reshape(seq_len, head_dim)
            v = qkv_all[pl.ds(first, per_seq), :, pl.ds(2 * att_w + i * head_dim, head_dim)].reshape(seq_len, head_dim)
            sc = dot_nt(q, k) * scale
            q_pos = p * tok + lax.broadcasted_iota(jnp.int32, sc.shape, 0)
            k_pos = lax.broadcasted_iota(jnp.int32, sc.shape, 1)
            sc = jnp.where(k_pos <= q_pos, sc, NEG_BIG)
            e = jnp.exp(sc - jnp.max(sc, axis=-1, keepdims=True))
            pr = e * (1.0 / jnp.sum(e, axis=-1, keepdims=True))
            return q, k, v, pr

        def fold(v):
            return jnp.sum(v.reshape(v.shape[0] // 8, 8, d_model), axis=0)

        def f_enter(j, u):
            @pl.when(is_first)
            def _():
                x_copy(u).wait()
                hslot[u] = a_all[u, my_half, :]
                for k in range(nz):
                    rs = pl.ds(k * row, row)
                    h32 = a_all[u, rs, :].astype(F32)
                    a_all[u, rs, :] = (h32 * rms_inverse(h32) * gain_a).astype(BF16)

        def f_relay_a(j, u):
            @pl.when(st > 0)
            def _():
                gather_a(u).relay()

        def f_collect_a(j, u):
            @pl.when(st > 0)
            def _():
                gather_a(u).collect()
                gather_a(u).own()

        def f_attention(j, u):
            @pl.when(j == 0)
            def _():
                for cp in qkv_copies:
                    cp.wait()
                w_copies[0].wait()

            s = sslot(u)
            p = lax.rem(u, per_seq)
            save_a(u).start()
            qkv_all[u] = dot_nn(a_all[u], wqkv[...]).astype(BF16)
            for i in range(n_head):
                _, _, v, pr = softmax_of(u, p, i)
                ost[s, :, pl.ds(i * head_dim, head_dim)] = dot_nn(pr.astype(BF16), v).astype(BF16)
            save_o(u).start()
            part[0, s] = dot_nn(ost[s], wout[...])
            Scatter(0, u).start()

        def scatter_relay(op):
            def run(j, u):
                Scatter(op, u).relay()
            return run

        def f_middle(j, u):
            sc = Scatter(0, u)

            @pl.when(inner)
            def _():
                @pl.when(st > 0)
                def _():
                    rdma(hout.at[0], hslot.at[u], hand_sem.at[0, 6], hsem.at[u], stage=st).wait_recv()

                for q in quarters:
                    m = hslot[u, q_rows(q), :].astype(F32) + sc.total(q)
                    m_all[u, q_rows(q), :] = m
                    bbuf[gslot(u), rows_of(near + q), :] = (m * rms_inverse(m) * gain_b).astype(BF16)
                    gather_b(u).send(q)

            sc.drain()
            save_o(u).wait()

            @pl.when(st > 0)
            def _():
                gather_a(u).drain()

        def f_relay_b(j, u):
            gather_b(u).relay()

        def f_collect_b(j, u):
            gather_b(u).collect()

        def f_mlp(j, u):
            @pl.when(j == 0)
            def _():
                w_copies[1].wait()
                w_copies[2].wait()

            s = sslot(u)
            save_a(u).wait()
            save_b(u).start()

            @pl.when(is_last & inner)
            def _():
                y_copy(u).start()

            u_all[u] = dot_nn(bbuf[gslot(u)], wup[...])

            def act(r, carry):
                rr = pl.ds(pl.multiple_of(r * sub_rows, sub_rows), sub_rows)
                v = u_all[u, rr, :]
                th = jnp.tanh(GELU_K * (v + GELU_C * (v * v * v)))
                zst[s, rr, :] = (0.5 * v * (1.0 + th)).astype(BF16)
                return carry

            lax.fori_loop(0, tok // sub_rows, act, 0)
            save_z(u).start()
            part[1, s] = dot_nn(zst[s], wdown[...])
            Scatter(1, u).start()

        def f_leave(j, u):
            sc = Scatter(1, u)
            s = lax.rem(j, n_hand)

            @pl.when((j == 0) & (st < last_s))
            def _():
                gain_send().wait_recv()

            @pl.when(inner)
            def _():
                @pl.when(st < last_s)
                def _():
                    @pl.when(j >= n_hand)
                    def _():
                        hand_sent(a_all, a_rs, u, j, st + 1, True)

                @pl.when(is_last)
                def _():
                    y_copy(u).wait()

                for q in quarters:
                    h_new = (m_all[u, q_rows(q), :] + sc.total(q)).astype(BF16)
                    h32 = h_new.astype(F32)

                    @pl.when(st < last_s)
                    def _():
                        aout[s, q_rows(q), :] = (h32 * rms_inverse(h32) * gain_next[0:1, :]).astype(BF16)
                        hand_quarter(a_all, a_rs, u, j, q, st + 1, begin)
                        hout[s, q_rows(q), :] = h_new

                    @pl.when(is_last)
                    def _():
                        diff = h32 - yslot[lax.rem(u, n_hand), q_rows(q), :].astype(F32)
                        d_all[u, rows_of(near + q), :] = (diff * inv_count).astype(BF16)
                        lossacc[...] += fold(diff * diff)

                @pl.when(st < last_s)
                def _():
                    hand_h(u, j).start()

            sc.drain()
            gather_b(u).drain()
            gather_b(u).drain_own()
            save_b(u).wait()
            save_z(u).wait()

        def run_phases(order, phases, back):
            lag = lags(order)

            def body(i, carry):
                for phase in order:
                    j = i - lag[phase]

                    @pl.when((j >= 0) & (j < n_unit))
                    def _():
                        phases[phase](j, (n_unit - 1 - j) if back else j)
                return carry

            lax.fori_loop(0, n_unit + lag[-1], body, 0)

        def hand_finish(buf, sems, next_stage, with_h):
            @pl.when(inner)
            def _():
                for j in range(n_unit - n_hand, n_unit):
                    hand_sent(buf, sems, j, j, next_stage, with_h)

        run_phases(FWD_ORDER, (
            f_enter, f_relay_a, f_collect_a, f_attention, scatter_relay(0), f_middle, f_relay_b, f_collect_b, f_mlp,
            scatter_relay(1), f_leave), False)

        def loss_send():
            return rdma(lossacc, lossacc, loss_sem.at[0], loss_sem.at[1], stage=st - 1)

        @pl.when(is_last)
        def _():
            loss_send().start()

        @pl.when(st < last_s)
        def _():
            hand_finish(a_all, a_rs, st + 1, True)

        def b_enter(j, u):
            @pl.when(is_last & inner)
            def _():
                for q in quarters:
                    gather_d(u).send(q)

        def b_relay_d(j, u):
            gather_d(u).relay()

        def b_collect_d(j, u):
            gather_d(u).collect()

            @pl.when(st < last_s)
            def _():
                gather_d(u).own()

        def b_mlp(j, u):
            s = sslot(u)
            save_d(u).start()
            part[0, s] = dot_nt(d_all[u], wdown[...])

            def act(r, carry):
                rr = pl.ds(pl.multiple_of(r * sub_rows, sub_rows), sub_rows)
                v = u_all[u, rr, :]
                v2 = v * v
                th = jnp.tanh(GELU_K * (v + GELU_C * (v2 * v)))
                slope = 0.5 * (1.0 + th) + 0.5 * v * (1.0 - th * th) * (GELU_K * (1.0 + 3.0 * GELU_C * v2))
                dust[s, rr, :] = (part[0, s, rr, :] * slope).astype(BF16)
                return carry

            lax.fori_loop(0, tok // sub_rows, act, 0)
            save_du(u).start()
            part[0, s] = dot_nt(dust[s], wup[...])
            Scatter(0, u).start()

        def b_middle(j, u):
            sc = Scatter(0, u)

            @pl.when(inner)
            def _():
                for q in quarters:
                    m = m_all[u, q_rows(q), :]
                    inv = rms_inverse(m)
                    normed = m * inv
                    dn = sc.total(q)
                    gb8[...] += fold(dn * normed)
                    dn = dn * gain_b
                    dm = d_all[u, rows_of(near + q), :].astype(F32) + inv * (
                        dn - normed * jnp.mean(dn * normed, axis=-1, keepdims=True))
                    m_all[u, q_rows(q), :] = dm
                    dmbuf[gslot(u), rows_of(near + q), :] = dm.astype(BF16)
                    gather_dm(u).send(q)

            sc.drain()
            gather_d(u).drain()

            @pl.when(is_last)
            def _():
                gather_d(u).drain_own()

            save_du(u).wait()

        def b_relay_dm(j, u):
            gather_dm(u).relay()

        def b_collect_dm(j, u):
            gather_dm(u).collect()

        def b_attention(j, u):
            s = sslot(u)
            p = lax.rem(u, per_seq)
            save_d(u).wait()
            save_dm(u).start()

            @pl.when(is_first)
            def _():
                x_again(u).start()

            @pl.when(p == per_seq - 1)
            def _():
                dkacc[...] = jnp.zeros_like(dkacc)
                dvacc[...] = jnp.zeros_like(dvacc)

            datt[...] = dot_nt(dmbuf[gslot(u)], wout[...]).astype(BF16)
            p_rows = pl.ds(pl.multiple_of(p * tok, tok), tok)
            for h in range(n_head):
                cols = pl.ds(h * head_dim, head_dim)
                q, k, v, pr = softmax_of(u, p, h)
                da = datt[:, cols]
                dp = dot_nt(da, v)
                ds = (pr * (dp - jnp.sum(pr * dp, axis=-1, keepdims=True)) * scale).astype(BF16)
                dvacc[:, cols] += dot_tn(pr.astype(BF16), da)
                dkacc[:, cols] += dot_tn(ds, q)
                dqkvst[s, :, cols] = dot_nn(ds, k).astype(BF16)
            dqkvst[s, :, pl.ds(att_w, att_w)] = dkacc[p_rows, :].astype(BF16)
            dqkvst[s, :, pl.ds(2 * att_w, att_w)] = dvacc[p_rows, :].astype(BF16)
            save_dqkv(u).start()
            part[1, s] = dot_nt(dqkvst[s], wqkv[...])

            @pl.when(st > 0)
            def _():
                Scatter(1, u).start()

        def b_relay_h(j, u):
            @pl.when(st > 0)
            def _():
                Scatter(1, u).relay()

        def b_leave(j, u):
            s = lax.rem(j, n_hand)

            @pl.when(st > 0)
            def _():
                sc = Scatter(1, u)

                @pl.when(inner)
                def _():
                    @pl.when(j >= n_hand)
                    def _():
                        hand_sent(d_all, d_rs, u, j, st - 1, False)

                    for q in quarters:
                        h32 = hslot[u, q_rows(q), :].astype(F32)
                        inv = rms_inverse(h32)
                        normed = h32 * inv
                        dn = sc.total(q)
                        ga8[...] += fold(dn * normed)
                        dg = dn * gain_a
                        aout[s, q_rows(q), :] = (m_all[u, q_rows(q), :] + inv * (
                            dg - normed * jnp.mean(dg * normed, axis=-1, keepdims=True))).astype(BF16)
                        hand_quarter(d_all, d_rs, u, j, q, st - 1, begin)

                sc.drain()

            @pl.when(is_first)
            def _():
                x_again(u).wait()
                for k in range(nz):
                    rs = pl.ds(k * row, row)
                    h32 = xtmp[sslot(u), rs, :].astype(F32)
                    ga8[...] += fold(part[1, sslot(u), rs, :] * (h32 * rms_inverse(h32)))

            gather_dm(u).drain()
            gather_dm(u).drain_own()
            save_dm(u).wait()
            save_dqkv(u).wait()

        run_phases(BWD_ORDER, (
            b_enter, b_relay_d, b_collect_d, b_mlp, scatter_relay(0), b_middle, b_relay_dm, b_collect_dm, b_attention,
            b_relay_h, b_leave), True)

        @pl.when(st > 0)
        def _():
            hand_finish(d_all, d_rs, st - 1, False)
            gain_send().wait_send()

        @pl.when(is_last)
        def _():
            loss_send().wait_send()

        @pl.when(st < last_s)
        def _():
            loss_send().wait_recv()

            @pl.when(st > 0)
            def _():
                loss_send().start()
                loss_send().wait_send()

        loss_row = jnp.sum(jnp.sum(lossacc[...], axis=0, keepdims=True), axis=1, keepdims=True)
        gx[z, 0:1, :] = jnp.sum(ga8[...], axis=0, keepdims=True)
        gx[z, 1:2, :] = jnp.sum(gb8[...], axis=0, keepdims=True)
        gx[z, 2:8, :] = jnp.broadcast_to(loss_row, (6, d_model))

        def gx_send(dz):
            return rdma(gx.at[z], gx.at[z], gx_s.at[dz], gx_r.at[z], model=lax.rem(z + dz, nz))

        def gx_recv(dz):
            k = lax.rem(z + dz, nz)
            return rdma(gx.at[k], gx.at[k], gx_s.at[dz], gx_r.at[k], model=k)

        for dz in range(1, nz):
            gx_send(dz).start()
        for dz in range(1, nz):
            gx_recv(dz).wait_recv()
        red_out[...] = gx[0] + gx[1] + gx[2] + gx[3]
        for dz in range(1, nz):
            gx_send(dz).wait_send()

    any_spec = pl.BlockSpec(memory_space=pl.ANY)
    vmem_spec = pl.BlockSpec(memory_space=pltpu.VMEM)

    def out(width):
        return jax.ShapeDtypeStruct((n_unit, tok, width), BF16)

    dma = pltpu.SemaphoreType.DMA
    vmem = pltpu.VMEM
    return pl.pallas_call(
        kernel,
        out_shape=(out(d_model), out(d_model), out(d_model), out(d_model), out(qkv_w), out(att_w), out(ff_w), out(ff_w),
                   jax.ShapeDtypeStruct((8, d_model), F32)),
        in_specs=[any_spec] * 6 + [vmem_spec],
        out_specs=(any_spec,) * 8 + (vmem_spec,),
        scratch_shapes=[
            vmem((d_model, qkv_w), BF16), vmem((att_w, d_model), BF16), vmem((d_model, ff_w), BF16), vmem((ff_w, d_model), BF16),
            vmem((n_unit, half, d_model), BF16), vmem((n_hand, half, d_model), BF16),
            vmem((n_unit, tok, d_model), BF16), vmem((n_unit, tok, d_model), BF16),
            vmem((n_gath, tok, d_model), BF16), vmem((n_gath, tok, d_model), BF16), vmem((n_send, tok, d_model), BF16),
            vmem((n_unit, tok, qkv_w), BF16), vmem((n_unit, tok, ff_w), F32), vmem((n_unit, half, d_model), F32),
            vmem((n_send, tok, att_w), BF16), vmem((n_send, tok, ff_w), BF16), vmem((n_send, tok, ff_w), BF16),
            vmem((n_send, tok, qkv_w), BF16), vmem((tok, att_w), BF16), vmem((2, n_send, tok, d_model), F32),
            vmem((2, n_recv, nz, row, d_model), BF16), vmem((2, n_recv, 2, row, d_model), BF16),
            vmem((2, n_send, nz, row, d_model), BF16),
            vmem((n_hand, half, d_model), BF16), vmem((n_hand, half, d_model), BF16),
            vmem((seq_len, att_w), F32), vmem((seq_len, att_w), F32),
            vmem((2, d_model), F32), vmem((2, d_model), F32),
            vmem((8, d_model), F32), vmem((8, d_model), F32), vmem((8, d_model), F32), vmem((nz, 8, d_model), F32),
            dma((n_slab + 3,)), dma((n_unit,)), dma((n_hand,)), dma((n_send,)), dma((2,)), dma((n_hand, 7)), dma((8, n_gath)),
            dma((n_unit, nz)), dma((n_unit, nz)), dma((n_gath, 2)), dma((n_gath, nz)),
            dma((n_gath, nz)), dma((n_gath, nz)), dma((n_gath, 2)), dma((n_gath, nz)),
            dma((2, n_recv, nz)), dma((2, n_recv, 2)), dma((2, n_send, nz)),
            dma((2,)), dma((nz,)), dma((nz,)),
        ],
        compiler_params=pltpu.CompilerParams(collective_id=0, has_side_effects=True, vmem_limit_bytes=67_043_328),
        name="layer_step",
    )(x_in, y_target, w_qkv, w_out, w_up, w_down, gain)


def weight_grad(act, grad):
    return lax.dot_general(act, grad, (((0, 1), (0, 1)), ((), ())), preferred_element_type=F32)


def solution(mesh):
    dims = dict(mesh.shape)

    def device_fn(x_in, y_target, w_qkv, w_out, w_up, w_down, norm_gain):
        n_batch, seq_len, d_model = x_in.shape
        heads, head_dim = w_qkv.shape[3], w_qkv.shape[4]
        a, b, d, dm, dqkv, o, zz, du, red = layer_step(
            dims, x_in, y_target,
            w_qkv[0].transpose(1, 2, 0, 3).reshape(3 * heads, d_model, head_dim),
            w_out[0].reshape(heads * head_dim, d_model), w_up[0], w_down[0], norm_gain[0])
        grad_qkv = weight_grad(a, dqkv).reshape(1, d_model, 3, heads, head_dim)
        grad_out = weight_grad(o, dm).reshape(1, heads, head_dim, d_model)
        grad_up = weight_grad(b, du)[None]
        grad_down = weight_grad(zz, d)[None]
        loss = 0.5 * red[2, 0:1] / (n_batch * seq_len * d_model)
        return loss, grad_qkv, grad_out, grad_up, grad_down, red[None, 0:2]

    act_spec = P("data", None, None)
    weight_specs = (
        P("stage", None, None, "model", None),
        P("stage", "model", None, None),
        P("stage", None, "model"),
        P("stage", "model", None),
        P("stage", None, None),
    )
    grad_specs = (
        P(("data", "stage"), None, None, "model", None),
        P(("data", "stage"), "model", None, None),
        P(("data", "stage"), None, "model"),
        P(("data", "stage"), "model", None),
        P(("data", "stage"), None, None),
    )
    return jax.shard_map(
        device_fn,
        mesh=mesh,
        in_specs=(act_spec, act_spec) + weight_specs,
        out_specs=(P("data"),) + grad_specs,
        check_vma=False,
    )
```

time: 857 us -> 775 us (0.904)
  Pallas kernels: 803 us -> 721 us
    pallas_call x1, Pallas kernels: 803 us -> 721 us  [layer_step(): pl.pallas_call(kernel, out_shape=(out(d_model), out(d_model), out(d_model...]
where the time goes in v3:
time: 775 us; the launch traced here: 774 us
  Pallas kernels  721 us (93%)
  matrix products  40.2 us (5%)
  local copies, waits for them, and re-layouts  10.7 us (1%)
    pallas_call x1, Pallas kernels, layer_step(): pl.pallas_call(kernel, out_shape=(out(d_model), out(d_model), out(d_model...  721 us
    dot_general x4, matrix products, weight_grad(): lax.dot_general(act, grad, (((0, 1), (0, 1)), ((), ())), preferred_elemen...  40.2 us

profile of v3, /device:TPU:0, one launch (start us, length us, event | category | flops | bytes accessed | tf_op | source)
XLA Modules:
  0.0 774.4 jit_solution(5380685427907004530)
XLA Ops:
  0.6 721.0 %layer_step.1 = (bf16[12,128,1536]{2,1,0:T(8,128)(2,1)}, bf16[12,128,1536]{2,1,0:T(8,128)(2,1)}, bf16[12,128,1536]{2,1,0:T(8,128)(2,1)}, bf16[12,128,1536]{2,1,0...) custom-call(bf16[3,512,1536]{2,1,0:T(8,128)(2,1)} %x_ref.1, ...), custom_call_target="tpu_custom_call" | custom-call | tf_op jit(solution)/shard_map/layer_step/pallas_call | solution.py:714
  721.6 1.2 slice.6
  723.5 10.7 %fusion = f32[1536,1152,1]{0,1,2:T(8,128)} fusion(bf16[12,128,1536]{2,1,0:T(8,128)(2,1)} %get-tuple-element.16, bf16[12,128,1152]{2,1,0:T(8,128)(2,1)} %get-tuple-element.17), kind=kOutput, calls=%fused_computation.3 | convolution fusion | flops 5435817984 | bytes 15335424 | tf_op jit(solution)/shard_map/dot_general | solution.py:746
  734.1 0.0 copy-start
  734.1 8.1 %copy.17 = f32[1,1536,3,3,128]{4,1,3,2,0:T(8,128)} copy(f32[1,1536,3,3,128]{1,4,3,2,0:T(8,128)} %bitcast.32) | data formatting | bytes 14155776
  742.3 1.4 slice_bitcast_fusion
  743.7 0.0 copy-done
  743.7 0.0 slice-start
  743.7 0.0 slice-start.2
  743.7 5.9 fusion.1
  749.6 0.0 slice-start.1
  749.6 0.0 slice-start.3
  749.6 13.1 %convolution_bitcast_fusion.1 = f32[1,1536,1536]{2,1,0:T(8,128)} fusion(bf16[12,128,1536]{2,1,0:T(8,128)(2,1)} %get-tuple-element.20, bf16[12,128,1536]{2,1,0:T(8,128)(2,1)} %get-tuple-element.21), kind=kOutput, calls=%fused_computation.1 | convolution fusion | flops 7247757312 | bytes 18874368 | tf_op jit(solution)/shard_map/dot_general | solution.py:746
  762.7 0.0 slice-done
  762.8 0.0 slice-done.2
  762.8 0.0 slice-done.1
  762.8 0.0 slice-done.3
  762.8 10.5 %convolution_bitcast_fusion = f32[1,1536,1536]{2,1,0:T(8,128)} fusion(bf16[12,128,1536]{2,1,0:T(8,128)(2,1)S(1)} %bitcast.42, bf16[12,128,1536]{2,1,0:T(8,128)(2,1)S(1)} %bitcast.40), kind=kOutput, calls=%fused_computation | convolution fusion | flops 7247757312 | bytes 18874368 | tf_op jit(solution)/shard_map/dot_general | solution.py:746
  (2 shorter events, 0.0 us)
Async XLA Ops:
  734.1 9.5 %copy-start = (bf16[12,128,384]{2,1,0:T(8,128)(2,1)S(1)}, bf16[12,128,384]{2,1,0:T(8,128)(2,1)}, u32[]{:S(2)}) copy-start(bf16[12,128,384]{2,1,0:T(8,128)(2,1)} %get-tuple-element.18) | copy-start | bytes 3538948
  743.7 19.1 %slice-start = ((s8[4718592]{0:T(1024)(128)(4,1)}), s8[4194304]{0:T(1024)(128)(4,1)S(1)}, s32[]{:S(2)}) async-start(s8[4718592]{0:T(1024)(128)(4,1)} %bitcast.39), calls=%async_computation | async-start | bytes 8388608
  743.7 19.1 %slice-start.2 = ((s8[4718592]{0:T(1024)(128)(4,1)}), s8[4194304]{0:T(1024)(128)(4,1)S(1)}, s32[]{:S(2)}) async-start(s8[4718592]{0:T(1024)(128)(4,1)} %bitcast.41), calls=%async_computation.2 | async-start | bytes 8388608
  749.6 13.2 %slice-start.1 = ((s8[4718592]{0:T(1024)(128)(4,1)}), s8[524288]{0:T(1024)(128)(4,1)S(1)}, s32[]{:S(2)}) async-start(s8[4718592]{0:T(1024)(128)(4,1)} %bitcast.39), calls=%async_computation.1 | async-start | bytes 1048576
  749.6 13.2 %slice-start.3 = ((s8[4718592]{0:T(1024)(128)(4,1)}), s8[524288]{0:T(1024)(128)(4,1)S(1)}, s32[]{:S(2)}) async-start(s8[4718592]{0:T(1024)(128)(4,1)} %bitcast.41), calls=%async_computation.3 | async-start | bytes 1048576

commit v4 on v3

--- a/solution.py
+++ b/solution.py
@@ -30,8 +30,8 @@
     return lax.rsqrt(jnp.mean(v32 * v32, axis=-1, keepdims=True) + NORM_EPS)
 
 
-FWD_ORDER = (4, 10, 0, 1, 7, 8, 5, 2, 9, 6, 3)
-BWD_ORDER = (9, 3, 6, 4, 1, 10, 0, 5, 7, 8, 2)
+FWD_ORDER = (2, 6, 10, 0, 9, 5, 3, 7, 8, 1, 4)
+BWD_ORDER = (2, 1, 9, 5, 0, 3, 7, 4, 10, 6, 8)
 
 
 def lags(order):
@@ -50,7 +50,7 @@
     att_w = w_out.shape[0]
     ff_w = w_up.shape[1]
     n_head = att_w // head_dim
-    tok = 128
+    tok = 64
     row = tok // nz
     per_seq = seq_len // tok
     n_unit = n_seq * per_seq
@@ -59,7 +59,7 @@
     last_z, last_s = nz - 1, ns - 1
     sub_rows = 16
     half = tok // 2
-    n_send, n_recv, n_gath, n_hand = 1, 2, 3, 2
+    n_send, n_recv, n_gath, n_hand = 2, 3, 4, 2
     quarters = range(2)
 
     def kernel(x_ref, y_ref, wqkv_h, wout_h, wup_h, wdown_h, gain_ref,

time: 775 us -> 749 us (0.966)
  Pallas kernels: 721 us -> 695 us
    pallas_call x1, Pallas kernels: 721 us -> 695 us  [layer_step(): pl.pallas_call(kernel, out_shape=(out(d_model), out(d_model), out(d_model...]
where the time goes in v4:
time: 749 us; the launch traced here: 748 us
  Pallas kernels  695 us (93%)
  matrix products  39.8 us (5%)
  local copies, waits for them, and re-layouts  10.7 us (1%)
    pallas_call x1, Pallas kernels, layer_step(): pl.pallas_call(kernel, out_shape=(out(d_model), out(d_model), out(d_model...  695 us
    dot_general x4, matrix products, weight_grad(): lax.dot_general(act, grad, (((0, 1), (0, 1)), ((), ())), preferred_elemen...  39.8 us

profile of v4, /device:TPU:0, one launch (start us, length us, event | category | flops | bytes accessed | tf_op | source)
XLA Modules:
  0.0 748.2 jit_solution(17652279562391207402)
XLA Ops:
  0.6 695.2 %layer_step.1 = (bf16[24,64,1536]{2,1,0:T(8,128)(2,1)}, bf16[24,64,1536]{2,1,0:T(8,128)(2,1)}, bf16[24,64,1536]{2,1,0:T(8,128)(2,1)}, bf16[24,64,1536]{2,1,0:T(8...) custom-call(bf16[3,512,1536]{2,1,0:T(8,128)(2,1)} %x_ref.1, ...), custom_call_target="tpu_custom_call" | custom-call | tf_op jit(solution)/shard_map/layer_step/pallas_call | solution.py:714
  695.9 1.2 slice.6
  697.7 10.5 %fusion = f32[1536,1152,1]{0,1,2:T(8,128)} fusion(bf16[24,64,1536]{2,1,0:T(8,128)(2,1)} %get-tuple-element.16, bf16[24,64,1152]{2,1,0:T(8,128)(2,1)} %get-tuple-element.17), kind=kOutput, calls=%fused_computation.3 | convolution fusion | flops 5435817984 | bytes 15335424 | tf_op jit(solution)/shard_map/dot_general | solution.py:746
  708.2 0.0 copy-start
  708.2 8.1 %copy.13 = f32[1,1536,3,3,128]{4,1,3,2,0:T(8,128)} copy(f32[1,1536,3,3,128]{1,4,3,2,0:T(8,128)} %bitcast.32) | data formatting | bytes 14155776
  716.3 1.4 slice_bitcast_fusion
  717.7 0.0 copy-done
  717.7 0.0 slice-start
  717.7 0.0 slice-start.2
  717.7 5.9 fusion.1
  723.6 0.0 slice-start.1
  723.6 0.0 slice-start.3
  723.6 13.1 %convolution_bitcast_fusion.1 = f32[1,1536,1536]{2,1,0:T(8,128)} fusion(bf16[24,64,1536]{2,1,0:T(8,128)(2,1)} %get-tuple-element.20, bf16[24,64,1536]{2,1,0:T(8,128)(2,1)} %get-tuple-element.21), kind=kOutput, calls=%fused_computation.1 | convolution fusion | flops 7247757312 | bytes 18874368 | tf_op jit(solution)/shard_map/dot_general | solution.py:746
  736.8 0.0 slice-done
  736.8 0.0 slice-done.2
  736.8 0.0 slice-done.1
  736.8 0.0 slice-done.3
  736.8 10.3 %convolution_bitcast_fusion = f32[1,1536,1536]{2,1,0:T(8,128)} fusion(bf16[24,64,1536]{2,1,0:T(8,128)(2,1)S(1)} %bitcast.42, bf16[24,64,1536]{2,1,0:T(8,128)(2,1)S(1)} %bitcast.40), kind=kOutput, calls=%fused_computation | convolution fusion | flops 7247757312 | bytes 18874368 | tf_op jit(solution)/shard_map/dot_general | solution.py:746
  (2 shorter events, 0.0 us)
Async XLA Ops:
  708.2 9.5 %copy-start = (bf16[24,64,384]{2,1,0:T(8,128)(2,1)S(1)}, bf16[24,64,384]{2,1,0:T(8,128)(2,1)}, u32[]{:S(2)}) copy-start(bf16[24,64,384]{2,1,0:T(8,128)(2,1)} %get-tuple-element.18) | copy-start | bytes 3538948
  717.7 19.1 %slice-start = ((s8[4718592]{0:T(1024)(128)(4,1)}), s8[4194304]{0:T(1024)(128)(4,1)S(1)}, s32[]{:S(2)}) async-start(s8[4718592]{0:T(1024)(128)(4,1)} %bitcast.39), calls=%async_computation | async-start | bytes 8388608
  717.7 19.1 %slice-start.2 = ((s8[4718592]{0:T(1024)(128)(4,1)}), s8[4194304]{0:T(1024)(128)(4,1)S(1)}, s32[]{:S(2)}) async-start(s8[4718592]{0:T(1024)(128)(4,1)} %bitcast.41), calls=%async_computation.2 | async-start | bytes 8388608
  723.6 13.2 %slice-start.1 = ((s8[4718592]{0:T(1024)(128)(4,1)}), s8[524288]{0:T(1024)(128)(4,1)S(1)}, s32[]{:S(2)}) async-start(s8[4718592]{0:T(1024)(128)(4,1)} %bitcast.39), calls=%async_computation.1 | async-start | bytes 1048576
  723.6 13.2 %slice-start.3 = ((s8[4718592]{0:T(1024)(128)(4,1)}), s8[524288]{0:T(1024)(128)(4,1)S(1)}, s32[]{:S(2)}) async-start(s8[4718592]{0:T(1024)(128)(4,1)} %bitcast.41), calls=%async_computation.3 | async-start | bytes 1048576

commit v5 on v4

--- a/solution.py
+++ b/solution.py
@@ -742,8 +742,78 @@
     )(x_in, y_target, w_qkv, w_out, w_up, w_down, gain)
 
 
-def weight_grad(act, grad):
-    return lax.dot_general(act, grad, (((0, 1), (0, 1)), ((), ())), preferred_element_type=F32)
+def weight_grads(o, dm, a, dqkv, b, du, zz, d, head_dim):
+    n_tok = o.shape[0] * o.shape[1]
+    rows = 256
+
+    def flat(v):
+        return v.reshape(n_tok, v.shape[2])
+
+    acts = [flat(v) for v in (o, dm, a, dqkv, b, du, zz, d)]
+    att_w, d_model = acts[0].shape[1], acts[1].shape[1]
+    qkv_w, ff_w = acts[3].shape[1], acts[5].shape[1]
+    n_slab = qkv_w // head_dim
+
+    def kernel(*refs):
+        src, outs, held, tiles = refs[:8], refs[8:12], refs[12:20], refs[20:24]
+        in_sem, out_sem = refs[24:]
+        loads = [pltpu.make_async_copy(src[i], held[i], in_sem.at[i]) for i in range(8)]
+        for cp in loads:
+            cp.start()
+
+        def stores(pair, i, slot):
+            n = tiles[pair].shape[1]
+            at = pl.ds(pl.multiple_of(i * n, n), n)
+            sem = out_sem.at[pair, slot]
+            if pair == 1:
+                return [pltpu.make_async_copy(tiles[1].at[slot, :, pl.ds(k * head_dim, head_dim)], outs[1].at[k, at, :], sem)
+                        for k in range(n_slab)]
+            return [pltpu.make_async_copy(tiles[pair].at[slot], outs[pair].at[at, :], sem)]
+
+        def finish(cps):
+            for cp in cps:
+                cp.wait()
+
+        counts = []
+        for pair in range(4):
+            loads[2 * pair].wait()
+            loads[2 * pair + 1].wait()
+            left, right, tile = held[2 * pair], held[2 * pair + 1], tiles[pair]
+            n = tile.shape[1]
+            count = left.shape[1] // n
+            counts.append(count)
+
+            def body(i, carry):
+                slot = lax.rem(i, 2)
+
+                @pl.when(i >= 2)
+                def _():
+                    finish(stores(pair, i - 2, slot))
+
+                tile[slot] = dot_tn(left[:, pl.ds(pl.multiple_of(i * n, n), n)], right[...])
+                for cp in stores(pair, i, slot):
+                    cp.start()
+                return carry
+
+            lax.fori_loop(0, count, body, 0)
+        for pair in range(4):
+            for i in range(max(0, counts[pair] - 2), counts[pair]):
+                finish(stores(pair, i, i % 2))
+
+    any_spec = pl.BlockSpec(memory_space=pl.ANY)
+    return pl.pallas_call(
+        kernel,
+        out_shape=(jax.ShapeDtypeStruct((att_w, d_model), F32), jax.ShapeDtypeStruct((n_slab, d_model, head_dim), F32),
+                   jax.ShapeDtypeStruct((d_model, ff_w), F32), jax.ShapeDtypeStruct((ff_w, d_model), F32)),
+        in_specs=[any_spec] * 8,
+        out_specs=(any_spec,) * 4,
+        scratch_shapes=[pltpu.VMEM(v.shape, BF16) for v in acts] + [
+            pltpu.VMEM((1, att_w, d_model), F32), pltpu.VMEM((2, rows, qkv_w), F32),
+            pltpu.VMEM((2, rows, ff_w), F32), pltpu.VMEM((2, rows, d_model), F32),
+            pltpu.SemaphoreType.DMA((8,)), pltpu.SemaphoreType.DMA((4, 2))],
+        compiler_params=pltpu.CompilerParams(vmem_limit_bytes=67_043_328),
+        name="weight_grads",
+    )(*acts)
 
 
 def solution(mesh):
@@ -756,10 +826,11 @@
             dims, x_in, y_target,
             w_qkv[0].transpose(1, 2, 0, 3).reshape(3 * heads, d_model, head_dim),
             w_out[0].reshape(heads * head_dim, d_model), w_up[0], w_down[0], norm_gain[0])
-        grad_qkv = weight_grad(a, dqkv).reshape(1, d_model, 3, heads, head_dim)
-        grad_out = weight_grad(o, dm).reshape(1, heads, head_dim, d_model)
-        grad_up = weight_grad(b, du)[None]
-        grad_down = weight_grad(zz, d)[None]
+        g_out, g_qkv, g_up, g_down = weight_grads(o, dm, a, dqkv, b, du, zz, d, head_dim)
+        grad_qkv = g_qkv.reshape(3, heads, d_model, head_dim).transpose(2, 0, 1, 3)[None]
+        grad_out = g_out.reshape(1, heads, head_dim, d_model)
+        grad_up = g_up[None]
+        grad_down = g_down[None]
         loss = 0.5 * red[2, 0:1] / (n_batch * seq_len * d_model)
         return loss, grad_qkv, grad_out, grad_up, grad_down, red[None, 0:2]
 

time: 749 us -> 731 us (0.976)
  matrix products: 39.8 us -> 0 us
  Pallas kernels: 695 us -> 726 us
  local copies, waits for them, and re-layouts: 10.7 us -> 2.6 us
    dot_general x4 -> x0, matrix products: 39.8 us -> none  [weight_grad(): lax.dot_general(act, grad, (((0, 1), (0, 1)), ((), ())), preferred_elemen...]
    pallas_call x0 -> x1, Pallas kernels: none -> 30.8 us  [weight_grads(): pl.pallas_call(kernel, out_shape=(jax.ShapeDtypeStruct((att_w, d_model),...]
    unnamed x11 -> x0, local copies, waits for them, and re-layouts: 8.15 us -> none
where the time goes in v5:
time: 731 us
  Pallas kernels  726 us (99%)
    pallas_call x1, Pallas kernels, layer_step(): pl.pallas_call(kernel, out_shape=(out(d_model), out(d_model), out(d_model...  695 us
    pallas_call x1, Pallas kernels, weight_grads(): pl.pallas_call(kernel, out_shape=(jax.ShapeDtypeStruct((att_w, d_model),...  30.8 us

profile of v5, /device:TPU:0, one launch (start us, length us, event | category | flops | bytes accessed | tf_op | source)
XLA Modules:
  0.0 731.0 jit_solution(12410599654207557321)
XLA Ops:
  0.6 695.2 %layer_step.1 = (bf16[24,64,1536]{2,1,0:T(8,128)(2,1)}, bf16[24,64,1536]{2,1,0:T(8,128)(2,1)}, bf16[24,64,1536]{2,1,0:T(8,128)(2,1)}, bf16[24,64,1536]{2,1,0:T(8...) custom-call(bf16[3,512,1536]{2,1,0:T(8,128)(2,1)} %x_ref.1, ...), custom_call_target="tpu_custom_call" | custom-call | tf_op jit(solution)/shard_map/layer_step/pallas_call | solution.py:714
  695.8 30.8 %weight_grads.1 = (f32[384,1536]{1,0:T(8,128)}, f32[9,1536,128]{2,1,0:T(8,128)}, f32[1536,1536]{1,0:T(8,128)}, f32[1536,1536]{1,0:T(8,128)}) custom-call(bf16[1536,384]{1,0:T(8,128)(2,1)} %bitcast.39, bf16[1536,1536]{1,0:T(8,128)(2,1)} %bitcast.33, bf16[1536,1536]{1,0:T(8,128)(2,1)} %bitcast.30, bf16[1536,1152]{1,0:T(8,128)(2,1)} %bitcast.37, ...), custom_call_target="tpu_custom_call" | custom-call | tf_op jit(solution)/shard_map/weight_grads/pallas_call | solution.py:804
  726.6 1.4 slice_bitcast_fusion
  728.0 1.2 slice.6

commit v6 on v5

--- a/solution.py
+++ b/solution.py
@@ -30,14 +30,17 @@
     return lax.rsqrt(jnp.mean(v32 * v32, axis=-1, keepdims=True) + NORM_EPS)
 
 
-FWD_ORDER = (2, 6, 10, 0, 9, 5, 3, 7, 8, 1, 4)
-BWD_ORDER = (2, 1, 9, 5, 0, 3, 7, 4, 10, 6, 8)
-
-
-def lags(order):
-    place = {phase: i for i, phase in enumerate(order)}
+ORDER = (
+    (0, 3), (0, 7), (1, 2), (1, 9), (1, 3), (1, 1), (1, 5), (0, 8), (0, 4), (0, 0), (0, 1), (0, 6), (1, 10), (1,
+    7), (0, 10), (1, 4), (1, 0), (1, 8), (1, 6), (0, 2), (0, 9), (0, 5),
+)
+BACK_START, BACK_STEP = 11, 13
+
+
+def lags(back):
+    place = {phase: i for i, (is_back, phase) in enumerate(ORDER) if is_back == int(back)}
     lag = [0]
-    for phase in range(1, len(order)):
+    for phase in range(1, len(place)):
         lag.append(lag[-1] + (1 if place[phase] < place[phase - 1] else 0))
     return lag
 
@@ -51,7 +54,9 @@
     ff_w = w_up.shape[1]
     n_head = att_w // head_dim
     tok = 64
-    row = tok // nz
+    n_part = 1
+    row = tok // (2 * n_part)
+    n_block = 2 * n_part
     per_seq = seq_len // tok
     n_unit = n_seq * per_seq
     scale = head_dim ** -0.5
@@ -60,16 +65,16 @@
     sub_rows = 16
     half = tok // 2
     n_send, n_recv, n_gath, n_hand = 2, 3, 4, 2
-    quarters = range(2)
+    quarters = range(n_part)
 
     def kernel(x_ref, y_ref, wqkv_h, wout_h, wup_h, wdown_h, gain_ref,
                a_out, b_out, d_out, dm_out, dqkv_out, o_out, z_out, du_out, red_out,
                wqkv, wout, wup, wdown, hslot, yslot, a_all, d_all, bbuf, dmbuf, xtmp,
                qkv_all, u_all, m_all, ost, zst, dust, dqkvst, datt, part,
-               recv_o, recv_i, send_p, hout, aout, dkacc, dvacc,
+               recv_o, recv_i, send_p, hout, aout, dout, dkacc, dvacc,
                gains, gain_next, lossacc, ga8, gb8, gx,
-               w_sem, hsem, ysem, x_sem, gain_sem, hand_sem, save_sem,
-               a_rs, d_rs, g1_si, g1_so, b_rs, dm_rs, g2_si, g2_so,
+               w_sem, hsem, ysem, x_sem, gain_sem, hand_sem, back_sem, save_sem,
+               a_rs, d_rs, a_si, a_so, d_si, d_so, b_rs, dm_rs, b_si, b_so, dm_si, dm_so,
                rs_ro, rs_ri, rs_s, loss_sem, gx_s, gx_r):
         z = lax.axis_index("model")
         st = lax.axis_index("stage")
@@ -78,8 +83,8 @@
         inner = (z > 0) & (z < last_z)
         outer = (z == 0) | (z == last_z)
         side = lax.div(z, 2)
-        near = 2 * side
-        far = 2 - near
+        near = n_part * side
+        far = n_part - near
         inner_peer = 1 + lax.rem(z, 2)
         outer_peer = last_z * side
         my_half = pl.ds(pl.multiple_of(side * half, half), half)
@@ -103,9 +108,9 @@
             q, first = tokens_of(u)
             return pltpu.make_async_copy(x_ref.at[q, pl.ds(first, tok), :], a_all.at[u], hsem.at[u])
 
-        def x_again(u):
+        def x_again(j, u):
             q, first = tokens_of(u)
-            slot = lax.rem(u, n_send)
+            slot = lax.rem(j, n_send)
             return pltpu.make_async_copy(x_ref.at[q, pl.ds(first, tok), :], xtmp.at[slot], x_sem.at[slot])
 
         def y_copy(u):
@@ -171,7 +176,7 @@
             def collect(self):
                 @pl.when(outer)
                 def _():
-                    for k in range(nz):
+                    for k in range(n_block):
                         self.outward(k).wait_recv()
 
             def own(self):
@@ -194,16 +199,16 @@
                         self.outward(near + q).wait_send()
 
         def gather_a(u):
-            return Gather(a_all, u, a_rs, g1_si, g1_so, lax.rem(u, n_gath))
-
-        def gather_d(u):
-            return Gather(d_all, u, d_rs, g1_si, g1_so, lax.rem(u, n_gath))
+            return Gather(a_all, u, a_rs, a_si, a_so, lax.rem(u, n_gath))
+
+        def gather_d(j, u):
+            return Gather(d_all, u, d_rs, d_si, d_so, lax.rem(j, n_gath))
 
         def gather_b(u):
-            return Gather(bbuf, lax.rem(u, n_gath), b_rs, g2_si, g2_so, lax.rem(u, n_gath))
-
-        def gather_dm(u):
-            return Gather(dmbuf, lax.rem(u, n_gath), dm_rs, g2_si, g2_so, lax.rem(u, n_gath))
+            return Gather(bbuf, lax.rem(u, n_gath), b_rs, b_si, b_so, lax.rem(u, n_gath))
+
+        def gather_dm(j):
+            return Gather(dmbuf, lax.rem(j, n_gath), dm_rs, dm_si, dm_so, lax.rem(j, n_gath))
 
         class Scatter:
             def __init__(self, op, u):
@@ -223,7 +228,7 @@
             def start(self):
                 @pl.when(outer)
                 def _():
-                    for k in (far, far + 1, near, near + 1):
+                    for k in [far + q for q in quarters] + [near + q for q in quarters]:
                         send_p[self.op, self.ss, k] = self.mine(k).astype(BF16)
                         self.in_copy(k).start()
 
@@ -246,7 +251,7 @@
             def drain(self):
                 @pl.when(outer)
                 def _():
-                    for k in range(nz):
+                    for k in range(n_block):
                         self.in_copy(k).wait_send()
 
                 @pl.when(inner)
@@ -254,8 +259,8 @@
                     for q in quarters:
                         self.cross_copy(far + q, q).wait_send()
 
-        def save(kind, src, src_slot, dst, u):
-            return pltpu.make_async_copy(src.at[src_slot], dst.at[u], save_sem.at[kind, lax.rem(u, n_gath)])
+        def save(kind, src, src_slot, dst, j, u):
+            return pltpu.make_async_copy(src.at[src_slot], dst.at[u], save_sem.at[kind, lax.rem(j, n_gath)])
 
         def sslot(u):
             return lax.rem(u, n_send)
@@ -267,47 +272,48 @@
             return pl.ds(q * row, row)
 
         def save_a(u):
-            return save(0, a_all, u, a_out, u)
+            return save(0, a_all, u, a_out, u, u)
 
         def save_o(u):
-            return save(1, ost, sslot(u), o_out, u)
+            return save(1, ost, sslot(u), o_out, u, u)
 
         def save_b(u):
-            return save(2, bbuf, gslot(u), b_out, u)
+            return save(2, bbuf, gslot(u), b_out, u, u)
 
         def save_z(u):
-            return save(3, zst, sslot(u), z_out, u)
-
-        def save_d(u):
-            return save(4, d_all, u, d_out, u)
-
-        def save_du(u):
-            return save(5, dust, sslot(u), du_out, u)
-
-        def save_dm(u):
-            return save(6, dmbuf, gslot(u), dm_out, u)
-
-        def save_dqkv(u):
-            return save(7, dqkvst, sslot(u), dqkv_out, u)
+            return save(3, zst, sslot(u), z_out, u, u)
+
+        def save_d(j, u):
+            return save(4, d_all, u, d_out, j, u)
+
+        def save_du(j, u):
+            return save(5, dust, sslot(j), du_out, j, u)
+
+        def save_dm(j, u):
+            return save(6, dmbuf, gslot(j), dm_out, j, u)
+
+        def save_dqkv(j, u):
+            return save(7, dqkvst, sslot(j), dqkv_out, j, u)
 
         gain_a = gains[0:1, :]
         gain_b = gains[1:2, :]
 
         def hand_h(u, j):
             s = lax.rem(j, n_hand)
-            return rdma(hout.at[s], hslot.at[u], hand_sem.at[s, 6], hsem.at[u], stage=st + 1)
-
-        def hand_quarter(buf, sems, u, j, q, next_stage, act):
+            return rdma(hout.at[s], hslot.at[u], hand_sem.at[s, 3 * n_part], hsem.at[u], stage=st + 1)
+
+        def hand_quarter(back, u, j, q, act):
             s = lax.rem(j, n_hand)
             k = near + q
+            src, buf, sems, own = (dout, d_all, d_rs, back_sem) if back else (aout, a_all, a_rs, hand_sem)
             for i, peer in enumerate((inner_peer, outer_peer, z)):
-                act(rdma(aout.at[s, q_rows(q), :], buf.at[u, rows_of(k), :], hand_sem.at[s, 3 * q + i], sems.at[u, k],
-                         model=peer, stage=next_stage))
-
-        def hand_sent(buf, sems, u, j, next_stage, with_h):
+                act(rdma(src.at[s, q_rows(q), :], buf.at[u, rows_of(k), :], own.at[s, 3 * q + i], sems.at[u, k],
+                         model=peer, stage=(st - 1) if back else (st + 1)))
+
+        def hand_sent(back, u, j):
             for q in quarters:
-                hand_quarter(buf, sems, u, j, q, next_stage, sent)
-            if with_h:
+                hand_quarter(back, u, j, q, sent)
+            if not back:
                 hand_h(u, j).wait_send()
 
         def begin(cp):
@@ -338,7 +344,7 @@
             def _():
                 x_copy(u).wait()
                 hslot[u] = a_all[u, my_half, :]
-                for k in range(nz):
+                for k in range(n_block):
                     rs = pl.ds(k * row, row)
                     h32 = a_all[u, rs, :].astype(F32)
                     a_all[u, rs, :] = (h32 * rms_inverse(h32) * gain_a).astype(BF16)
@@ -374,7 +380,7 @@
 
         def scatter_relay(op):
             def run(j, u):
-                Scatter(op, u).relay()
+                Scatter(op, j).relay()
             return run
 
         def f_middle(j, u):
@@ -384,7 +390,7 @@
             def _():
                 @pl.when(st > 0)
                 def _():
-                    rdma(hout.at[0], hslot.at[u], hand_sem.at[0, 6], hsem.at[u], stage=st).wait_recv()
+                    rdma(hout.at[0], hslot.at[u], hand_sem.at[0, 3 * n_part], hsem.at[u], stage=st).wait_recv()
 
                 for q in quarters:
                     m = hslot[u, q_rows(q), :].astype(F32) + sc.total(q)
@@ -447,7 +453,7 @@
                 def _():
                     @pl.when(j >= n_hand)
                     def _():
-                        hand_sent(a_all, a_rs, u, j, st + 1, True)
+                        hand_sent(False, u, j)
 
                 @pl.when(is_last)
                 def _():
@@ -460,7 +466,7 @@
                     @pl.when(st < last_s)
                     def _():
                         aout[s, q_rows(q), :] = (h32 * rms_inverse(h32) * gain_next[0:1, :]).astype(BF16)
-                        hand_quarter(a_all, a_rs, u, j, q, st + 1, begin)
+                        hand_quarter(False, u, j, q, begin)
                         hout[s, q_rows(q), :] = h_new
 
                     @pl.when(is_last)
@@ -479,61 +485,29 @@
             save_b(u).wait()
             save_z(u).wait()
 
-        def run_phases(order, phases, back):
-            lag = lags(order)
-
-            def body(i, carry):
-                for phase in order:
-                    j = i - lag[phase]
-
-                    @pl.when((j >= 0) & (j < n_unit))
-                    def _():
-                        phases[phase](j, (n_unit - 1 - j) if back else j)
-                return carry
-
-            lax.fori_loop(0, n_unit + lag[-1], body, 0)
-
-        def hand_finish(buf, sems, next_stage, with_h):
-            @pl.when(inner)
-            def _():
-                for j in range(n_unit - n_hand, n_unit):
-                    hand_sent(buf, sems, j, j, next_stage, with_h)
-
-        run_phases(FWD_ORDER, (
-            f_enter, f_relay_a, f_collect_a, f_attention, scatter_relay(0), f_middle, f_relay_b, f_collect_b, f_mlp,
-            scatter_relay(1), f_leave), False)
-
-        def loss_send():
-            return rdma(lossacc, lossacc, loss_sem.at[0], loss_sem.at[1], stage=st - 1)
-
-        @pl.when(is_last)
-        def _():
-            loss_send().start()
-
-        @pl.when(st < last_s)
-        def _():
-            hand_finish(a_all, a_rs, st + 1, True)
+        forward = (f_enter, f_relay_a, f_collect_a, f_attention, scatter_relay(0), f_middle, f_relay_b, f_collect_b, f_mlp,
+                   scatter_relay(1), f_leave)
 
         def b_enter(j, u):
             @pl.when(is_last & inner)
             def _():
                 for q in quarters:
-                    gather_d(u).send(q)
+                    gather_d(j, u).send(q)
 
         def b_relay_d(j, u):
-            gather_d(u).relay()
+            gather_d(j, u).relay()
 
         def b_collect_d(j, u):
-            gather_d(u).collect()
+            gather_d(j, u).collect()
 
             @pl.when(st < last_s)
             def _():
-                gather_d(u).own()
+                gather_d(j, u).own()
 
         def b_mlp(j, u):
-            s = sslot(u)
-            save_d(u).start()
-            part[0, s] = dot_nt(d_all[u], wdown[...])
+            s = sslot(j)
+            save_d(j, u).start()
+            part[2, s] = dot_nt(d_all[u], wdown[...])
 
             def act(r, carry):
                 rr = pl.ds(pl.multiple_of(r * sub_rows, sub_rows), sub_rows)
@@ -541,16 +515,16 @@
                 v2 = v * v
                 th = jnp.tanh(GELU_K * (v + GELU_C * (v2 * v)))
                 slope = 0.5 * (1.0 + th) + 0.5 * v * (1.0 - th * th) * (GELU_K * (1.0 + 3.0 * GELU_C * v2))
-                dust[s, rr, :] = (part[0, s, rr, :] * slope).astype(BF16)
+                dust[s, rr, :] = (part[2, s, rr, :] * slope).astype(BF16)
                 return carry
 
             lax.fori_loop(0, tok // sub_rows, act, 0)
-            save_du(u).start()
-            part[0, s] = dot_nt(dust[s], wup[...])
-            Scatter(0, u).start()
+            save_du(j, u).start()
+            part[2, s] = dot_nt(dust[s], wup[...])
+            Scatter(2, j).start()
 
         def b_middle(j, u):
-            sc = Scatter(0, u)
+            sc = Scatter(2, j)
 
             @pl.when(inner)
             def _():
@@ -564,40 +538,40 @@
                     dm = d_all[u, rows_of(near + q), :].astype(F32) + inv * (
                         dn - normed * jnp.mean(dn * normed, axis=-1, keepdims=True))
                     m_all[u, q_rows(q), :] = dm
-                    dmbuf[gslot(u), rows_of(near + q), :] = dm.astype(BF16)
-                    gather_dm(u).send(q)
+                    dmbuf[gslot(j), rows_of(near + q), :] = dm.astype(BF16)
+                    gather_dm(j).send(q)
 
             sc.drain()
-            gather_d(u).drain()
+            gather_d(j, u).drain()
 
             @pl.when(is_last)
             def _():
-                gather_d(u).drain_own()
-
-            save_du(u).wait()
+                gather_d(j, u).drain_own()
+
+            save_du(j, u).wait()
 
         def b_relay_dm(j, u):
-            gather_dm(u).relay()
+            gather_dm(j).relay()
 
         def b_collect_dm(j, u):
-            gather_dm(u).collect()
+            gather_dm(j).collect()
 
         def b_attention(j, u):
-            s = sslot(u)
+            s = sslot(j)
             p = lax.rem(u, per_seq)
-            save_d(u).wait()
-            save_dm(u).start()
+            save_d(j, u).wait()
+            save_dm(j, u).start()
 
             @pl.when(is_first)
             def _():
-                x_again(u).start()
+                x_again(j, u).start()
 
             @pl.when(p == per_seq - 1)
             def _():
                 dkacc[...] = jnp.zeros_like(dkacc)
                 dvacc[...] = jnp.zeros_like(dvacc)
 
-            datt[...] = dot_nt(dmbuf[gslot(u)], wout[...]).astype(BF16)
+            datt[...] = dot_nt(dmbuf[gslot(j)], wout[...]).astype(BF16)
             p_rows = pl.ds(pl.multiple_of(p * tok, tok), tok)
             for h in range(n_head):
                 cols = pl.ds(h * head_dim, head_dim)
@@ -610,30 +584,30 @@
                 dqkvst[s, :, cols] = dot_nn(ds, k).astype(BF16)
             dqkvst[s, :, pl.ds(att_w, att_w)] = dkacc[p_rows, :].astype(BF16)
             dqkvst[s, :, pl.ds(2 * att_w, att_w)] = dvacc[p_rows, :].astype(BF16)
-            save_dqkv(u).start()
-            part[1, s] = dot_nt(dqkvst[s], wqkv[...])
+            save_dqkv(j, u).start()
+            part[3, s] = dot_nt(dqkvst[s], wqkv[...])
 
             @pl.when(st > 0)
             def _():
-                Scatter(1, u).start()
+                Scatter(3, j).start()
 
         def b_relay_h(j, u):
             @pl.when(st > 0)
             def _():
-                Scatter(1, u).relay()
+                Scatter(3, j).relay()
 
         def b_leave(j, u):
             s = lax.rem(j, n_hand)
 
             @pl.when(st > 0)
             def _():
-                sc = Scatter(1, u)
+                sc = Scatter(3, j)
 
                 @pl.when(inner)
                 def _():
                     @pl.when(j >= n_hand)
                     def _():
-                        hand_sent(d_all, d_rs, u, j, st - 1, False)
+                        hand_sent(True, u, j)
 
                     for q in quarters:
                         h32 = hslot[u, q_rows(q), :].astype(F32)
@@ -642,32 +616,65 @@
                         dn = sc.total(q)
                         ga8[...] += fold(dn * normed)
                         dg = dn * gain_a
-                        aout[s, q_rows(q), :] = (m_all[u, q_rows(q), :] + inv * (
+                        dout[s, q_rows(q), :] = (m_all[u, q_rows(q), :] + inv * (
                             dg - normed * jnp.mean(dg * normed, axis=-1, keepdims=True))).astype(BF16)
-                        hand_quarter(d_all, d_rs, u, j, q, st - 1, begin)
+                        hand_quarter(True, u, j, q, begin)
 
                 sc.drain()
 
             @pl.when(is_first)
             def _():
-                x_again(u).wait()
-                for k in range(nz):
+                x_again(j, u).wait()
+                for k in range(n_block):
                     rs = pl.ds(k * row, row)
-                    h32 = xtmp[sslot(u), rs, :].astype(F32)
-                    ga8[...] += fold(part[1, sslot(u), rs, :] * (h32 * rms_inverse(h32)))
-
-            gather_dm(u).drain()
-            gather_dm(u).drain_own()
-            save_dm(u).wait()
-            save_dqkv(u).wait()
-
-        run_phases(BWD_ORDER, (
-            b_enter, b_relay_d, b_collect_d, b_mlp, scatter_relay(0), b_middle, b_relay_dm, b_collect_dm, b_attention,
-            b_relay_h, b_leave), True)
+                    h32 = xtmp[sslot(j), rs, :].astype(F32)
+                    ga8[...] += fold(part[3, sslot(j), rs, :] * (h32 * rms_inverse(h32)))
+
+            gather_dm(j).drain()
+            gather_dm(j).drain_own()
+            save_dm(j, u).wait()
+            save_dqkv(j, u).wait()
+
+        backward = (b_enter, b_relay_d, b_collect_d, b_mlp, scatter_relay(2), b_middle, b_relay_dm, b_collect_dm,
+                    b_attention, b_relay_h, b_leave)
+        f_lag, b_lag = lags(False), lags(True)
+        back_from = BACK_START + BACK_STEP * (last_s - st)
+
+        def turn(i, carry):
+            for back, phase in ORDER:
+                j = (i - back_from - b_lag[phase]) if back else (i - f_lag[phase])
+
+                @pl.when((j >= 0) & (j < n_unit))
+                def _():
+                    if back:
+                        seq = lax.div(j, per_seq)
+                        backward[phase](j, 2 * seq * per_seq + (per_seq - 1) - j)
+                    else:
+                        forward[phase](j, j)
+            return carry
+
+        lax.fori_loop(0, n_unit + back_from + b_lag[-1], turn, 0)
+
+        def loss_send():
+            return rdma(lossacc, lossacc, loss_sem.at[0], loss_sem.at[1], stage=st - 1)
+
+        def hand_finish(back):
+            @pl.when(inner)
+            def _():
+                for j in range(n_unit - n_hand, n_unit):
+                    hand_sent(back, j, j)
+
+        @pl.when(is_last)
+        def _():
+            loss_send().start()
+
+        @pl.when(st < last_s)
+        def _():
+            hand_finish(False)
 
         @pl.when(st > 0)
         def _():
-            hand_finish(d_all, d_rs, st - 1, False)
+            hand_finish(True)
             gain_send().wait_send()
 
         @pl.when(is_last)
@@ -724,17 +731,18 @@
             vmem((n_gath, tok, d_model), BF16), vmem((n_gath, tok, d_model), BF16), vmem((n_send, tok, d_model), BF16),
             vmem((n_unit, tok, qkv_w), BF16), vmem((n_unit, tok, ff_w), F32), vmem((n_unit, half, d_model), F32),
             vmem((n_send, tok, att_w), BF16), vmem((n_send, tok, ff_w), BF16), vmem((n_send, tok, ff_w), BF16),
-            vmem((n_send, tok, qkv_w), BF16), vmem((tok, att_w), BF16), vmem((2, n_send, tok, d_model), F32),
-            vmem((2, n_recv, nz, row, d_model), BF16), vmem((2, n_recv, 2, row, d_model), BF16),
-            vmem((2, n_send, nz, row, d_model), BF16),
-            vmem((n_hand, half, d_model), BF16), vmem((n_hand, half, d_model), BF16),
+            vmem((n_send, tok, qkv_w), BF16), vmem((tok, att_w), BF16), vmem((4, n_send, tok, d_model), F32),
+            vmem((4, n_recv, n_block, row, d_model), BF16), vmem((4, n_recv, n_part, row, d_model), BF16),
+            vmem((4, n_send, n_block, row, d_model), BF16),
+            vmem((n_hand, half, d_model), BF16), vmem((n_hand, half, d_model), BF16), vmem((n_hand, half, d_model), BF16),
             vmem((seq_len, att_w), F32), vmem((seq_len, att_w), F32),
             vmem((2, d_model), F32), vmem((2, d_model), F32),
             vmem((8, d_model), F32), vmem((8, d_model), F32), vmem((8, d_model), F32), vmem((nz, 8, d_model), F32),
-            dma((n_slab + 3,)), dma((n_unit,)), dma((n_hand,)), dma((n_send,)), dma((2,)), dma((n_hand, 7)), dma((8, n_gath)),
-            dma((n_unit, nz)), dma((n_unit, nz)), dma((n_gath, 2)), dma((n_gath, nz)),
-            dma((n_gath, nz)), dma((n_gath, nz)), dma((n_gath, 2)), dma((n_gath, nz)),
-            dma((2, n_recv, nz)), dma((2, n_recv, 2)), dma((2, n_send, nz)),
+            dma((n_slab + 3,)), dma((n_unit,)), dma((n_hand,)), dma((n_send,)), dma((2,)), dma((n_hand, 3 * n_part + 1)), dma((n_hand, 3 * n_part)), dma((8, n_gath)),
+            dma((n_unit, n_block)), dma((n_unit, n_block)), dma((n_gath, n_part)), dma((n_gath, n_block)),
+            dma((n_gath, n_part)), dma((n_gath, n_block)), dma((n_gath, n_block)), dma((n_gath, n_block)),
+            dma((n_gath, n_part)), dma((n_gath, n_block)), dma((n_gath, n_part)), dma((n_gath, n_block)),
+            dma((4, n_recv, n_block)), dma((4, n_recv, n_part)), dma((4, n_send, n_block)),
             dma((2,)), dma((nz,)), dma((nz,)),
         ],
         compiler_params=pltpu.CompilerParams(collective_id=0, has_side_effects=True, vmem_limit_bytes=67_043_328),
@@ -742,7 +750,7 @@
     )(x_in, y_target, w_qkv, w_out, w_up, w_down, gain)
 
 
-def weight_grads(o, dm, a, dqkv, b, du, zz, d, head_dim):
+def weight_grads(o, dm, a, dqkv, b, du, zz, d, red, head_dim, loss_scale):
     n_tok = o.shape[0] * o.shape[1]
     rows = 256
 
@@ -755,8 +763,10 @@
     n_slab = qkv_w // head_dim
 
     def kernel(*refs):
-        src, outs, held, tiles = refs[:8], refs[8:12], refs[12:20], refs[20:24]
-        in_sem, out_sem = refs[24:]
+        src, red_ref, outs = refs[:8], refs[8], refs[9:13]
+        gain_out, loss_out = refs[13:15]
+        held, tiles = refs[15:23], refs[23:27]
+        in_sem, out_sem = refs[27:]
         loads = [pltpu.make_async_copy(src[i], held[i], in_sem.at[i]) for i in range(8)]
         for cp in loads:
             cp.start()
@@ -774,6 +784,8 @@
             for cp in cps:
                 cp.wait()
 
+        gain_out[...] = red_ref[0:2, :]
+        loss_out[...] = red_ref[2:3, 0:1] * loss_scale
         counts = []
         for pair in range(4):
             loads[2 * pair].wait()
@@ -801,19 +813,21 @@
                 finish(stores(pair, i, i % 2))
 
     any_spec = pl.BlockSpec(memory_space=pl.ANY)
+    vmem_spec = pl.BlockSpec(memory_space=pltpu.VMEM)
     return pl.pallas_call(
         kernel,
         out_shape=(jax.ShapeDtypeStruct((att_w, d_model), F32), jax.ShapeDtypeStruct((n_slab, d_model, head_dim), F32),
-                   jax.ShapeDtypeStruct((d_model, ff_w), F32), jax.ShapeDtypeStruct((ff_w, d_model), F32)),
-        in_specs=[any_spec] * 8,
-        out_specs=(any_spec,) * 4,
+                   jax.ShapeDtypeStruct((d_model, ff_w), F32), jax.ShapeDtypeStruct((ff_w, d_model), F32),
+                   jax.ShapeDtypeStruct((2, d_model), F32), jax.ShapeDtypeStruct((1, 1), F32)),
+        in_specs=[any_spec] * 8 + [vmem_spec],
+        out_specs=(any_spec,) * 4 + (vmem_spec,) * 2,
         scratch_shapes=[pltpu.VMEM(v.shape, BF16) for v in acts] + [
             pltpu.VMEM((1, att_w, d_model), F32), pltpu.VMEM((2, rows, qkv_w), F32),
             pltpu.VMEM((2, rows, ff_w), F32), pltpu.VMEM((2, rows, d_model), F32),
             pltpu.SemaphoreType.DMA((8,)), pltpu.SemaphoreType.DMA((4, 2))],
         compiler_params=pltpu.CompilerParams(vmem_limit_bytes=67_043_328),
         name="weight_grads",
-    )(*acts)
+    )(*acts, red)
 
 
 def solution(mesh):
@@ -826,13 +840,13 @@
             dims, x_in, y_target,
             w_qkv[0].transpose(1, 2, 0, 3).reshape(3 * heads, d_model, head_dim),
             w_out[0].reshape(heads * head_dim, d_model), w_up[0], w_down[0], norm_gain[0])
-        g_out, g_qkv, g_up, g_down = weight_grads(o, dm, a, dqkv, b, du, zz, d, head_dim)
+        g_out, g_qkv, g_up, g_down, g_gain, loss = weight_grads(
+            o, dm, a, dqkv, b, du, zz, d, red, head_dim, 0.5 / (n_batch * seq_len * d_model))
         grad_qkv = g_qkv.reshape(3, heads, d_model, head_dim).transpose(2, 0, 1, 3)[None]
         grad_out = g_out.reshape(1, heads, head_dim, d_model)
         grad_up = g_up[None]
         grad_down = g_down[None]
-        loss = 0.5 * red[2, 0:1] / (n_batch * seq_len * d_model)
-        return loss, grad_qkv, grad_out, grad_up, grad_down, red[None, 0:2]
+        return loss.reshape(1), grad_qkv, grad_out, grad_up, grad_down, g_gain[None]
 
     act_spec = P("data", None, None)
     weight_specs = (

time: 731 us -> 716 us (0.979)
  Pallas kernels: 726 us -> 715 us
    pallas_call x1, Pallas kernels: 695 us -> 683 us  [layer_step(): pl.pallas_call(kernel, out_shape=(out(d_model), out(d_model), out(d_model...]
where the time goes in v6:
time: 716 us
  Pallas kernels  715 us (100%)
    pallas_call x1, Pallas kernels, layer_step(): pl.pallas_call(kernel, out_shape=(out(d_model), out(d_model), out(d_model...  683 us
    pallas_call x1, Pallas kernels, weight_grads(): pl.pallas_call(kernel, out_shape=(jax.ShapeDtypeStruct((att_w, d_model),...  32.2 us

profile of v6, /device:TPU:0, one launch (start us, length us, event | category | flops | bytes accessed | tf_op | source)
XLA Modules:
  0.0 715.8 jit_solution(15203434179057416284)
XLA Ops:
  0.6 682.9 %layer_step.1 = (bf16[24,64,1536]{2,1,0:T(8,128)(2,1)}, bf16[24,64,1536]{2,1,0:T(8,128)(2,1)}, bf16[24,64,1536]{2,1,0:T(8,128)(2,1)}, bf16[24,64,1536]{2,1,0:T(8...) custom-call(bf16[3,512,1536]{2,1,0:T(8,128)(2,1)} %x_ref.1, ...), custom_call_target="tpu_custom_call" | custom-call | tf_op jit(solution)/shard_map/layer_step/pallas_call | solution.py:721
  683.6 32.2 %weight_grads.1 = (f32[384,1536]{1,0:T(8,128)}, f32[9,1536,128]{2,1,0:T(8,128)}, f32[1536,1536]{1,0:T(8,128)}, f32[1536,1536]{1,0:T(8,128)}, f32[2,1536]{1,0:T(2,128)}, /*index=5*/f32[1,1]{1,0:T(1,128)}) custom-call(bf16[1536,384]{1,0:T(8,128)(2,1)} %bitcast.38, bf16[1536,1536]{1,0:T(8,128)(2,1)} %bitcast.30, bf16[1536,1536]{1,0:T(8,128)(2,1)} %bitcast.27, ...), custom_call_target="tpu_custom_call" | custom-call | tf_op jit(solution)/shard_map/weight_grads/pallas_call | solution.py:817

commit v7 on v6

--- a/solution.py
+++ b/solution.py
@@ -31,10 +31,10 @@
 
 
 ORDER = (
-    (0, 3), (0, 7), (1, 2), (1, 9), (1, 3), (1, 1), (1, 5), (0, 8), (0, 4), (0, 0), (0, 1), (0, 6), (1, 10), (1,
-    7), (0, 10), (1, 4), (1, 0), (1, 8), (1, 6), (0, 2), (0, 9), (0, 5),
+    (1, 6), (0, 3), (1, 2), (0, 7), (0, 9), (0, 5), (1, 3), (0, 8), (1, 9), (0, 1), (1, 1), (1, 7), (0, 0), (0,
+    2), (1, 5), (1, 8), (0, 4), (0, 6), (1, 0), (0, 10), (1, 4), (1, 10),
 )
-BACK_START, BACK_STEP = 11, 13
+BACK_START, BACK_STEP = 13, 10
 
 
 def lags(back):
@@ -54,7 +54,7 @@
     ff_w = w_up.shape[1]
     n_head = att_w // head_dim
     tok = 64
-    n_part = 1
+    n_part = 2
     row = tok // (2 * n_part)
     n_block = 2 * n_part
     per_seq = seq_len // tok

time: 716 us -> 691 us (0.965)
  Pallas kernels: 715 us -> 690 us
    pallas_call x1, Pallas kernels: 683 us -> 658 us  [layer_step(): pl.pallas_call(kernel, out_shape=(out(d_model), out(d_model), out(d_model...]
where the time goes in v7:
time: 691 us
  Pallas kernels  690 us (100%)
    pallas_call x1, Pallas kernels, layer_step(): pl.pallas_call(kernel, out_shape=(out(d_model), out(d_model), out(d_model...  658 us
    pallas_call x1, Pallas kernels, weight_grads(): pl.pallas_call(kernel, out_shape=(jax.ShapeDtypeStruct((att_w, d_model),...  32.2 us

profile of v7, /device:TPU:0, one launch (start us, length us, event | category | flops | bytes accessed | tf_op | source)
XLA Modules:
  0.0 690.6 jit_solution(7618510524784897966)
XLA Ops:
  0.6 657.7 %layer_step.1 = (bf16[24,64,1536]{2,1,0:T(8,128)(2,1)}, bf16[24,64,1536]{2,1,0:T(8,128)(2,1)}, bf16[24,64,1536]{2,1,0:T(8,128)(2,1)}, bf16[24,64,1536]{2,1,0:T(8...) custom-call(bf16[3,512,1536]{2,1,0:T(8,128)(2,1)} %x_ref.1, ...), custom_call_target="tpu_custom_call" | custom-call | tf_op jit(solution)/shard_map/layer_step/pallas_call | solution.py:721
  658.4 32.2 %weight_grads.1 = (f32[384,1536]{1,0:T(8,128)}, f32[9,1536,128]{2,1,0:T(8,128)}, f32[1536,1536]{1,0:T(8,128)}, f32[1536,1536]{1,0:T(8,128)}, f32[2,1536]{1,0:T(2,128)}, /*index=5*/f32[1,1]{1,0:T(1,128)}) custom-call(bf16[1536,384]{1,0:T(8,128)(2,1)} %bitcast.38, bf16[1536,1536]{1,0:T(8,128)(2,1)} %bitcast.30, bf16[1536,1536]{1,0:T(8,128)(2,1)} %bitcast.27, ...), custom_call_target="tpu_custom_call" | custom-call | tf_op jit(solution)/shard_map/weight_grads/pallas_call | solution.py:817

commit v8 on v7

--- a/solution.py
+++ b/solution.py
@@ -225,16 +225,24 @@
             def mine(self, k):
                 return part[self.op, self.ss, rows_of(k), :]
 
-            def start(self):
+            def start(self, j):
                 @pl.when(outer)
                 def _():
+                    @pl.when(j >= n_send)
+                    def _():
+                        self.drain_outer()
+
                     for k in [far + q for q in quarters] + [near + q for q in quarters]:
                         send_p[self.op, self.ss, k] = self.mine(k).astype(BF16)
                         self.in_copy(k).start()
 
-            def relay(self):
+            def relay(self, j):
                 @pl.when(inner)
                 def _():
+                    @pl.when(j >= n_send)
+                    def _():
+                        self.drain_inner()
+
                     for q in quarters:
                         k = far + q
                         self.in_copy(k).wait_recv()
@@ -248,19 +256,26 @@
                 self.cross_copy(k, q).wait_recv()
                 return (self.mine(k) + recv_o[self.op, self.rs, k].astype(F32)) + recv_i[self.op, self.rs, q].astype(F32)
 
+            def drain_outer(self):
+                for k in range(n_block):
+                    self.in_copy(k).wait_send()
+
+            def drain_inner(self):
+                for q in quarters:
+                    self.cross_copy(far + q, q).wait_send()
+
             def drain(self):
                 @pl.when(outer)
                 def _():
-                    for k in range(n_block):
-                        self.in_copy(k).wait_send()
+                    self.drain_outer()
 
                 @pl.when(inner)
                 def _():
-                    for q in quarters:
-                        self.cross_copy(far + q, q).wait_send()
+                    self.drain_inner()
 
         def save(kind, src, src_slot, dst, j, u):
-            return pltpu.make_async_copy(src.at[src_slot], dst.at[u], save_sem.at[kind, lax.rem(j, n_gath)])
+            return pltpu.make_async_copy(src.at[src_slot], dst.at[u],
+                                         save_sem.at[kind, lax.rem(j, n_send if kind % 2 else n_gath)])
 
         def sslot(u):
             return lax.rem(u, n_send)
@@ -352,6 +367,10 @@
         def f_relay_a(j, u):
             @pl.when(st > 0)
             def _():
+                @pl.when(j >= n_gath)
+                def _():
+                    gather_a(u).drain()
+
                 gather_a(u).relay()
 
         def f_collect_a(j, u):
@@ -366,6 +385,17 @@
                 for cp in qkv_copies:
                     cp.wait()
                 w_copies[0].wait()
+
+            @pl.when(j >= n_gath)
+            def _():
+                save_a(u).wait()
+                save_b(u).wait()
+                gather_b(u).drain()
+                gather_b(u).drain_own()
+
+            @pl.when(j >= n_send)
+            def _():
+                save_o(u).wait()
 
             s = sslot(u)
             p = lax.rem(u, per_seq)
@@ -376,11 +406,11 @@
                 ost[s, :, pl.ds(i * head_dim, head_dim)] = dot_nn(pr.astype(BF16), v).astype(BF16)
             save_o(u).start()
             part[0, s] = dot_nn(ost[s], wout[...])
-            Scatter(0, u).start()
+            Scatter(0, u).start(j)
 
         def scatter_relay(op):
             def run(j, u):
-                Scatter(op, j).relay()
+                Scatter(op, j).relay(j)
             return run
 
         def f_middle(j, u):
@@ -398,13 +428,6 @@
                     bbuf[gslot(u), rows_of(near + q), :] = (m * rms_inverse(m) * gain_b).astype(BF16)
                     gather_b(u).send(q)
 
-            sc.drain()
-            save_o(u).wait()
-
-            @pl.when(st > 0)
-            def _():
-                gather_a(u).drain()
-
         def f_relay_b(j, u):
             gather_b(u).relay()
 
@@ -418,7 +441,10 @@
                 w_copies[2].wait()
 
             s = sslot(u)
-            save_a(u).wait()
+            @pl.when(j >= n_send)
+            def _():
+                save_z(u).wait()
+
             save_b(u).start()
 
             @pl.when(is_last & inner)
@@ -437,7 +463,7 @@
             lax.fori_loop(0, tok // sub_rows, act, 0)
             save_z(u).start()
             part[1, s] = dot_nn(zst[s], wdown[...])
-            Scatter(1, u).start()
+            Scatter(1, u).start(j)
 
         def f_leave(j, u):
             sc = Scatter(1, u)
@@ -479,22 +505,24 @@
                 def _():
                     hand_h(u, j).start()
 
-            sc.drain()
-            gather_b(u).drain()
-            gather_b(u).drain_own()
-            save_b(u).wait()
-            save_z(u).wait()
-
         forward = (f_enter, f_relay_a, f_collect_a, f_attention, scatter_relay(0), f_middle, f_relay_b, f_collect_b, f_mlp,
                    scatter_relay(1), f_leave)
 
         def b_enter(j, u):
             @pl.when(is_last & inner)
             def _():
+                @pl.when(j >= n_gath)
+                def _():
+                    gather_d(j, u).drain_own()
+
                 for q in quarters:
                     gather_d(j, u).send(q)
 
         def b_relay_d(j, u):
+            @pl.when(j >= n_gath)
+            def _():
+                gather_d(j, u).drain()
+
             gather_d(j, u).relay()
 
         def b_collect_d(j, u):
@@ -505,6 +533,17 @@
                 gather_d(j, u).own()
 
         def b_mlp(j, u):
+            @pl.when(j >= n_gath)
+            def _():
+                save_d(j, u).wait()
+                save_dm(j, u).wait()
+                gather_dm(j).drain()
+                gather_dm(j).drain_own()
+
+            @pl.when(j >= n_send)
+            def _():
+                save_du(j, u).wait()
+
             s = sslot(j)
             save_d(j, u).start()
             part[2, s] = dot_nt(d_all[u], wdown[...])
@@ -521,7 +560,7 @@
             lax.fori_loop(0, tok // sub_rows, act, 0)
             save_du(j, u).start()
             part[2, s] = dot_nt(dust[s], wup[...])
-            Scatter(2, j).start()
+            Scatter(2, j).start(j)
 
         def b_middle(j, u):
             sc = Scatter(2, j)
@@ -541,15 +580,6 @@
                     dmbuf[gslot(j), rows_of(near + q), :] = dm.astype(BF16)
                     gather_dm(j).send(q)
 
-            sc.drain()
-            gather_d(j, u).drain()
-
-            @pl.when(is_last)
-            def _():
-                gather_d(j, u).drain_own()
-
-            save_du(j, u).wait()
-
         def b_relay_dm(j, u):
             gather_dm(j).relay()
 
@@ -559,7 +589,10 @@
         def b_attention(j, u):
             s = sslot(j)
             p = lax.rem(u, per_seq)
-            save_d(j, u).wait()
+            @pl.when(j >= n_send)
+            def _():
+                save_dqkv(j, u).wait()
+
             save_dm(j, u).start()
 
             @pl.when(is_first)
@@ -589,12 +622,12 @@
 
             @pl.when(st > 0)
             def _():
-                Scatter(3, j).start()
+                Scatter(3, j).start(j)
 
         def b_relay_h(j, u):
             @pl.when(st > 0)
             def _():
-                Scatter(3, j).relay()
+                Scatter(3, j).relay(j)
 
         def b_leave(j, u):
             s = lax.rem(j, n_hand)
@@ -620,8 +653,6 @@
                             dg - normed * jnp.mean(dg * normed, axis=-1, keepdims=True))).astype(BF16)
                         hand_quarter(True, u, j, q, begin)
 
-                sc.drain()
-
             @pl.when(is_first)
             def _():
                 x_again(j, u).wait()
@@ -630,17 +661,69 @@
                     h32 = xtmp[sslot(j), rs, :].astype(F32)
                     ga8[...] += fold(part[3, sslot(j), rs, :] * (h32 * rms_inverse(h32)))
 
-            gather_dm(j).drain()
-            gather_dm(j).drain_own()
-            save_dm(j, u).wait()
-            save_dqkv(j, u).wait()
-
         backward = (b_enter, b_relay_d, b_collect_d, b_mlp, scatter_relay(2), b_middle, b_relay_dm, b_collect_dm,
                     b_attention, b_relay_h, b_leave)
         f_lag, b_lag = lags(False), lags(True)
         back_from = BACK_START + BACK_STEP * (last_s - st)
 
+        def hand_finish(back):
+            @pl.when(inner)
+            def _():
+                for j in range(n_unit - n_hand, n_unit):
+                    hand_sent(back, j, j)
+
+        def finish_forward():
+            for j in range(n_unit - n_gath, n_unit):
+                save_a(j).wait()
+                save_b(j).wait()
+                gather_b(j).drain()
+                gather_b(j).drain_own()
+
+                @pl.when(st > 0)
+                def _():
+                    gather_a(j).drain()
+
+            for j in range(n_unit - n_send, n_unit):
+                save_o(j).wait()
+                save_z(j).wait()
+                Scatter(0, j).drain()
+                Scatter(1, j).drain()
+
+            @pl.when(st < last_s)
+            def _():
+                hand_finish(False)
+
+        def finish_backward():
+            for j in range(n_unit - n_gath, n_unit):
+                save_d(j, j).wait()
+                save_dm(j, j).wait()
+                gather_dm(j).drain()
+                gather_dm(j).drain_own()
+                gather_d(j, j).drain()
+
+                @pl.when(is_last)
+                def _():
+                    gather_d(j, j).drain_own()
+
+            for j in range(n_unit - n_send, n_unit):
+                save_du(j, j).wait()
+                save_dqkv(j, j).wait()
+                Scatter(2, j).drain()
+
+                @pl.when(st > 0)
+                def _():
+                    Scatter(3, j).drain()
+
+            @pl.when(st > 0)
+            def _():
+                hand_finish(True)
+                gain_send().wait_send()
+
         def turn(i, carry):
+            @pl.when(i == n_unit + f_lag[-1])
+            def _():
+                finish_forward()
+
             for back, phase in ORDER:
                 j = (i - back_from - b_lag[phase]) if back else (i - f_lag[phase])
 
@@ -658,37 +741,17 @@
         def loss_send():
             return rdma(lossacc, lossacc, loss_sem.at[0], loss_sem.at[1], stage=st - 1)
 
-        def hand_finish(back):
-            @pl.when(inner)
-            def _():
-                for j in range(n_unit - n_hand, n_unit):
-                    hand_sent(back, j, j)
-
         @pl.when(is_last)
         def _():
             loss_send().start()
 
         @pl.when(st < last_s)
         def _():
-            hand_finish(False)
-
-        @pl.when(st > 0)
-        def _():
-            hand_finish(True)
-            gain_send().wait_send()
-
-        @pl.when(is_last)
-        def _():
-            loss_send().wait_send()
-
-        @pl.when(st < last_s)
-        def _():
             loss_send().wait_recv()
 
             @pl.when(st > 0)
             def _():
                 loss_send().start()
-                loss_send().wait_send()
 
         loss_row = jnp.sum(jnp.sum(lossacc[...], axis=0, keepdims=True), axis=1, keepdims=True)
         gx[z, 0:1, :] = jnp.sum(ga8[...], axis=0, keepdims=True)
@@ -704,6 +767,12 @@
 
         for dz in range(1, nz):
             gx_send(dz).start()
+        finish_backward()
+
+        @pl.when(st > 0)
+        def _():
+            loss_send().wait_send()
+
         for dz in range(1, nz):
             gx_recv(dz).wait_recv()
         red_out[...] = gx[0] + gx[1] + gx[2] + gx[3]

time: 691 us -> 692 us (level)
  no operation moved by 1% of the time
where the time goes in v8:
time: 692 us
  Pallas kernels  691 us (100%)
    pallas_call x1, Pallas kernels, layer_step(): pl.pallas_call(kernel, out_shape=(out(d_model), out(d_model), out(d_model...  659 us
    pallas_call x1, Pallas kernels, weight_grads(): pl.pallas_call(kernel, out_shape=(jax.ShapeDtypeStruct((att_w, d_model),...  32.2 us

profile of v8, /device:TPU:0, one launch (start us, length us, event | category | flops | bytes accessed | tf_op | source)
XLA Modules:
  0.0 691.8 jit_solution(2613133648196697606)
XLA Ops:
  0.6 659.0 %layer_step.1 = (bf16[24,64,1536]{2,1,0:T(8,128)(2,1)}, bf16[24,64,1536]{2,1,0:T(8,128)(2,1)}, bf16[24,64,1536]{2,1,0:T(8,128)(2,1)}, bf16[24,64,1536]{2,1,0:T(8...) custom-call(bf16[3,512,1536]{2,1,0:T(8,128)(2,1)} %x_ref.1, ...), custom_call_target="tpu_custom_call" | custom-call | tf_op jit(solution)/shard_map/layer_step/pallas_call | solution.py:790
  659.6 32.2 %weight_grads.1 = (f32[384,1536]{1,0:T(8,128)}, f32[9,1536,128]{2,1,0:T(8,128)}, f32[1536,1536]{1,0:T(8,128)}, f32[1536,1536]{1,0:T(8,128)}, f32[2,1536]{1,0:T(2,128)}, /*index=5*/f32[1,1]{1,0:T(1,128)}) custom-call(bf16[1536,384]{1,0:T(8,128)(2,1)} %bitcast.38, bf16[1536,1536]{1,0:T(8,128)(2,1)} %bitcast.30, bf16[1536,1536]{1,0:T(8,128)(2,1)} %bitcast.27, ...), custom_call_target="tpu_custom_call" | custom-call | tf_op jit(solution)/shard_map/weight_grads/pallas_call | solution.py:886

commit v9 on v8

--- a/solution.py
+++ b/solution.py
@@ -31,10 +31,10 @@
 
 
 ORDER = (
-    (1, 6), (0, 3), (1, 2), (0, 7), (0, 9), (0, 5), (1, 3), (0, 8), (1, 9), (0, 1), (1, 1), (1, 7), (0, 0), (0,
-    2), (1, 5), (1, 8), (0, 4), (0, 6), (1, 0), (0, 10), (1, 4), (1, 10),
+    (1, 6), (1, 3), (0, 4), (0, 0), (1, 9), (0, 1), (1, 1), (0, 12), (1, 7), (0, 6), (1, 5), (0, 10), (1, 0), (0,
+    9), (1, 8), (0, 5), (0, 2), (1, 4), (0, 11), (1, 10), (1, 2), (0, 3), (0, 7), (0, 8),
 )
-BACK_START, BACK_STEP = 13, 10
+BACK_START, BACK_STEP = 11, 12
 
 
 def lags(back):
@@ -59,6 +59,7 @@
     n_block = 2 * n_part
     per_seq = seq_len // tok
     n_unit = n_seq * per_seq
+    key_step = per_seq // 4
     scale = head_dim ** -0.5
     inv_count = 1.0 / (n_seq * seq_len * d_model)
     last_z, last_s = nz - 1, ns - 1
@@ -69,17 +70,19 @@
 
     def kernel(x_ref, y_ref, wqkv_h, wout_h, wup_h, wdown_h, gain_ref,
                a_out, b_out, d_out, dm_out, dqkv_out, o_out, z_out, du_out, red_out,
-               wqkv, wout, wup, wdown, hslot, yslot, a_all, d_all, bbuf, dmbuf, xtmp,
+               wqkv, wout, wup, wdown, hslot, yslot, a_all, d_all, nbuf, bbuf, dmbuf, xtmp,
                qkv_all, u_all, m_all, ost, zst, dust, dqkvst, datt, part,
                recv_o, recv_i, send_p, hout, aout, dout, dkacc, dvacc,
                gains, gain_next, lossacc, ga8, gb8, gx,
                w_sem, hsem, ysem, x_sem, gain_sem, hand_sem, back_sem, save_sem,
-               a_rs, d_rs, a_si, a_so, d_si, d_so, b_rs, dm_rs, b_si, b_so, dm_si, dm_so,
+               a_rs, d_rs, a_si, a_so, d_si, d_so, n_rs, n_si, n_so, n_fw, b_rs, dm_rs, b_si, b_so, dm_si, dm_so,
                rs_ro, rs_ri, rs_s, loss_sem, gx_s, gx_r):
         z = lax.axis_index("model")
         st = lax.axis_index("stage")
         is_first = st == 0
         is_last = st == last_s
+        crosses = st == ns // 2 - 1
+        crossed = st == ns // 2
         inner = (z > 0) & (z < last_z)
         outer = (z == 0) | (z == last_z)
         side = lax.div(z, 2)
@@ -121,12 +124,17 @@
 
         @pl.when(is_first)
         def _():
-            @pl.loop(0, n_unit)
+            for u in range(n_send):
+                x_copy(u).start()
+
+        for cp in qkv_copies + w_copies:
+            cp.start()
+
+        @pl.when(is_first)
+        def _():
+            @pl.loop(n_send, n_unit)
             def _(u):
                 x_copy(u).start()
-
-        for cp in qkv_copies + w_copies:
-            cp.start()
 
         barrier = pltpu.get_barrier_semaphore()
         for i in range(1, nz * ns):
@@ -204,6 +212,13 @@
         def gather_d(j, u):
             return Gather(d_all, u, d_rs, d_si, d_so, lax.rem(j, n_gath))
 
+        def gather_n(u):
+            return Gather(nbuf, lax.rem(u, n_gath), n_rs, n_si, n_so, lax.rem(u, n_gath))
+
+        def forward_n(u, k):
+            g = lax.rem(u, n_gath)
+            return rdma(nbuf.at[g, rows_of(k), :], a_all.at[u, rows_of(k), :], n_fw.at[g, k], a_rs.at[u, k], stage=st + 1)
+
         def gather_b(u):
             return Gather(bbuf, lax.rem(u, n_gath), b_rs, b_si, b_so, lax.rem(u, n_gath))
 
@@ -325,11 +340,13 @@
                 act(rdma(src.at[s, q_rows(q), :], buf.at[u, rows_of(k), :], own.at[s, 3 * q + i], sems.at[u, k],
                          model=peer, stage=(st - 1) if back else (st + 1)))
 
-        def hand_sent(back, u, j):
-            for q in quarters:
-                hand_quarter(back, u, j, q, sent)
-            if not back:
-                hand_h(u, j).wait_send()
+        def hand_sent(u, j):
+            @pl.when(st != ns // 2 - 1)
+            def _():
+                for q in quarters:
+                    hand_quarter(False, u, j, q, sent)
+
+            hand_h(u, j).wait_send()
 
         def begin(cp):
             cp.start()
@@ -337,12 +354,13 @@
         def sent(cp):
             cp.wait_send()
 
-        def softmax_of(u, p, i):
+        def softmax_of(u, p, i, n_tile):
             first = u - p
+            n_key = n_tile * tok
             cols = pl.ds(i * head_dim, head_dim)
             q = qkv_all[u, :, cols]
-            k = qkv_all[pl.ds(first, per_seq), :, pl.ds(att_w + i * head_dim, head_dim)].reshape(seq_len, head_dim)
-            v = qkv_all[pl.ds(first, per_seq), :, pl.ds(2 * att_w + i * head_dim, head_dim)].reshape(seq_len, head_dim)
+            k = qkv_all[pl.ds(first, n_tile), :, pl.ds(att_w + i * head_dim, head_dim)].reshape(n_key, head_dim)
+            v = qkv_all[pl.ds(first, n_tile), :, pl.ds(2 * att_w + i * head_dim, head_dim)].reshape(n_key, head_dim)
             sc = dot_nt(q, k) * scale
             q_pos = p * tok + lax.broadcasted_iota(jnp.int32, sc.shape, 0)
             k_pos = lax.broadcasted_iota(jnp.int32, sc.shape, 1)
@@ -351,6 +369,12 @@
             pr = e * (1.0 / jnp.sum(e, axis=-1, keepdims=True))
             return q, k, v, pr
 
+        def by_reach(p, body):
+            for n_tile in range(key_step, per_seq + 1, key_step):
+                @pl.when((p >= n_tile - key_step) & (p < n_tile))
+                def _():
+                    body(n_tile)
+
         def fold(v):
             return jnp.sum(v.reshape(v.shape[0] // 8, 8, d_model), axis=0)
 
@@ -365,7 +389,7 @@
                     a_all[u, rs, :] = (h32 * rms_inverse(h32) * gain_a).astype(BF16)
 
         def f_relay_a(j, u):
-            @pl.when(st > 0)
+            @pl.when((st > 0) & (st != ns // 2))
             def _():
                 @pl.when(j >= n_gath)
                 def _():
@@ -374,10 +398,15 @@
                 gather_a(u).relay()
 
         def f_collect_a(j, u):
-            @pl.when(st > 0)
+            @pl.when((st > 0) & (st != ns // 2))
             def _():
                 gather_a(u).collect()
                 gather_a(u).own()
+
+            @pl.when(crossed)
+            def _():
+                for k in range(n_block):
+                    forward_n(u, k).wait_recv()
 
         def f_attention(j, u):
             @pl.when(j == 0)
@@ -401,9 +430,12 @@
             p = lax.rem(u, per_seq)
             save_a(u).start()
             qkv_all[u] = dot_nn(a_all[u], wqkv[...]).astype(BF16)
-            for i in range(n_head):
-                _, _, v, pr = softmax_of(u, p, i)
-                ost[s, :, pl.ds(i * head_dim, head_dim)] = dot_nn(pr.astype(BF16), v).astype(BF16)
+            def attend(n_tile):
+                for i in range(n_head):
+                    _, _, v, pr = softmax_of(u, p, i, n_tile)
+                    ost[s, :, pl.ds(i * head_dim, head_dim)] = dot_nn(pr.astype(BF16), v).astype(BF16)
+
+            by_reach(p, attend)
             save_o(u).start()
             part[0, s] = dot_nn(ost[s], wout[...])
             Scatter(0, u).start(j)
@@ -444,6 +476,10 @@
             @pl.when(j >= n_send)
             def _():
                 save_z(u).wait()
+
+            @pl.when(crosses & (j >= n_gath))
+            def _():
+                drain_n(u)
 
             save_b(u).start()
 
@@ -479,7 +515,7 @@
                 def _():
                     @pl.when(j >= n_hand)
                     def _():
-                        hand_sent(False, u, j)
+                        hand_sent(u, j)
 
                 @pl.when(is_last)
                 def _():
@@ -491,8 +527,19 @@
 
                     @pl.when(st < last_s)
                     def _():
-                        aout[s, q_rows(q), :] = (h32 * rms_inverse(h32) * gain_next[0:1, :]).astype(BF16)
-                        hand_quarter(False, u, j, q, begin)
+                        a_new = (h32 * rms_inverse(h32) * gain_next[0:1, :]).astype(BF16)
+
+                        @pl.when(crosses)
+                        def _():
+                            nbuf[gslot(u), rows_of(near + q), :] = a_new
+                            gather_n(u).send(q)
+                            forward_n(u, near + q).start()
+
+                        @pl.when(st != ns // 2 - 1)
+                        def _():
+                            aout[s, q_rows(q), :] = a_new
+                            hand_quarter(False, u, j, q, begin)
+
                         hout[s, q_rows(q), :] = h_new
 
                     @pl.when(is_last)
@@ -505,8 +552,28 @@
                 def _():
                     hand_h(u, j).start()
 
+        def f_relay_n(j, u):
+            @pl.when(crosses & inner)
+            def _():
+                gather_n(u).relay()
+                for q in quarters:
+                    forward_n(u, far + q).start()
+
+        def f_forward_n(j, u):
+            @pl.when(crosses & outer)
+            def _():
+                gather_n(u).collect()
+                for k in range(n_block):
+                    forward_n(u, k).start()
+
+        def drain_n(u):
+            for k in range(n_block):
+                forward_n(u, k).wait_send()
+            gather_n(u).drain()
+            gather_n(u).drain_own()
+
         forward = (f_enter, f_relay_a, f_collect_a, f_attention, scatter_relay(0), f_middle, f_relay_b, f_collect_b, f_mlp,
-                   scatter_relay(1), f_leave)
+                   scatter_relay(1), f_leave, f_relay_n, f_forward_n)
 
         def b_enter(j, u):
             @pl.when(is_last & inner)
@@ -606,15 +673,20 @@
 
             datt[...] = dot_nt(dmbuf[gslot(j)], wout[...]).astype(BF16)
             p_rows = pl.ds(pl.multiple_of(p * tok, tok), tok)
-            for h in range(n_head):
-                cols = pl.ds(h * head_dim, head_dim)
-                q, k, v, pr = softmax_of(u, p, h)
-                da = datt[:, cols]
-                dp = dot_nt(da, v)
-                ds = (pr * (dp - jnp.sum(pr * dp, axis=-1, keepdims=True)) * scale).astype(BF16)
-                dvacc[:, cols] += dot_tn(pr.astype(BF16), da)
-                dkacc[:, cols] += dot_tn(ds, q)
-                dqkvst[s, :, cols] = dot_nn(ds, k).astype(BF16)
+
+            def attend_back(n_tile):
+                keys = pl.ds(0, n_tile * tok)
+                for h in range(n_head):
+                    cols = pl.ds(h * head_dim, head_dim)
+                    q, k, v, pr = softmax_of(u, p, h, n_tile)
+                    da = datt[:, cols]
+                    dp = dot_nt(da, v)
+                    ds = (pr * (dp - jnp.sum(pr * dp, axis=-1, keepdims=True)) * scale).astype(BF16)
+                    dvacc[keys, cols] += dot_tn(pr.astype(BF16), da)
+                    dkacc[keys, cols] += dot_tn(ds, q)
+                    dqkvst[s, :, cols] = dot_nn(ds, k).astype(BF16)
+
+            by_reach(p, attend_back)
             dqkvst[s, :, pl.ds(att_w, att_w)] = dkacc[p_rows, :].astype(BF16)
             dqkvst[s, :, pl.ds(2 * att_w, att_w)] = dvacc[p_rows, :].astype(BF16)
             save_dqkv(j, u).start()
@@ -640,7 +712,8 @@
                 def _():
                     @pl.when(j >= n_hand)
                     def _():
-                        hand_sent(True, u, j)
+                        for q in quarters:
+                            hand_quarter(True, u, j, q, sent)
 
                     for q in quarters:
                         h32 = hslot[u, q_rows(q), :].astype(F32)
@@ -670,7 +743,11 @@
             @pl.when(inner)
             def _():
                 for j in range(n_unit - n_hand, n_unit):
-                    hand_sent(back, j, j)
+                    if back:
+                        for q in quarters:
+                            hand_quarter(True, j, j, q, sent)
+                    else:
+                        hand_sent(j, j)
 
         def finish_forward():
             for j in range(n_unit - n_gath, n_unit):
@@ -679,9 +756,13 @@
                 gather_b(j).drain()
                 gather_b(j).drain_own()
 
-                @pl.when(st > 0)
+                @pl.when((st > 0) & (st != ns // 2))
                 def _():
                     gather_a(j).drain()
+
+                @pl.when(crosses)
+                def _():
+                    drain_n(j)
 
             for j in range(n_unit - n_send, n_unit):
                 save_o(j).wait()
@@ -797,7 +878,8 @@
             vmem((d_model, qkv_w), BF16), vmem((att_w, d_model), BF16), vmem((d_model, ff_w), BF16), vmem((ff_w, d_model), BF16),
             vmem((n_unit, half, d_model), BF16), vmem((n_hand, half, d_model), BF16),
             vmem((n_unit, tok, d_model), BF16), vmem((n_unit, tok, d_model), BF16),
-            vmem((n_gath, tok, d_model), BF16), vmem((n_gath, tok, d_model), BF16), vmem((n_send, tok, d_model), BF16),
+            vmem((n_gath, tok, d_model), BF16), vmem((n_gath, tok, d_model), BF16), vmem((n_gath, tok, d_model), BF16),
+            vmem((n_send, tok, d_model), BF16),
             vmem((n_unit, tok, qkv_w), BF16), vmem((n_unit, tok, ff_w), F32), vmem((n_unit, half, d_model), F32),
             vmem((n_send, tok, att_w), BF16), vmem((n_send, tok, ff_w), BF16), vmem((n_send, tok, ff_w), BF16),
             vmem((n_send, tok, qkv_w), BF16), vmem((tok, att_w), BF16), vmem((4, n_send, tok, d_model), F32),
@@ -809,7 +891,9 @@
             vmem((8, d_model), F32), vmem((8, d_model), F32), vmem((8, d_model), F32), vmem((nz, 8, d_model), F32),
             dma((n_slab + 3,)), dma((n_unit,)), dma((n_hand,)), dma((n_send,)), dma((2,)), dma((n_hand, 3 * n_part + 1)), dma((n_hand, 3 * n_part)), dma((8, n_gath)),
             dma((n_unit, n_block)), dma((n_unit, n_block)), dma((n_gath, n_part)), dma((n_gath, n_block)),
-            dma((n_gath, n_part)), dma((n_gath, n_block)), dma((n_gath, n_block)), dma((n_gath, n_block)),
+            dma((n_gath, n_part)), dma((n_gath, n_block)),
+            dma((n_gath, n_block)), dma((n_gath, n_part)), dma((n_gath, n_block)), dma((n_gath, n_block)),
+            dma((n_gath, n_block)), dma((n_gath, n_block)),
             dma((n_gath, n_part)), dma((n_gath, n_block)), dma((n_gath, n_part)), dma((n_gath, n_block)),
             dma((4, n_recv, n_block)), dma((4, n_recv, n_part)), dma((4, n_send, n_block)),
             dma((2,)), dma((nz,)), dma((nz,)),

time: 692 us -> 710 us (1.026)
  Pallas kernels: 691 us -> 709 us
    pallas_call x1, Pallas kernels: 659 us -> 677 us  [layer_step(): pl.pallas_call(kernel, out_shape=(out(d_model), out(d_model), out(d_model...]
where the time goes in v9:
time: 710 us
  Pallas kernels  709 us (100%)
    pallas_call x1, Pallas kernels, layer_step(): pl.pallas_call(kernel, out_shape=(out(d_model), out(d_model), out(d_model...  677 us
    pallas_call x1, Pallas kernels, weight_grads(): pl.pallas_call(kernel, out_shape=(jax.ShapeDtypeStruct((att_w, d_model),...  32.2 us

profile of v9, /device:TPU:0, one launch (start us, length us, event | category | flops | bytes accessed | tf_op | source)
XLA Modules:
  0.0 709.9 jit_solution(10833455379863587828)
XLA Ops:
  0.6 676.9 %layer_step.1 = (bf16[24,64,1536]{2,1,0:T(8,128)(2,1)}, bf16[24,64,1536]{2,1,0:T(8,128)(2,1)}, bf16[24,64,1536]{2,1,0:T(8,128)(2,1)}, bf16[24,64,1536]{2,1,0:T(8...) custom-call(bf16[3,512,1536]{2,1,0:T(8,128)(2,1)} %x_ref.1, ...), custom_call_target="tpu_custom_call" | custom-call | tf_op jit(solution)/shard_map/layer_step/pallas_call | solution.py:871
  677.6 32.2 %weight_grads.1 = (f32[384,1536]{1,0:T(8,128)}, f32[9,1536,128]{2,1,0:T(8,128)}, f32[1536,1536]{1,0:T(8,128)}, f32[1536,1536]{1,0:T(8,128)}, f32[2,1536]{1,0:T(2,128)}, /*index=5*/f32[1,1]{1,0:T(1,128)}) custom-call(bf16[1536,384]{1,0:T(8,128)(2,1)} %bitcast.38, bf16[1536,1536]{1,0:T(8,128)(2,1)} %bitcast.30, bf16[1536,1536]{1,0:T(8,128)(2,1)} %bitcast.27, ...), custom_call_target="tpu_custom_call" | custom-call | tf_op jit(solution)/shard_map/weight_grads/pallas_call | solution.py:970

commit v10 on v8

--- a/solution.py
+++ b/solution.py
@@ -59,6 +59,7 @@
     n_block = 2 * n_part
     per_seq = seq_len // tok
     n_unit = n_seq * per_seq
+    key_step = per_seq // 4
     scale = head_dim ** -0.5
     inv_count = 1.0 / (n_seq * seq_len * d_model)
     last_z, last_s = nz - 1, ns - 1
@@ -121,12 +122,17 @@
 
         @pl.when(is_first)
         def _():
-            @pl.loop(0, n_unit)
+            for u in range(n_send):
+                x_copy(u).start()
+
+        for cp in qkv_copies + w_copies:
+            cp.start()
+
+        @pl.when(is_first)
+        def _():
+            @pl.loop(n_send, n_unit)
             def _(u):
                 x_copy(u).start()
-
-        for cp in qkv_copies + w_copies:
-            cp.start()
 
         barrier = pltpu.get_barrier_semaphore()
         for i in range(1, nz * ns):
@@ -337,12 +343,13 @@
         def sent(cp):
             cp.wait_send()
 
-        def softmax_of(u, p, i):
+        def softmax_of(u, p, i, n_tile):
             first = u - p
+            n_key = n_tile * tok
             cols = pl.ds(i * head_dim, head_dim)
             q = qkv_all[u, :, cols]
-            k = qkv_all[pl.ds(first, per_seq), :, pl.ds(att_w + i * head_dim, head_dim)].reshape(seq_len, head_dim)
-            v = qkv_all[pl.ds(first, per_seq), :, pl.ds(2 * att_w + i * head_dim, head_dim)].reshape(seq_len, head_dim)
+            k = qkv_all[pl.ds(first, n_tile), :, pl.ds(att_w + i * head_dim, head_dim)].reshape(n_key, head_dim)
+            v = qkv_all[pl.ds(first, n_tile), :, pl.ds(2 * att_w + i * head_dim, head_dim)].reshape(n_key, head_dim)
             sc = dot_nt(q, k) * scale
             q_pos = p * tok + lax.broadcasted_iota(jnp.int32, sc.shape, 0)
             k_pos = lax.broadcasted_iota(jnp.int32, sc.shape, 1)
@@ -351,6 +358,12 @@
             pr = e * (1.0 / jnp.sum(e, axis=-1, keepdims=True))
             return q, k, v, pr
 
+        def by_reach(p, body):
+            for n_tile in range(key_step, per_seq + 1, key_step):
+                @pl.when((p >= n_tile - key_step) & (p < n_tile))
+                def _():
+                    body(n_tile)
+
         def fold(v):
             return jnp.sum(v.reshape(v.shape[0] // 8, 8, d_model), axis=0)
 
@@ -401,9 +414,12 @@
             p = lax.rem(u, per_seq)
             save_a(u).start()
             qkv_all[u] = dot_nn(a_all[u], wqkv[...]).astype(BF16)
-            for i in range(n_head):
-                _, _, v, pr = softmax_of(u, p, i)
-                ost[s, :, pl.ds(i * head_dim, head_dim)] = dot_nn(pr.astype(BF16), v).astype(BF16)
+            def attend(n_tile):
+                for i in range(n_head):
+                    _, _, v, pr = softmax_of(u, p, i, n_tile)
+                    ost[s, :, pl.ds(i * head_dim, head_dim)] = dot_nn(pr.astype(BF16), v).astype(BF16)
+
+            by_reach(p, attend)
             save_o(u).start()
             part[0, s] = dot_nn(ost[s], wout[...])
             Scatter(0, u).start(j)
@@ -606,15 +622,20 @@
 
             datt[...] = dot_nt(dmbuf[gslot(j)], wout[...]).astype(BF16)
             p_rows = pl.ds(pl.multiple_of(p * tok, tok), tok)
-            for h in range(n_head):
-                cols = pl.ds(h * head_dim, head_dim)
-                q, k, v, pr = softmax_of(u, p, h)
-                da = datt[:, cols]
-                dp = dot_nt(da, v)
-                ds = (pr * (dp - jnp.sum(pr * dp, axis=-1, keepdims=True)) * scale).astype(BF16)
-                dvacc[:, cols] += dot_tn(pr.astype(BF16), da)
-                dkacc[:, cols] += dot_tn(ds, q)
-                dqkvst[s, :, cols] = dot_nn(ds, k).astype(BF16)
+
+            def attend_back(n_tile):
+                keys = pl.ds(0, n_tile * tok)
+                for h in range(n_head):
+                    cols = pl.ds(h * head_dim, head_dim)
+                    q, k, v, pr = softmax_of(u, p, h, n_tile)
+                    da = datt[:, cols]
+                    dp = dot_nt(da, v)
+                    ds = (pr * (dp - jnp.sum(pr * dp, axis=-1, keepdims=True)) * scale).astype(BF16)
+                    dvacc[keys, cols] += dot_tn(pr.astype(BF16), da)
+                    dkacc[keys, cols] += dot_tn(ds, q)
+                    dqkvst[s, :, cols] = dot_nn(ds, k).astype(BF16)
+
+            by_reach(p, attend_back)
             dqkvst[s, :, pl.ds(att_w, att_w)] = dkacc[p_rows, :].astype(BF16)
             dqkvst[s, :, pl.ds(2 * att_w, att_w)] = dvacc[p_rows, :].astype(BF16)
             save_dqkv(j, u).start()

time: 692 us -> 699 us (1.010)
  Pallas kernels: 691 us -> 698 us
where the time goes in v10:
time: 699 us; the launch traced here: 698 us
  Pallas kernels  698 us (100%)
    pallas_call x1, Pallas kernels, layer_step(): pl.pallas_call(kernel, out_shape=(out(d_model), out(d_model), out(d_model...  665 us
    pallas_call x1, Pallas kernels, weight_grads(): pl.pallas_call(kernel, out_shape=(jax.ShapeDtypeStruct((att_w, d_model),...  32.2 us

profile of v10, /device:TPU:0, one launch (start us, length us, event | category | flops | bytes accessed | tf_op | source)
XLA Modules:
  0.0 698.3 jit_solution(1978920748151241123)
XLA Ops:
  0.6 665.3 %layer_step.1 = (bf16[24,64,1536]{2,1,0:T(8,128)(2,1)}, bf16[24,64,1536]{2,1,0:T(8,128)(2,1)}, bf16[24,64,1536]{2,1,0:T(8,128)(2,1)}, bf16[24,64,1536]{2,1,0:T(8...) custom-call(bf16[3,512,1536]{2,1,0:T(8,128)(2,1)} %x_ref.1, ...), custom_call_target="tpu_custom_call" | custom-call | tf_op jit(solution)/shard_map/layer_step/pallas_call | solution.py:811
  666.0 32.2 %weight_grads.1 = (f32[384,1536]{1,0:T(8,128)}, f32[9,1536,128]{2,1,0:T(8,128)}, f32[1536,1536]{1,0:T(8,128)}, f32[1536,1536]{1,0:T(8,128)}, f32[2,1536]{1,0:T(2,128)}, /*index=5*/f32[1,1]{1,0:T(1,128)}) custom-call(bf16[1536,384]{1,0:T(8,128)(2,1)} %bitcast.38, bf16[1536,1536]{1,0:T(8,128)(2,1)} %bitcast.30, bf16[1536,1536]{1,0:T(8,128)(2,1)} %bitcast.27, ...), custom_call_target="tpu_custom_call" | custom-call | tf_op jit(solution)/shard_map/weight_grads/pallas_call | solution.py:907

commit v11 on v8

--- a/solution.py
+++ b/solution.py
@@ -148,55 +148,57 @@
             gain_send().start()
 
         class Gather:
-            def __init__(self, buf, slot, rsem, si, so, sslot):
-                self.buf, self.slot, self.rsem, self.si, self.so, self.sslot = buf, slot, rsem, si, so, sslot
+            def __init__(self, buf, slot, rsem, own_sem, far_sem, sslot):
+                self.buf, self.slot, self.rsem = buf, slot, rsem
+                self.own_sem, self.far_sem = own_sem.at[sslot], far_sem.at[sslot]
 
             def block(self, k):
                 return self.buf.at[self.slot, rows_of(k), :]
 
-            def inward(self, k, q):
-                return rdma(self.block(k), self.block(k), self.si.at[self.sslot, q], self.rsem.at[self.slot, k],
-                            model=inner_peer)
-
-            def outward(self, k):
-                return rdma(self.block(k), self.block(k), self.so.at[self.sslot, k], self.rsem.at[self.slot, k],
-                            model=outer_peer)
+            def inward(self, k):
+                return rdma(self.block(k), self.block(k), self.own_sem, self.rsem.at[self.slot, k], model=inner_peer)
+
+            def outward(self, k, sem):
+                return rdma(self.block(k), self.block(k), sem, self.rsem.at[self.slot, n_block], model=outer_peer)
+
+            def unit(self):
+                ref = self.buf.at[self.slot]
+                return rdma(ref, ref, self.own_sem, self.rsem.at[self.slot, n_block], model=outer_peer)
+
+            def half_unit(self):
+                ref = self.buf.at[self.slot, my_half, :]
+                return rdma(ref, ref, self.far_sem, self.rsem.at[self.slot, n_block], model=outer_peer)
 
             def send(self, q):
-                self.inward(near + q, q).start()
-                self.outward(near + q).start()
+                self.inward(near + q).start()
+                self.outward(near + q, self.own_sem).start()
 
             def relay(self):
                 @pl.when(inner)
                 def _():
                     for q in quarters:
-                        self.outward(far + q).wait_recv()
-                        self.outward(far + q).start()
+                        self.inward(far + q).wait_recv()
+                        self.outward(far + q, self.far_sem).start()
 
             def collect(self):
                 @pl.when(outer)
                 def _():
-                    for k in range(n_block):
-                        self.outward(k).wait_recv()
+                    self.unit().wait_recv()
 
             def own(self):
                 @pl.when(inner)
                 def _():
-                    for q in quarters:
-                        self.outward(near + q).wait_recv()
+                    self.half_unit().wait_recv()
 
             def drain(self):
                 @pl.when(inner)
                 def _():
-                    for q in quarters:
-                        self.outward(far + q).wait_send()
+                    self.half_unit().wait_send()
 
             def drain_own(self):
                 @pl.when(inner)
                 def _():
-                    for q in quarters:
-                        self.inward(near + q, q).wait_send()
-                        self.outward(near + q).wait_send()
+                    self.unit().wait_send()
 
         def gather_a(u):
             return Gather(a_all, u, a_rs, a_si, a_so, lax.rem(u, n_gath))
@@ -214,13 +216,17 @@
             def __init__(self, op, u):
                 self.op, self.ss, self.rs = op, lax.rem(u, n_send), lax.rem(u, n_recv)
 
-            def in_copy(self, k):
+            def in_copy(self, k, q):
                 return rdma(send_p.at[self.op, self.ss, k], recv_o.at[self.op, self.rs, k],
-                            rs_s.at[self.op, self.ss, k], rs_ro.at[self.op, self.rs, k], model=inner_peer)
+                            rs_s.at[self.op, self.ss], rs_ro.at[self.op, self.rs, q], model=inner_peer)
 
             def cross_copy(self, k, q):
                 return rdma(send_p.at[self.op, self.ss, k], recv_i.at[self.op, self.rs, q],
-                            rs_s.at[self.op, self.ss, k], rs_ri.at[self.op, self.rs, q], model=inner_peer)
+                            rs_s.at[self.op, self.ss], rs_ri.at[self.op, self.rs, q], model=inner_peer)
+
+            def near_copies(self):
+                return rdma(send_p.at[self.op, self.ss, pl.ds(near, n_part)], recv_o.at[self.op, self.rs, pl.ds(near, n_part)],
+                            rs_s.at[self.op, self.ss], rs_ro.at[self.op, self.rs, n_part], model=inner_peer)
 
             def mine(self, k):
                 return part[self.op, self.ss, rows_of(k), :]
@@ -232,9 +238,9 @@
                     def _():
                         self.drain_outer()
 
-                    for k in [far + q for q in quarters] + [near + q for q in quarters]:
+                    for k, q in [(far + q, q) for q in quarters] + [(near + q, n_part) for q in quarters]:
                         send_p[self.op, self.ss, k] = self.mine(k).astype(BF16)
-                        self.in_copy(k).start()
+                        self.in_copy(k, q).start()
 
             def relay(self, j):
                 @pl.when(inner)
@@ -245,24 +251,24 @@
 
                     for q in quarters:
                         k = far + q
-                        self.in_copy(k).wait_recv()
+                        self.in_copy(k, q).wait_recv()
                         send_p[self.op, self.ss, k] = (
                             self.mine(k) + recv_o[self.op, self.rs, k].astype(F32)).astype(BF16)
                         self.cross_copy(k, q).start()
 
             def total(self, q):
                 k = near + q
-                self.in_copy(k).wait_recv()
+                if q == 0:
+                    self.near_copies().wait_recv()
                 self.cross_copy(k, q).wait_recv()
                 return (self.mine(k) + recv_o[self.op, self.rs, k].astype(F32)) + recv_i[self.op, self.rs, q].astype(F32)
 
             def drain_outer(self):
-                for k in range(n_block):
-                    self.in_copy(k).wait_send()
+                ref = send_p.at[self.op, self.ss]
+                rdma(ref, ref, rs_s.at[self.op, self.ss], rs_ro.at[self.op, self.rs, 0], model=inner_peer).wait_send()
 
             def drain_inner(self):
-                for q in quarters:
-                    self.cross_copy(far + q, q).wait_send()
+                self.near_copies().wait_send()
 
             def drain(self):
                 @pl.when(outer)
@@ -315,27 +321,23 @@
 
         def hand_h(u, j):
             s = lax.rem(j, n_hand)
-            return rdma(hout.at[s], hslot.at[u], hand_sem.at[s, 3 * n_part], hsem.at[u], stage=st + 1)
-
-        def hand_quarter(back, u, j, q, act):
+            return rdma(hout.at[s], hslot.at[u], hand_sem.at[s, 1], hsem.at[u], stage=st + 1)
+
+        def hand_quarter(back, u, j, q):
             s = lax.rem(j, n_hand)
             k = near + q
             src, buf, sems, own = (dout, d_all, d_rs, back_sem) if back else (aout, a_all, a_rs, hand_sem)
-            for i, peer in enumerate((inner_peer, outer_peer, z)):
-                act(rdma(src.at[s, q_rows(q), :], buf.at[u, rows_of(k), :], own.at[s, 3 * q + i], sems.at[u, k],
-                         model=peer, stage=(st - 1) if back else (st + 1)))
+            for peer, side_sem, to in ((inner_peer, 0, k), (outer_peer, 0, n_block), (z, 1, n_block)):
+                rdma(src.at[s, q_rows(q), :], buf.at[u, rows_of(k), :], own.at[s, side_sem], sems.at[u, to],
+                     model=peer, stage=(st - 1) if back else (st + 1)).start()
 
         def hand_sent(back, u, j):
-            for q in quarters:
-                hand_quarter(back, u, j, q, sent)
-            if not back:
-                hand_h(u, j).wait_send()
-
-        def begin(cp):
-            cp.start()
-
-        def sent(cp):
-            cp.wait_send()
+            s = lax.rem(j, n_hand)
+            own = back_sem if back else hand_sem
+            whole, part_of = d_all.at[u], hslot.at[u]
+            rdma(whole, whole, own.at[s, 0], d_rs.at[u, 0], model=z).wait_send()
+            last = part_of if back else whole
+            rdma(last, last, own.at[s, 1], d_rs.at[u, 0], model=z).wait_send()
 
         def softmax_of(u, p, i):
             first = u - p
@@ -420,7 +422,7 @@
             def _():
                 @pl.when(st > 0)
                 def _():
-                    rdma(hout.at[0], hslot.at[u], hand_sem.at[0, 3 * n_part], hsem.at[u], stage=st).wait_recv()
+                    rdma(hout.at[0], hslot.at[u], hand_sem.at[0, 1], hsem.at[u], stage=st).wait_recv()
 
                 for q in quarters:
                     m = hslot[u, q_rows(q), :].astype(F32) + sc.total(q)
@@ -492,7 +494,7 @@
                     @pl.when(st < last_s)
                     def _():
                         aout[s, q_rows(q), :] = (h32 * rms_inverse(h32) * gain_next[0:1, :]).astype(BF16)
-                        hand_quarter(False, u, j, q, begin)
+                        hand_quarter(False, u, j, q)
                         hout[s, q_rows(q), :] = h_new
 
                     @pl.when(is_last)
@@ -651,7 +653,7 @@
                         dg = dn * gain_a
                         dout[s, q_rows(q), :] = (m_all[u, q_rows(q), :] + inv * (
                             dg - normed * jnp.mean(dg * normed, axis=-1, keepdims=True))).astype(BF16)
-                        hand_quarter(True, u, j, q, begin)
+                        hand_quarter(True, u, j, q)
 
             @pl.when(is_first)
             def _():
@@ -807,11 +809,12 @@
             vmem((seq_len, att_w), F32), vmem((seq_len, att_w), F32),
             vmem((2, d_model), F32), vmem((2, d_model), F32),
             vmem((8, d_model), F32), vmem((8, d_model), F32), vmem((8, d_model), F32), vmem((nz, 8, d_model), F32),
-            dma((n_slab + 3,)), dma((n_unit,)), dma((n_hand,)), dma((n_send,)), dma((2,)), dma((n_hand, 3 * n_part + 1)), dma((n_hand, 3 * n_part)), dma((8, n_gath)),
-            dma((n_unit, n_block)), dma((n_unit, n_block)), dma((n_gath, n_part)), dma((n_gath, n_block)),
-            dma((n_gath, n_part)), dma((n_gath, n_block)), dma((n_gath, n_block)), dma((n_gath, n_block)),
-            dma((n_gath, n_part)), dma((n_gath, n_block)), dma((n_gath, n_part)), dma((n_gath, n_block)),
-            dma((4, n_recv, n_block)), dma((4, n_recv, n_part)), dma((4, n_send, n_block)),
+            dma((n_slab + 3,)), dma((n_unit,)), dma((n_hand,)), dma((n_send,)), dma((2,)), dma((n_hand, 2)), dma((n_hand, 2)),
+            dma((8, n_gath)),
+            dma((n_unit, n_block + 1)), dma((n_unit, n_block + 1)), dma((n_gath,)), dma((n_gath,)), dma((n_gath,)), dma((n_gath,)),
+            dma((n_gath, n_block + 1)), dma((n_gath, n_block + 1)),
+            dma((n_gath,)), dma((n_gath,)), dma((n_gath,)), dma((n_gath,)),
+            dma((4, n_recv, n_part + 1)), dma((4, n_recv, n_part)), dma((4, n_send)),
             dma((2,)), dma((nz,)), dma((nz,)),
         ],
         compiler_params=pltpu.CompilerParams(collective_id=0, has_side_effects=True, vmem_limit_bytes=67_043_328),

time: 692 us -> 690 us (level)
  no operation moved by 1% of the time
where the time goes in v11:
time: 690 us; the launch traced here: 689 us
  Pallas kernels  689 us (100%)
    pallas_call x1, Pallas kernels, layer_step(): pl.pallas_call(kernel, out_shape=(out(d_model), out(d_model), out(d_model...  657 us
    pallas_call x1, Pallas kernels, weight_grads(): pl.pallas_call(kernel, out_shape=(jax.ShapeDtypeStruct((att_w, d_model),...  32.2 us

profile of v11, /device:TPU:0, one launch (start us, length us, event | category | flops | bytes accessed | tf_op | source)
XLA Modules:
  0.0 689.4 jit_solution(9358880919042005071)
XLA Ops:
  0.6 656.6 %layer_step.1 = (bf16[24,64,1536]{2,1,0:T(8,128)(2,1)}, bf16[24,64,1536]{2,1,0:T(8,128)(2,1)}, bf16[24,64,1536]{2,1,0:T(8,128)(2,1)}, bf16[24,64,1536]{2,1,0:T(8...) custom-call(bf16[3,512,1536]{2,1,0:T(8,128)(2,1)} %x_ref.1, ...), custom_call_target="tpu_custom_call" | custom-call | tf_op jit(solution)/shard_map/layer_step/pallas_call | solution.py:792
  657.3 32.2 %weight_grads.1 = (f32[384,1536]{1,0:T(8,128)}, f32[9,1536,128]{2,1,0:T(8,128)}, f32[1536,1536]{1,0:T(8,128)}, f32[1536,1536]{1,0:T(8,128)}, f32[2,1536]{1,0:T(2,128)}, /*index=5*/f32[1,1]{1,0:T(1,128)}) custom-call(bf16[1536,384]{1,0:T(8,128)(2,1)} %bitcast.38, bf16[1536,1536]{1,0:T(8,128)(2,1)} %bitcast.30, bf16[1536,1536]{1,0:T(8,128)(2,1)} %bitcast.27, ...), custom_call_target="tpu_custom_call" | custom-call | tf_op jit(solution)/shard_map/weight_grads/pallas_call | solution.py:889

commit v12 on v11

--- a/solution.py
+++ b/solution.py
@@ -87,11 +87,20 @@
         far = n_part - near
         inner_peer = 1 + lax.rem(z, 2)
         outer_peer = last_z * side
+        outer_count = 1 - lax.rem(lax.div(z + 1, 2), 2)
+        first_count = lax.div(ns - st, ns)
         my_half = pl.ds(pl.multiple_of(side * half, half), half)
 
         def rdma(src, dst, ssem, rsem, **dev):
             return pltpu.make_async_remote_copy(src_ref=src, dst_ref=dst, send_sem=ssem, recv_sem=rsem,
                                                 device_id=dev, device_id_type=MESH)
+
+        def repeat(count, body):
+            def turn(i, carry):
+                body(i)
+                return carry
+
+            lax.fori_loop(0, count, turn, 0)
 
         def rows_of(k):
             return pl.ds(pl.multiple_of(k * row, row), row)
@@ -121,12 +130,17 @@
 
         @pl.when(is_first)
         def _():
-            @pl.loop(0, n_unit)
+            for u in range(n_send):
+                x_copy(u).start()
+
+        for cp in qkv_copies + w_copies:
+            cp.start()
+
+        @pl.when(is_first)
+        def _():
+            @pl.loop(n_send, n_unit)
             def _(u):
                 x_copy(u).start()
-
-        for cp in qkv_copies + w_copies:
-            cp.start()
 
         barrier = pltpu.get_barrier_semaphore()
         for i in range(1, nz * ns):
@@ -232,15 +246,16 @@
                 return part[self.op, self.ss, rows_of(k), :]
 
             def start(self, j):
-                @pl.when(outer)
-                def _():
-                    @pl.when(j >= n_send)
-                    def _():
-                        self.drain_outer()
-
-                    for k, q in [(far + q, q) for q in quarters] + [(near + q, n_part) for q in quarters]:
-                        send_p[self.op, self.ss, k] = self.mine(k).astype(BF16)
-                        self.in_copy(k, q).start()
+                @pl.when(outer & (j >= n_send))
+                def _():
+                    self.drain_outer()
+
+                def send(k, q):
+                    send_p[self.op, self.ss, k] = self.mine(k).astype(BF16)
+                    self.in_copy(k, q).start()
+
+                repeat(outer_count * n_part, lambda q: send(far + q, q))
+                repeat(outer_count * n_part, lambda q: send(near + q, n_part))
 
             def relay(self, j):
                 @pl.when(inner)
@@ -360,11 +375,16 @@
             @pl.when(is_first)
             def _():
                 x_copy(u).wait()
+
+            def keep(i):
                 hslot[u] = a_all[u, my_half, :]
-                for k in range(n_block):
-                    rs = pl.ds(k * row, row)
-                    h32 = a_all[u, rs, :].astype(F32)
-                    a_all[u, rs, :] = (h32 * rms_inverse(h32) * gain_a).astype(BF16)
+
+            def norm(k):
+                h32 = a_all[u, rows_of(k), :].astype(F32)
+                a_all[u, rows_of(k), :] = (h32 * rms_inverse(h32) * gain_a).astype(BF16)
+
+            repeat(first_count, keep)
+            repeat(first_count * n_block, norm)
 
         def f_relay_a(j, u):
             @pl.when(st > 0)
@@ -658,10 +678,12 @@
             @pl.when(is_first)
             def _():
                 x_again(j, u).wait()
-                for k in range(n_block):
-                    rs = pl.ds(k * row, row)
-                    h32 = xtmp[sslot(j), rs, :].astype(F32)
-                    ga8[...] += fold(part[3, sslot(j), rs, :] * (h32 * rms_inverse(h32)))
+
+            def gain_rows(k):
+                h32 = xtmp[sslot(j), rows_of(k), :].astype(F32)
+                ga8[...] += fold(part[3, sslot(j), rows_of(k), :] * (h32 * rms_inverse(h32)))
+
+            repeat(first_count * n_block, gain_rows)
 
         backward = (b_enter, b_relay_d, b_collect_d, b_mlp, scatter_relay(2), b_middle, b_relay_dm, b_collect_dm,
                     b_attention, b_relay_h, b_leave)
@@ -824,7 +846,7 @@
 
 def weight_grads(o, dm, a, dqkv, b, du, zz, d, red, head_dim, loss_scale):
     n_tok = o.shape[0] * o.shape[1]
-    rows = 256
+    rows, n_piece = 256, 3
 
     def flat(v):
         return v.reshape(n_tok, v.shape[2])
@@ -839,8 +861,11 @@
         gain_out, loss_out = refs[13:15]
         held, tiles = refs[15:23], refs[23:27]
         in_sem, out_sem = refs[27:]
-        loads = [pltpu.make_async_copy(src[i], held[i], in_sem.at[i]) for i in range(8)]
-        for cp in loads:
+        piece = n_tok // n_piece
+        first = [[pltpu.make_async_copy(src[i].at[pl.ds(c * piece, piece), :], held[i].at[pl.ds(c * piece, piece), :],
+                                        in_sem.at[8 + 2 * c + i]) for i in range(2)] for c in range(n_piece)]
+        loads = [pltpu.make_async_copy(src[i], held[i], in_sem.at[i]) for i in range(2, 8)]
+        for cp in sum(first, []) + loads:
             cp.start()
 
         def stores(pair, i, slot):
@@ -859,9 +884,18 @@
         gain_out[...] = red_ref[0:2, :]
         loss_out[...] = red_ref[2:3, 0:1] * loss_scale
         counts = []
-        for pair in range(4):
-            loads[2 * pair].wait()
-            loads[2 * pair + 1].wait()
+        for c in range(n_piece):
+            at = pl.ds(c * piece, piece)
+            for cp in first[c]:
+                cp.wait()
+            sums = dot_tn(held[0][at, :], held[1][at, :])
+            tiles[0][0] = sums if c == 0 else tiles[0][0] + sums
+        for cp in stores(0, 0, 0):
+            cp.start()
+        counts.append(1)
+        for pair in range(1, 4):
+            loads[2 * pair - 2].wait()
+            loads[2 * pair - 1].wait()
             left, right, tile = held[2 * pair], held[2 * pair + 1], tiles[pair]
             n = tile.shape[1]
             count = left.shape[1] // n
@@ -896,7 +930,7 @@
         scratch_shapes=[pltpu.VMEM(v.shape, BF16) for v in acts] + [
             pltpu.VMEM((1, att_w, d_model), F32), pltpu.VMEM((2, rows, qkv_w), F32),
             pltpu.VMEM((2, rows, ff_w), F32), pltpu.VMEM((2, rows, d_model), F32),
-            pltpu.SemaphoreType.DMA((8,)), pltpu.SemaphoreType.DMA((4, 2))],
+            pltpu.SemaphoreType.DMA((8 + 2 * n_piece,)), pltpu.SemaphoreType.DMA((4, 2))],
         compiler_params=pltpu.CompilerParams(vmem_limit_bytes=67_043_328),
         name="weight_grads",
     )(*acts, red)

time: 690 us -> 695 us (level)
  no operation moved by 1% of the time
where the time goes in v12:
time: 695 us
  Pallas kernels  694 us (100%)
    pallas_call x1, Pallas kernels, layer_step(): pl.pallas_call(kernel, out_shape=(out(d_model), out(d_model), out(d_model...  661 us
    pallas_call x1, Pallas kernels, weight_grads(): pl.pallas_call(kernel, out_shape=(jax.ShapeDtypeStruct((att_w, d_model),...  33 us

profile of v12, /device:TPU:0, one launch (start us, length us, event | category | flops | bytes accessed | tf_op | source)
XLA Modules:
  0.0 695.0 jit_solution(6152686062503504276)
XLA Ops:
  0.6 661.4 %layer_step.1 = (bf16[24,64,1536]{2,1,0:T(8,128)(2,1)}, bf16[24,64,1536]{2,1,0:T(8,128)(2,1)}, bf16[24,64,1536]{2,1,0:T(8,128)(2,1)}, bf16[24,64,1536]{2,1,0:T(8...) custom-call(bf16[3,512,1536]{2,1,0:T(8,128)(2,1)} %x_ref.1, ...), custom_call_target="tpu_custom_call" | custom-call | tf_op jit(solution)/shard_map/layer_step/pallas_call | solution.py:814
  662.0 33.0 %weight_grads.1 = (f32[384,1536]{1,0:T(8,128)}, f32[9,1536,128]{2,1,0:T(8,128)}, f32[1536,1536]{1,0:T(8,128)}, f32[1536,1536]{1,0:T(8,128)}, f32[2,1536]{1,0:T(2,128)}, /*index=5*/f32[1,1]{1,0:T(1,128)}) custom-call(bf16[1536,384]{1,0:T(8,128)(2,1)} %bitcast.38, bf16[1536,1536]{1,0:T(8,128)(2,1)} %bitcast.30, bf16[1536,1536]{1,0:T(8,128)(2,1)} %bitcast.27, ...), custom_call_target="tpu_custom_call" | custom-call | tf_op jit(solution)/shard_map/weight_grads/pallas_call | solution.py:923

commit v13 on v11

--- a/solution.py
+++ b/solution.py
@@ -455,14 +455,12 @@
 
             u_all[u] = dot_nn(bbuf[gslot(u)], wup[...])
 
-            def act(r, carry):
-                rr = pl.ds(pl.multiple_of(r * sub_rows, sub_rows), sub_rows)
+            for r in range(tok // sub_rows):
+                rr = pl.ds(r * sub_rows, sub_rows)
                 v = u_all[u, rr, :]
                 th = jnp.tanh(GELU_K * (v + GELU_C * (v * v * v)))
                 zst[s, rr, :] = (0.5 * v * (1.0 + th)).astype(BF16)
-                return carry
-
-            lax.fori_loop(0, tok // sub_rows, act, 0)
+
             save_z(u).start()
             part[1, s] = dot_nn(zst[s], wdown[...])
             Scatter(1, u).start(j)
@@ -550,16 +548,14 @@
             save_d(j, u).start()
             part[2, s] = dot_nt(d_all[u], wdown[...])
 
-            def act(r, carry):
-                rr = pl.ds(pl.multiple_of(r * sub_rows, sub_rows), sub_rows)
+            for r in range(tok // sub_rows):
+                rr = pl.ds(r * sub_rows, sub_rows)
                 v = u_all[u, rr, :]
                 v2 = v * v
                 th = jnp.tanh(GELU_K * (v + GELU_C * (v2 * v)))
                 slope = 0.5 * (1.0 + th) + 0.5 * v * (1.0 - th * th) * (GELU_K * (1.0 + 3.0 * GELU_C * v2))
                 dust[s, rr, :] = (part[2, s, rr, :] * slope).astype(BF16)
-                return carry
-
-            lax.fori_loop(0, tok // sub_rows, act, 0)
+
             save_du(j, u).start()
             part[2, s] = dot_nt(dust[s], wup[...])
             Scatter(2, j).start(j)

time: 690 us -> 680 us (0.986)
  Pallas kernels: 689 us -> 679 us
    pallas_call x1, Pallas kernels: 657 us -> 647 us  [layer_step(): pl.pallas_call(kernel, out_shape=(out(d_model), out(d_model), out(d_model...]
where the time goes in v13:
time: 680 us
  Pallas kernels  679 us (100%)
    pallas_call x1, Pallas kernels, layer_step(): pl.pallas_call(kernel, out_shape=(out(d_model), out(d_model), out(d_model...  647 us
    pallas_call x1, Pallas kernels, weight_grads(): pl.pallas_call(kernel, out_shape=(jax.ShapeDtypeStruct((att_w, d_model),...  32.2 us

profile of v13, /device:TPU:0, one launch (start us, length us, event | category | flops | bytes accessed | tf_op | source)
XLA Modules:
  0.0 679.6 jit_solution(6041430405875309974)
XLA Ops:
  0.6 646.8 %layer_step.1 = (bf16[24,64,1536]{2,1,0:T(8,128)(2,1)}, bf16[24,64,1536]{2,1,0:T(8,128)(2,1)}, bf16[24,64,1536]{2,1,0:T(8,128)(2,1)}, bf16[24,64,1536]{2,1,0:T(8...) custom-call(bf16[3,512,1536]{2,1,0:T(8,128)(2,1)} %x_ref.1, ...), custom_call_target="tpu_custom_call" | custom-call | tf_op jit(solution)/shard_map/layer_step/pallas_call | solution.py:788
  647.4 32.2 %weight_grads.1 = (f32[384,1536]{1,0:T(8,128)}, f32[9,1536,128]{2,1,0:T(8,128)}, f32[1536,1536]{1,0:T(8,128)}, f32[1536,1536]{1,0:T(8,128)}, f32[2,1536]{1,0:T(2,128)}, /*index=5*/f32[1,1]{1,0:T(1,128)}) custom-call(bf16[1536,384]{1,0:T(8,128)(2,1)} %bitcast.38, bf16[1536,1536]{1,0:T(8,128)(2,1)} %bitcast.30, bf16[1536,1536]{1,0:T(8,128)(2,1)} %bitcast.27, ...), custom_call_target="tpu_custom_call" | custom-call | tf_op jit(solution)/shard_map/weight_grads/pallas_call | solution.py:885

commit v14 on v13

--- a/solution.py
+++ b/solution.py
@@ -134,6 +134,8 @@
             pl.semaphore_signal(barrier, inc=1, device_id_type=MESH,
                                 device_id={"model": lax.rem(z + dz, nz), "stage": lax.rem(st + dst, ns)})
         qkv_all[...] = jnp.zeros_like(qkv_all)
+        dkacc[...] = jnp.zeros_like(dkacc)
+        dvacc[...] = jnp.zeros_like(dvacc)
         lossacc[...] = jnp.zeros_like(lossacc)
         ga8[...] = jnp.zeros_like(ga8)
         gb8[...] = jnp.zeros_like(gb8)
@@ -597,11 +599,6 @@
             def _():
                 x_again(j, u).start()
 
-            @pl.when(p == per_seq - 1)
-            def _():
-                dkacc[...] = jnp.zeros_like(dkacc)
-                dvacc[...] = jnp.zeros_like(dvacc)
-
             datt[...] = dot_nt(dmbuf[gslot(j)], wout[...]).astype(BF16)
             p_rows = pl.ds(pl.multiple_of(p * tok, tok), tok)
             for h in range(n_head):
@@ -615,6 +612,8 @@
                 dqkvst[s, :, cols] = dot_nn(ds, k).astype(BF16)
             dqkvst[s, :, pl.ds(att_w, att_w)] = dkacc[p_rows, :].astype(BF16)
             dqkvst[s, :, pl.ds(2 * att_w, att_w)] = dvacc[p_rows, :].astype(BF16)
+            dkacc[p_rows, :] = jnp.zeros((tok, att_w), F32)
+            dvacc[p_rows, :] = jnp.zeros((tok, att_w), F32)
             save_dqkv(j, u).start()
             part[3, s] = dot_nt(dqkvst[s], wqkv[...])
 

time: 680 us -> 680 us (level)
  no operation moved by 1% of the time
where the time goes in v14:
time: 680 us
  Pallas kernels  679 us (100%)
    pallas_call x1, Pallas kernels, layer_step(): pl.pallas_call(kernel, out_shape=(out(d_model), out(d_model), out(d_model...  647 us
    pallas_call x1, Pallas kernels, weight_grads(): pl.pallas_call(kernel, out_shape=(jax.ShapeDtypeStruct((att_w, d_model),...  32.2 us

profile of v14, /device:TPU:0, one launch (start us, length us, event | category | flops | bytes accessed | tf_op | source)
XLA Modules:
  0.0 680.1 jit_solution(17507254157121897535)
XLA Ops:
  0.6 647.3 %layer_step.1 = (bf16[24,64,1536]{2,1,0:T(8,128)(2,1)}, bf16[24,64,1536]{2,1,0:T(8,128)(2,1)}, bf16[24,64,1536]{2,1,0:T(8,128)(2,1)}, bf16[24,64,1536]{2,1,0:T(8...) custom-call(bf16[3,512,1536]{2,1,0:T(8,128)(2,1)} %x_ref.1, ...), custom_call_target="tpu_custom_call" | custom-call | tf_op jit(solution)/shard_map/layer_step/pallas_call | solution.py:787
  647.9 32.2 %weight_grads.1 = (f32[384,1536]{1,0:T(8,128)}, f32[9,1536,128]{2,1,0:T(8,128)}, f32[1536,1536]{1,0:T(8,128)}, f32[1536,1536]{1,0:T(8,128)}, f32[2,1536]{1,0:T(2,128)}, /*index=5*/f32[1,1]{1,0:T(1,128)}) custom-call(bf16[1536,384]{1,0:T(8,128)(2,1)} %bitcast.38, bf16[1536,1536]{1,0:T(8,128)(2,1)} %bitcast.30, bf16[1536,1536]{1,0:T(8,128)(2,1)} %bitcast.27, ...), custom_call_target="tpu_custom_call" | custom-call | tf_op jit(solution)/shard_map/weight_grads/pallas_call | solution.py:884
